TPU v7x, 32 devices: a whole 2x2x4 slice. The times are simulated.
32 devices in a mesh: row: 4 (over z), col: 8 (over y, x, core).
Axes of the slice: x: 2, y: 2, z: 4, core: 2. Of those that a mesh axis runs over, the one named last changes fastest.
Arguments:
- features: bfloat16 [64, 131072], P(None, ('row', 'col')), may hold values from -6 to 6
- tile_rows: int32 [4, 8, 512], P('row', 'col'), may hold values from 0 to 255, as said below
- tile_cols: int32 [4, 8, 512], P('row', 'col'), may hold values from 0 to 127
- tile_count: int32 [4, 8], P('row', 'col'), may hold values from 1 to 512, as said below
- tile_data: bfloat16 [4, 8, 512, 128, 128], P('row', 'col'), may hold values from -0.21875 to 0.21875
Outputs:
- filtered: bfloat16 [512, 131072], P(None, ('row', 'col'))
Inputs may be any that keep to these rules, and one draw needn't show every extreme that they name: Within one device the pairs (tile_rows, tile_cols) of all 512 slots are distinct. `tile_count`: some device has all 512 slots live in every draw.
All inputs are finite; a program needn't handle non-finite values.
Results may differ from a plain program's by a relative error of at most 0.009.
Values may be sent and summed in bfloat16 or wider, within the bound.
No kernel may reach another device: no remote copies, remote signals or barrier semaphores. Data moves between devices by JAX's collectives and lax.ppermute only.
A program may use at most 128 MiB of HBM per device.

v0:
```python
import functools

import jax
import jax.numpy as jnp
from jax import lax
from jax.experimental import pallas as pl
from jax.experimental.pallas import tpu as pltpu
from jax.sharding import PartitionSpec as P


SCALES = 8
TILE_SIZE = 128
CHUNKS = 2
GROUP = 64
FLIP_GROUP = 16


def bessel_pair(times):
    halved = times / 2.0
    square = halved * halved
    term_zero = jnp.ones_like(times)
    term_one = halved
    sum_zero = term_zero
    sum_one = term_one
    for degree in range(1, 24):
        term_zero = term_zero * square / float(degree * degree)
        term_one = term_one * square / float(degree * (degree + 1))
        sum_zero = sum_zero + term_zero
        sum_one = sum_one + term_one
    damping = jnp.exp(-times)
    return (damping * sum_zero, damping * sum_one)


def coefficients():
    times = 0.25 * 2.0 ** (jnp.arange(SCALES).astype(jnp.float32) / 2.0)
    bessel_zero, bessel_one = bessel_pair(times)
    return (bessel_zero, -2.0 * bessel_one, 2.0 * (bessel_zero - 2.0 * bessel_one / times))


def flip_kernel(group, first, place_ref, tiles_hbm, out_hbm, tiles_ref, flipped_ref, in_sems, out_sems):
    slots = tiles_ref.shape[0]
    live = jnp.clip(place_ref[0] - first, 0, slots)
    live_groups = lax.div(live + (group - 1), group)

    def load(index):
        source = tiles_hbm.at[pl.ds(first + index * group, group)]
        target = tiles_ref.at[pl.ds(index * group, group)]
        return pltpu.make_async_copy(source, target, in_sems.at[index])

    def save(index):
        span = pl.ds(index * group, group)
        return pltpu.make_async_copy(flipped_ref.at[span], out_hbm.at[span], out_sems.at[index])

    @pl.loop(0, live_groups)
    def _(index):
        load(index).start()

    @pl.loop(0, live_groups)
    def _(index):
        load(index).wait()
        for g in range(group):
            slot = index * group + g
            flipped_ref[slot] = tiles_ref[slot].T
        save(index).start()

    @pl.loop(0, live_groups)
    def _(index):
        save(index).wait()


def flip_tiles(place, slot_data, first, slots):
    group = min(FLIP_GROUP, slots)
    anywhere = pl.BlockSpec(memory_space=pl.ANY)
    shape = (slots, TILE_SIZE, TILE_SIZE)
    return pl.pallas_call(
        functools.partial(flip_kernel, group, first),
        in_specs=[pl.BlockSpec(memory_space=pltpu.SMEM), anywhere],
        out_specs=anywhere,
        scratch_shapes=[
            pltpu.VMEM(shape, jnp.bfloat16),
            pltpu.VMEM(shape, jnp.bfloat16),
            pltpu.SemaphoreType.DMA((slots // group,)),
            pltpu.SemaphoreType.DMA((slots // group,)),
        ],
        out_shape=jax.ShapeDtypeStruct(shape, jnp.bfloat16),
        cost_estimate=pl.CostEstimate(
            flops=2 * slots * TILE_SIZE**3,
            bytes_accessed=slots * TILE_SIZE * TILE_SIZE * 4,
            transcendentals=0,
        ),
    )(place, slot_data)


def tile_kernel(pieces, group, place_ref, rows_ref, cols_ref, tiles_low, tiles_high, *refs):
    piece_refs = refs[:pieces]
    keep_hbm, send_hbm = refs[pieces : pieces + 2]
    tiles_ref, panel_ref, acc_ref, keep_ref, send_ref, piece_sems, tile_sems, out_sems = refs[
        pieces + 2 :
    ]
    halves = keep_ref.shape[0]
    per_dev = panel_ref.shape[2] // TILE_SIZE
    live_groups = lax.div(place_ref[0] + (group - 1), group)
    low_groups = tiles_low.shape[0] // group

    def tile_copy(tiles_hbm, base, index):
        return pltpu.make_async_copy(
            tiles_hbm.at[pl.ds((index - base) * group, group)],
            tiles_ref.at[pl.ds(index * group, group)],
            tile_sems.at[index],
        )

    copies = [
        pltpu.make_async_copy(piece_refs[i], panel_ref.at[i], piece_sems.at[i])
        for i in range(pieces)
    ]
    for copy in copies:
        copy.start()

    @pl.loop(0, jnp.minimum(live_groups, low_groups))
    def _(index):
        tile_copy(tiles_low, 0, index).start()

    @pl.loop(low_groups, jnp.maximum(live_groups, low_groups))
    def _(index):
        tile_copy(tiles_high, low_groups, index).start()

    @pl.loop(0, acc_ref.shape[0] // 8)
    def _(index):
        acc_ref[pl.ds(index * 8, 8)] = jnp.zeros((8,) + acc_ref.shape[1:], jnp.float32)

    for copy in copies:
        copy.wait()

    @pl.loop(0, live_groups)
    def _(index):
        tile_copy(tiles_low, index, index).wait()
        for g in range(group):
            slot = index * group + g
            col = cols_ref[slot]
            row = rows_ref[slot]
            offset = pl.multiple_of((col & (per_dev - 1)) * TILE_SIZE, TILE_SIZE)
            picked = panel_ref[lax.div(col, per_dev), :, pl.ds(offset, TILE_SIZE)]
            product = lax.dot_general(
                picked, tiles_ref[slot], (((1,), (0,)), ((), ())),
                preferred_element_type=jnp.float32,
            )
            acc_ref[row] += product

    pair = place_ref[1]
    core = place_ref[2]

    def out_copies(h):
        return (
            pltpu.make_async_copy(send_ref.at[h], send_hbm.at[h], out_sems.at[0, h]),
            pltpu.make_async_copy(keep_ref.at[h], keep_hbm.at[h], out_sems.at[1, h]),
        )

    @pl.loop(0, halves)
    def _(h):
        base = (pair ^ h) * 2
        send_copy, keep_copy = out_copies(h)
        for ref, side, copy in ((send_ref, 1 - core, send_copy), (keep_ref, core, keep_copy)):
            start = (base + side) * per_dev
            for j in range(per_dev):
                ref[h, :, j * TILE_SIZE : (j + 1) * TILE_SIZE] = acc_ref[start + j].astype(
                    jnp.bfloat16
                )
            copy.start()

    @pl.loop(0, halves)
    def _(h):
        for copy in out_copies(h):
            copy.wait()


def tile_products(parts, place, slot_rows, slot_cols, tiles, block_rows, halves):
    channels, nodes = parts[0].shape
    slots = slot_rows.shape[0]
    group = min(GROUP, slots)
    pieces = len(parts)
    out = jax.ShapeDtypeStruct((halves, channels, nodes), jnp.bfloat16)
    anywhere = pl.BlockSpec(memory_space=pl.ANY)
    scalars = pl.BlockSpec(memory_space=pltpu.SMEM)
    return pl.pallas_call(
        functools.partial(tile_kernel, pieces, group),
        in_specs=[scalars] * 3 + [anywhere] * (2 + pieces),
        out_specs=[anywhere] * 2,
        scratch_shapes=[
            pltpu.VMEM((slots, TILE_SIZE, TILE_SIZE), jnp.bfloat16),
            pltpu.VMEM((pieces, channels, nodes), jnp.bfloat16),
            pltpu.VMEM((block_rows + 8, channels, TILE_SIZE), jnp.float32),
            pltpu.VMEM((halves, channels, nodes), jnp.bfloat16),
            pltpu.VMEM((halves, channels, nodes), jnp.bfloat16),
            pltpu.SemaphoreType.DMA((pieces,)),
            pltpu.SemaphoreType.DMA((slots // group,)),
            pltpu.SemaphoreType.DMA((2, halves)),
        ],
        out_shape=[out, out],
        cost_estimate=pl.CostEstimate(
            flops=2 * slots * channels * TILE_SIZE * TILE_SIZE * 8,
            bytes_accessed=slots * TILE_SIZE * TILE_SIZE * 2,
            transcendentals=0,
        ),
    )(place, slot_rows, slot_cols, *tiles, *parts)


def flip(size, mask):
    return [(i, i ^ mask) for i in range(size)]


def gather_parts(own, rows):
    def send(value, pairs):
        return lax.ppermute(value, "row", pairs)

    if rows == 4:
        far = send(own, flip(rows, 2))
        near = send(own, flip(rows, 1))
        inner = send(own, [(1, 2), (2, 1)])
        outer = send(far, [(2, 3), (1, 0)])
        return [own, near, far, inner, outer]
    return [own] + [send(own, flip(rows, mask)) for mask in range(1, rows)]


def reduce_parts(keep, send, cols):
    arrived = lax.ppermute(send, "col", flip(cols, 1))
    paired = [
        (keep[half].astype(jnp.float32) + arrived[half].astype(jnp.float32)).astype(jnp.bfloat16)
        for half in range(cols // 2)
    ]
    terms = [paired[0]]
    for half in range(1, cols // 2):
        terms.append(lax.ppermute(paired[half], "col", flip(cols, 2 * half)))
    total = terms[0].astype(jnp.float32)
    for term in terms[1:]:
        total = total + term.astype(jnp.float32)
    return total.astype(jnp.bfloat16)


def filter_bank(features, tile_rows, tile_cols, tile_count, tile_data):
    cols = lax.axis_size("col")
    rows = lax.axis_size("row")
    channels, nodes = features.shape
    per_dev = nodes // TILE_SIZE
    block_rows = per_dev * cols
    slot_data = tile_data.reshape(-1, TILE_SIZE, TILE_SIZE)
    slots = slot_data.shape[0]
    live = tile_count.reshape(())
    row_at, col_at = lax.axis_index("row"), lax.axis_index("col")
    slot_rows = jnp.where(jnp.arange(slots) < live, tile_rows.reshape(-1), block_rows)
    slot_cols = tile_cols.reshape(-1)
    source = (slot_cols // per_dev) ^ row_at
    if rows == 4:
        source = source + ((source == 3) & ((row_at == 0) | (row_at == 3))).astype(jnp.int32)
    slot_cols = source * per_dev + slot_cols % per_dev
    place = jnp.stack([live, col_at // 2, col_at % 2]).astype(jnp.int32)

    low = slots // 2
    tiles = []
    for begin, size in ((0, low), (low, slots - low)):
        tiles.append(flip_tiles(place, slot_data, begin, size))

    def apply_operator(field):
        parts = gather_parts(field, rows)
        keep, send = tile_products(parts, place, slot_rows, slot_cols, tiles, block_rows, cols // 2)
        return reduce_parts(keep, send, cols)

    width = channels // CHUNKS
    coef_zero, coef_one, coef_two = coefficients()
    outs = []
    fields = [features[i * width : (i + 1) * width] for i in range(CHUNKS)]
    firsts = [apply_operator(field) for field in fields]
    seconds = [apply_operator(first) for first in firsts]
    for field, first, second in zip(fields, firsts, seconds):
        base = field.astype(jnp.float32)
        first_wide = first.astype(jnp.float32)
        second_wide = second.astype(jnp.float32)
        outs.append(
            (
                coef_zero[:, None, None] * base[None]
                + coef_one[:, None, None] * first_wide[None]
                + coef_two[:, None, None] * (2.0 * second_wide - base)[None]
            ).astype(jnp.bfloat16)
        )
    return jnp.concatenate(outs, axis=1).reshape(-1, nodes)


def solution(mesh):
    return jax.shard_map(
        filter_bank,
        mesh=mesh,
        in_specs=(
            P(None, ("row", "col")),
            P("row", "col", None),
            P("row", "col", None),
            P("row", "col"),
            P("row", "col", None, None, None),
        ),
        out_specs=P(None, ("row", "col")),
        check_vma=False,
    )
```

profile of v0, /device:TPU:0, one launch (start us, length us, event | category | flops | bytes accessed | tf_op | source)
XLA Modules:
  0.0 169.1 jit_solution(2567276141945620790)
XLA Ops:
  1.2 4.1 %collective-permute-start.17 = (bf16[32,4096]{1,0:T(8,128)(2,1)S(1)}, bf16[32,4096]{1,0:T(8,128)(2,1)S(1)}, u32[]{:S(2)}, u32[]{:S(2)}) collective-permute-start(bf16[32,4096]{1,0:T(8,128)(2,1)S(1)} %get-tuple-element.39.refs_0_), channel_id=1, source_target_pairs={{0,16},{8,24},{16,0},{24,8},{1,17},{9,25},{17,1},{25,9},{2,18},{10... | collective-permute-start | bytes 786440 | tf_op jit(solution)/shard_map/ppermute | solution.py:213
  8.9 3.8 %shard_map.55.tiles_low = bf16[256,128,128]{2,1,0:T(8,128)(2,1)} custom-call(s32[3]{0:T(128)} %pad_add_fusion.place_ref, bf16[512,128,128]{2,1,0:T(8,128)(2,1)} %bitcast.60), custom_call_target="tpu_custom_call" | custom-call | flops 1073741824 | bytes 16777216 | tf_op jit(solution)/shard_map/pallas_call | solution.py:75
  12.7 5.5 %collective-permute-done.17.refs_2_ = bf16[32,4096]{1,0:T(8,128)(2,1)S(1)} collective-permute-done((bf16[32,4096]{1,0:T(8,128)(2,1)S(1)}, bf16[32,4096]{1,0:T(8,128)(2,1)S(1)}, u32[]{:S(2)}, u32[]{:S(2)}) %collective-permute-start.17) | collective-permute-done | bytes 262176 | tf_op jit(solution)/shard_map/ppermute | solution.py:213
  21.1 5.6 %collective-permute-done.19.refs_4_ = bf16[32,4096]{1,0:T(8,128)(2,1)S(1)} collective-permute-done((bf16[32,4096]{1,0:T(8,128)(2,1)S(1)}, bf16[32,4096]{1,0:T(8,128)(2,1)S(1)}, u32[]{:S(2)}, u32[]{:S(2)}) %collective-permute-start.19) | collective-permute-done | bytes 262176 | tf_op jit(solution)/shard_map/ppermute | solution.py:213
  27.3 5.7 %shard_map.59 = (bf16[4,32,4096]{2,1,0:T(8,128)(2,1)}, bf16[4,32,4096]{2,1,0:T(8,128)(2,1)}) custom-call(s32[3]{0:T(128)} %pad_add_fusion.place_ref, s32[512]{0:T(512)} %get-tuple-element.46.rows_ref, s32[512]{0:T(512)} %get-tuple-element.45.cols_ref, bf16[256,128,128]{2,1,0:T(8,128)(2,1)} %shard_map.55.tiles_low, ...), custom_call_target="tpu_custom_call" | custom-call | flops 4294967296 | bytes 16777216 | tf_op jit(solution)/shard_map/pallas_call | solution.py:184
  33.1 3.8 %collective-permute-start.1 = (bf16[32,4096]{1,0:T(8,128)(2,1)S(1)}, bf16[32,4096]{1,0:T(8,128)(2,1)S(1)}, u32[]{:S(2)}, u32[]{:S(2)}) collective-permute-start(bf16[32,4096]{1,0:T(8,128)(2,1)S(1)} %get-tuple-element.40.refs_0_), channel_id=1, source_target_pairs={{0,16},{8,24},{16,0},{24,8},{1,17},{9,25},{17,1},{25,9},{2,18},{10... | collective-permute-start | bytes 786440 | tf_op jit(solution)/shard_map/ppermute | solution.py:213
  39.3 10.4 %collective-permute-done.1.refs_2_ = bf16[32,4096]{1,0:T(8,128)(2,1)S(1)} collective-permute-done((bf16[32,4096]{1,0:T(8,128)(2,1)S(1)}, bf16[32,4096]{1,0:T(8,128)(2,1)S(1)}, u32[]{:S(2)}, u32[]{:S(2)}) %collective-permute-start.1) | collective-permute-done | bytes 262176 | tf_op jit(solution)/shard_map/ppermute | solution.py:213
  51.0 2.5 %fusion.21 = (bf16[32,4096]{1,0:T(8,128)(2,1)}, bf16[32,4096]{1,0:T(8,128)(2,1)S(1)}, bf16[32,4096]{1,0:T(8,128)(2,1)}) fusion(bf16[4,32,4096]{2,1,0:T(8,128)(2,1)S(1)} %collective-permute-done.20, bf16[4,32,4096]{2,1,0:T(8,128)(2,1)} %get-tuple-element.17), kind=kLoop, calls=%fused_computation.46 | loop fusion | flops 1572864 | bytes 2359296 | tf_op jit(solution)/shard_map/convert_element_type | solution.py:227
  60.1 5.7 %shard_map.57 = (bf16[4,32,4096]{2,1,0:T(8,128)(2,1)}, bf16[4,32,4096]{2,1,0:T(8,128)(2,1)}) custom-call(s32[3]{0:T(128)} %pad_add_fusion.place_ref, s32[512]{0:T(512)} %get-tuple-element.46.rows_ref, s32[512]{0:T(512)} %get-tuple-element.45.cols_ref, bf16[256,128,128]{2,1,0:T(8,128)(2,1)} %shard_map.55.tiles_low, ...), custom_call_target="tpu_custom_call" | custom-call | flops 4294967296 | bytes 16777216 | tf_op jit(solution)/shard_map/pallas_call | solution.py:184
  65.8 3.2 %collective-permute-done.22 = bf16[32,4096]{1,0:T(8,128)(2,1)} collective-permute-done((bf16[32,4096]{1,0:T(8,128)(2,1)}, bf16[32,4096]{1,0:T(8,128)(2,1)}, u32[]{:S(2)}, u32[]{:S(2)}) %collective-permute-start.22) | collective-permute-done | bytes 262176 | tf_op jit(solution)/shard_map/ppermute | solution.py:232
  70.4 3.1 %collective-permute-start.25 = (bf16[32,4096]{1,0:T(8,128)(2,1)S(1)}, bf16[32,4096]{1,0:T(8,128)(2,1)S(1)}, u32[]{:S(2)}, u32[]{:S(2)}) collective-permute-start(bf16[32,4096]{1,0:T(8,128)(2,1)S(1)} %get-tuple-element.24.refs_0_), channel_id=1, source_target_pairs={{0,16},{8,24},{16,0},{24,8},{1,17},{9,25},{17,1},{25,9},{2,18},{10... | collective-permute-start | bytes 786440 | tf_op jit(solution)/shard_map/ppermute | solution.py:213
  74.3 11.2 %collective-permute-done.25.refs_2_ = bf16[32,4096]{1,0:T(8,128)(2,1)S(1)} collective-permute-done((bf16[32,4096]{1,0:T(8,128)(2,1)S(1)}, bf16[32,4096]{1,0:T(8,128)(2,1)S(1)}, u32[]{:S(2)}, u32[]{:S(2)}) %collective-permute-start.25) | collective-permute-done | bytes 262176 | tf_op jit(solution)/shard_map/ppermute | solution.py:213
  93.9 5.7 %shard_map.60 = (bf16[4,32,4096]{2,1,0:T(8,128)(2,1)}, bf16[4,32,4096]{2,1,0:T(8,128)(2,1)}) custom-call(s32[3]{0:T(128)} %pad_add_fusion.place_ref, s32[512]{0:T(512)} %get-tuple-element.46.rows_ref, s32[512]{0:T(512)} %get-tuple-element.45.cols_ref, bf16[256,128,128]{2,1,0:T(8,128)(2,1)} %shard_map.55.tiles_low, ...), custom_call_target="tpu_custom_call" | custom-call | flops 4294967296 | bytes 16777216 | tf_op jit(solution)/shard_map/pallas_call | solution.py:184
  99.7 2.2 %collective-permute-done.6 = bf16[32,4096]{1,0:T(8,128)(2,1)} collective-permute-done((bf16[32,4096]{1,0:T(8,128)(2,1)}, bf16[32,4096]{1,0:T(8,128)(2,1)}, u32[]{:S(2)}, u32[]{:S(2)}) %collective-permute-start.6) | collective-permute-done | bytes 262176 | tf_op jit(solution)/shard_map/ppermute | solution.py:232
  103.3 5.0 %collective-permute-start.9 = (bf16[32,4096]{1,0:T(8,128)(2,1)S(1)}, bf16[32,4096]{1,0:T(8,128)(2,1)S(1)}, u32[]{:S(2)}, u32[]{:S(2)}) collective-permute-start(bf16[32,4096]{1,0:T(8,128)(2,1)S(1)} %get-tuple-element.22.refs_0_), channel_id=1, source_target_pairs={{0,16},{8,24},{16,0},{24,8},{1,17},{9,25},{17,1},{25,9},{2,18},{10... | collective-permute-start | bytes 786440 | tf_op jit(solution)/shard_map/ppermute | solution.py:213
  111.0 8.2 %collective-permute-done.9.refs_2_ = bf16[32,4096]{1,0:T(8,128)(2,1)S(1)} collective-permute-done((bf16[32,4096]{1,0:T(8,128)(2,1)S(1)}, bf16[32,4096]{1,0:T(8,128)(2,1)S(1)}, u32[]{:S(2)}, u32[]{:S(2)}) %collective-permute-start.9) | collective-permute-done | bytes 262176 | tf_op jit(solution)/shard_map/ppermute | solution.py:213
  122.5 6.8 %collective-permute-done.11.refs_4_ = bf16[32,4096]{1,0:T(8,128)(2,1)} collective-permute-done((bf16[32,4096]{1,0:T(8,128)(2,1)S(1)}, bf16[32,4096]{1,0:T(8,128)(2,1)}, u32[]{:S(2)}, u32[]{:S(2)}) %collective-permute-start.11) | collective-permute-done | bytes 262176 | tf_op jit(solution)/shard_map/ppermute | solution.py:213
  129.3 5.7 %shard_map.58 = (bf16[4,32,4096]{2,1,0:T(8,128)(2,1)}, bf16[4,32,4096]{2,1,0:T(8,128)(2,1)}) custom-call(s32[3]{0:T(128)} %pad_add_fusion.place_ref, s32[512]{0:T(512)} %get-tuple-element.46.rows_ref, s32[512]{0:T(512)} %get-tuple-element.45.cols_ref, bf16[256,128,128]{2,1,0:T(8,128)(2,1)} %shard_map.55.tiles_low, ...), custom_call_target="tpu_custom_call" | custom-call | flops 4294967296 | bytes 16777216 | tf_op jit(solution)/shard_map/pallas_call | solution.py:184
  137.8 2.2 %collective-permute-start.30 = (bf16[32,4096]{1,0:T(8,128)(2,1)S(1)}, bf16[32,4096]{1,0:T(8,128)(2,1)S(1)}, u32[]{:S(2)}, u32[]{:S(2)}) collective-permute-start(bf16[32,4096]{1,0:T(8,128)(2,1)S(1)} %get-tuple-element.33), channel_id=1, source_target_pairs={{0,4},{1,5},{2,6},{3,7},{4,0},{5,1},{6,2},{7,3},{8,12},{9,13},{10,... | collective-permute-start | bytes 786440 | tf_op jit(solution)/shard_map/ppermute | solution.py:232
  145.7 2.9 %collective-permute-start.15 = (bf16[32,4096]{1,0:T(8,128)(2,1)S(1)}, bf16[32,4096]{1,0:T(8,128)(2,1)S(1)}, u32[]{:S(2)}, u32[]{:S(2)}) collective-permute-start(bf16[32,4096]{1,0:T(8,128)(2,1)S(1)} %get-tuple-element.26), channel_id=1, source_target_pairs={{0,6},{1,7},{2,4},{3,5},{4,2},{5,3},{6,0},{7,1},{8,14},{9,15},{10,... | collective-permute-start | bytes 786440 | tf_op jit(solution)/shard_map/ppermute | solution.py:232
  148.7 4.0 %collective-permute-done.30 = bf16[32,4096]{1,0:T(8,128)(2,1)S(1)} collective-permute-done((bf16[32,4096]{1,0:T(8,128)(2,1)S(1)}, bf16[32,4096]{1,0:T(8,128)(2,1)S(1)}, u32[]{:S(2)}, u32[]{:S(2)}) %collective-permute-start.30) | collective-permute-done | bytes 262176 | tf_op jit(solution)/shard_map/ppermute | solution.py:232
  152.8 4.2 %collective-permute-done.13 = bf16[32,4096]{1,0:T(8,128)(2,1)S(1)} collective-permute-done((bf16[32,4096]{1,0:T(8,128)(2,1)S(1)}, bf16[32,4096]{1,0:T(8,128)(2,1)S(1)}, u32[]{:S(2)}, u32[]{:S(2)}) %collective-permute-start.13) | collective-permute-done | bytes 262176 | tf_op jit(solution)/shard_map/ppermute | solution.py:232
  157.0 6.5 %collective-permute-done.14 = bf16[32,4096]{1,0:T(8,128)(2,1)S(1)} collective-permute-done((bf16[32,4096]{1,0:T(8,128)(2,1)S(1)}, bf16[32,4096]{1,0:T(8,128)(2,1)S(1)}, u32[]{:S(2)}, u32[]{:S(2)}) %collective-permute-start.14) | collective-permute-done | bytes 262176 | tf_op jit(solution)/shard_map/ppermute | solution.py:232
  166.6 2.5 %pad_maximum_fusion = bf16[8,64,4096]{2,1,0:T(8,128)(2,1)} fusion(bf16[8,32,4096]{2,1,0:T(8,128)(2,1)S(1)} %get-tuple-element.44, bf16[8,32,4096]{2,1,0:T(8,128)(2,1)S(1)} %get-tuple-element.43), kind=kLoop, calls=%fused_computation | loop fusion | flops 8388608 | bytes 8388608 | tf_op jit(solution)/shard_map/concatenate | solution.py:284
  (106 shorter events, 47.5 us)
Async XLA Ops:
  1.2 16.9 %collective-permute-start.17 = (bf16[32,4096]{1,0:T(8,128)(2,1)S(1)}, bf16[32,4096]{1,0:T(8,128)(2,1)S(1)}, u32[]{:S(2)}, u32[]{:S(2)}) collective-permute-start(bf16[32,4096]{1,0:T(8,128)(2,1)S(1)} %get-tuple-element.39.refs_0_), channel_id=1, source_target_pairs={{0,16},{8,24},{16,0},{24,8},{1,17},{9,25},{17,1},{25,9},{2,18},{10... | collective-permute-start | bytes 786440 | tf_op jit(solution)/shard_map/ppermute | solution.py:213
  5.3 15.7 %collective-permute-start.16 = (bf16[32,4096]{1,0:T(8,128)(2,1)S(1)}, bf16[32,4096]{1,0:T(8,128)(2,1)S(1)}, u32[]{:S(2)}, u32[]{:S(2)}) collective-permute-start(bf16[32,4096]{1,0:T(8,128)(2,1)S(1)} %get-tuple-element.39.refs_0_), channel_id=1, source_target_pairs={{0,8},{8,0},{16,24},{24,16},{1,9},{9,1},{17,25},{25,17},{2,10},{10... | collective-permute-start | bytes 786440 | tf_op jit(solution)/shard_map/ppermute | solution.py:213
  6.9 14.2 %collective-permute-start.18 = (bf16[32,4096]{1,0:T(8,128)(2,1)S(1)}, bf16[32,4096]{1,0:T(8,128)(2,1)S(1)}, u32[]{:S(2)}, u32[]{:S(2)}) collective-permute-start(bf16[32,4096]{1,0:T(8,128)(2,1)S(1)} %get-tuple-element.39.refs_0_), channel_id=1, source_target_pairs={{8,16},{16,8},{9,17},{17,9},{10,18},{18,10},{11,19},{19,11},{12,20... | collective-permute-start | bytes 786440 | tf_op jit(solution)/shard_map/ppermute | solution.py:213
  33.0 17.9 %collective-permute-start.20 = (bf16[4,32,4096]{2,1,0:T(8,128)(2,1)}, bf16[4,32,4096]{2,1,0:T(8,128)(2,1)S(1)}, u32[]{:S(2)}, u32[]{:S(2)}) collective-permute-start(bf16[4,32,4096]{2,1,0:T(8,128)(2,1)} %get-tuple-element.18), channel_id=1, source_target_pairs={{0,1},{1,0},{2,3},{3,2},{4,5},{5,4},{6,7},{7,6},{8,9},{9,8},{10,11... | collective-permute-start | bytes 3145736 | tf_op jit(solution)/shard_map/ppermute | solution.py:225
  33.1 16.6 %collective-permute-start.1 = (bf16[32,4096]{1,0:T(8,128)(2,1)S(1)}, bf16[32,4096]{1,0:T(8,128)(2,1)S(1)}, u32[]{:S(2)}, u32[]{:S(2)}) collective-permute-start(bf16[32,4096]{1,0:T(8,128)(2,1)S(1)} %get-tuple-element.40.refs_0_), channel_id=1, source_target_pairs={{0,16},{8,24},{16,0},{24,8},{1,17},{9,25},{17,1},{25,9},{2,18},{10... | collective-permute-start | bytes 786440 | tf_op jit(solution)/shard_map/ppermute | solution.py:213
  36.8 20.0 %collective-permute-start = (bf16[32,4096]{1,0:T(8,128)(2,1)S(1)}, bf16[32,4096]{1,0:T(8,128)(2,1)S(1)}, u32[]{:S(2)}, u32[]{:S(2)}) collective-permute-start(bf16[32,4096]{1,0:T(8,128)(2,1)S(1)} %get-tuple-element.40.refs_0_), channel_id=1, source_target_pairs={{0,8},{8,0},{16,24},{24,16},{1,9},{9,1},{17,25},{25,17},{2,10},{10... | collective-permute-start | bytes 786440 | tf_op jit(solution)/shard_map/ppermute | solution.py:213
  38.6 19.5 %collective-permute-start.2 = (bf16[32,4096]{1,0:T(8,128)(2,1)S(1)}, bf16[32,4096]{1,0:T(8,128)(2,1)S(1)}, u32[]{:S(2)}, u32[]{:S(2)}) collective-permute-start(bf16[32,4096]{1,0:T(8,128)(2,1)S(1)} %get-tuple-element.40.refs_0_), channel_id=1, source_target_pairs={{8,16},{16,8},{9,17},{17,9},{10,18},{18,10},{11,19},{19,11},{12,20... | collective-permute-start | bytes 786440 | tf_op jit(solution)/shard_map/ppermute | solution.py:213
  53.5 12.4 %collective-permute-start.21 = (bf16[32,4096]{1,0:T(8,128)(2,1)}, bf16[32,4096]{1,0:T(8,128)(2,1)}, u32[]{:S(2)}, u32[]{:S(2)}) collective-permute-start(bf16[32,4096]{1,0:T(8,128)(2,1)} %get-tuple-element.34), channel_id=1, source_target_pairs={{0,2},{1,3},{2,0},{3,1},{4,6},{5,7},{6,4},{7,5},{8,10},{9,11},{10,... | collective-permute-start | bytes 786440 | tf_op jit(solution)/shard_map/ppermute | solution.py:232
  55.6 13.4 %collective-permute-start.22 = (bf16[32,4096]{1,0:T(8,128)(2,1)}, bf16[32,4096]{1,0:T(8,128)(2,1)}, u32[]{:S(2)}, u32[]{:S(2)}) collective-permute-start(bf16[32,4096]{1,0:T(8,128)(2,1)} %get-tuple-element.36), channel_id=1, source_target_pairs={{0,4},{1,5},{2,6},{3,7},{4,0},{5,1},{6,2},{7,3},{8,12},{9,13},{10,... | collective-permute-start | bytes 786440 | tf_op jit(solution)/shard_map/ppermute | solution.py:232
  56.8 12.2 %collective-permute-start.23 = (bf16[32,4096]{1,0:T(8,128)(2,1)S(1)}, bf16[32,4096]{1,0:T(8,128)(2,1)}, u32[]{:S(2)}, u32[]{:S(2)}) collective-permute-start(bf16[32,4096]{1,0:T(8,128)(2,1)S(1)} %get-tuple-element.35), channel_id=1, source_target_pairs={{0,6},{1,7},{2,4},{3,5},{4,2},{5,3},{6,0},{7,1},{8,14},{9,15},{10,... | collective-permute-start | bytes 786440 | tf_op jit(solution)/shard_map/ppermute | solution.py:232
  65.7 21.0 %collective-permute-start.4 = (bf16[4,32,4096]{2,1,0:T(8,128)(2,1)}, bf16[4,32,4096]{2,1,0:T(8,128)(2,1)S(1)}, u32[]{:S(2)}, u32[]{:S(2)}) collective-permute-start(bf16[4,32,4096]{2,1,0:T(8,128)(2,1)} %get-tuple-element.14), channel_id=1, source_target_pairs={{0,1},{1,0},{2,3},{3,2},{4,5},{5,4},{6,7},{7,6},{8,9},{9,8},{10,11... | collective-permute-start | bytes 3145736 | tf_op jit(solution)/shard_map/ppermute | solution.py:225
  70.4 15.1 %collective-permute-start.25 = (bf16[32,4096]{1,0:T(8,128)(2,1)S(1)}, bf16[32,4096]{1,0:T(8,128)(2,1)S(1)}, u32[]{:S(2)}, u32[]{:S(2)}) collective-permute-start(bf16[32,4096]{1,0:T(8,128)(2,1)S(1)} %get-tuple-element.24.refs_0_), channel_id=1, source_target_pairs={{0,16},{8,24},{16,0},{24,8},{1,17},{9,25},{17,1},{25,9},{2,18},{10... | collective-permute-start | bytes 786440 | tf_op jit(solution)/shard_map/ppermute | solution.py:213
  73.6 17.3 %collective-permute-start.24 = (bf16[32,4096]{1,0:T(8,128)(2,1)S(1)}, bf16[32,4096]{1,0:T(8,128)(2,1)S(1)}, u32[]{:S(2)}, u32[]{:S(2)}) collective-permute-start(bf16[32,4096]{1,0:T(8,128)(2,1)S(1)} %get-tuple-element.24.refs_0_), channel_id=1, source_target_pairs={{0,8},{8,0},{16,24},{24,16},{1,9},{9,1},{17,25},{25,17},{2,10},{10... | collective-permute-start | bytes 786440 | tf_op jit(solution)/shard_map/ppermute | solution.py:213
  73.6 18.8 %collective-permute-start.26 = (bf16[32,4096]{1,0:T(8,128)(2,1)S(1)}, bf16[32,4096]{1,0:T(8,128)(2,1)S(1)}, u32[]{:S(2)}, u32[]{:S(2)}) collective-permute-start(bf16[32,4096]{1,0:T(8,128)(2,1)S(1)} %get-tuple-element.24.refs_0_), channel_id=1, source_target_pairs={{8,16},{16,8},{9,17},{17,9},{10,18},{18,10},{11,19},{19,11},{12,20... | collective-permute-start | bytes 786440 | tf_op jit(solution)/shard_map/ppermute | solution.py:213
  90.9 11.0 %collective-permute-start.6 = (bf16[32,4096]{1,0:T(8,128)(2,1)}, bf16[32,4096]{1,0:T(8,128)(2,1)}, u32[]{:S(2)}, u32[]{:S(2)}) collective-permute-start(bf16[32,4096]{1,0:T(8,128)(2,1)} %get-tuple-element.30), channel_id=1, source_target_pairs={{0,4},{1,5},{2,6},{3,7},{4,0},{5,1},{6,2},{7,3},{8,12},{9,13},{10,... | collective-permute-start | bytes 786440 | tf_op jit(solution)/shard_map/ppermute | solution.py:232
  99.6 35.5 %collective-permute-start.28 = (bf16[4,32,4096]{2,1,0:T(8,128)(2,1)}, bf16[4,32,4096]{2,1,0:T(8,128)(2,1)}, u32[]{:S(2)}, u32[]{:S(2)}) collective-permute-start(bf16[4,32,4096]{2,1,0:T(8,128)(2,1)} %get-tuple-element.20), channel_id=1, source_target_pairs={{0,1},{1,0},{2,3},{3,2},{4,5},{5,4},{6,7},{7,6},{8,9},{9,8},{10,11... | collective-permute-start | bytes 3145736 | tf_op jit(solution)/shard_map/ppermute | solution.py:225
  103.3 15.9 %collective-permute-start.9 = (bf16[32,4096]{1,0:T(8,128)(2,1)S(1)}, bf16[32,4096]{1,0:T(8,128)(2,1)S(1)}, u32[]{:S(2)}, u32[]{:S(2)}) collective-permute-start(bf16[32,4096]{1,0:T(8,128)(2,1)S(1)} %get-tuple-element.22.refs_0_), channel_id=1, source_target_pairs={{0,16},{8,24},{16,0},{24,8},{1,17},{9,25},{17,1},{25,9},{2,18},{10... | collective-permute-start | bytes 786440 | tf_op jit(solution)/shard_map/ppermute | solution.py:213
  108.3 12.2 %collective-permute-start.10 = (bf16[32,4096]{1,0:T(8,128)(2,1)S(1)}, bf16[32,4096]{1,0:T(8,128)(2,1)S(1)}, u32[]{:S(2)}, u32[]{:S(2)}) collective-permute-start(bf16[32,4096]{1,0:T(8,128)(2,1)S(1)} %get-tuple-element.22.refs_0_), channel_id=1, source_target_pairs={{8,16},{16,8},{9,17},{17,9},{10,18},{18,10},{11,19},{19,11},{12,20... | collective-permute-start | bytes 786440 | tf_op jit(solution)/shard_map/ppermute | solution.py:213
  109.0 12.8 %collective-permute-start.8 = (bf16[32,4096]{1,0:T(8,128)(2,1)S(1)}, bf16[32,4096]{1,0:T(8,128)(2,1)S(1)}, u32[]{:S(2)}, u32[]{:S(2)}) collective-permute-start(bf16[32,4096]{1,0:T(8,128)(2,1)S(1)} %get-tuple-element.22.refs_0_), channel_id=1, source_target_pairs={{0,8},{8,0},{16,24},{24,16},{1,9},{9,1},{17,25},{25,17},{2,10},{10... | collective-permute-start | bytes 786440 | tf_op jit(solution)/shard_map/ppermute | solution.py:213
  137.8 15.0 %collective-permute-start.30 = (bf16[32,4096]{1,0:T(8,128)(2,1)S(1)}, bf16[32,4096]{1,0:T(8,128)(2,1)S(1)}, u32[]{:S(2)}, u32[]{:S(2)}) collective-permute-start(bf16[32,4096]{1,0:T(8,128)(2,1)S(1)} %get-tuple-element.33), channel_id=1, source_target_pairs={{0,4},{1,5},{2,6},{3,7},{4,0},{5,1},{6,2},{7,3},{8,12},{9,13},{10,... | collective-permute-start | bytes 786440 | tf_op jit(solution)/shard_map/ppermute | solution.py:232
  140.0 12.8 %collective-permute-start.31 = (bf16[32,4096]{1,0:T(8,128)(2,1)S(1)}, bf16[32,4096]{1,0:T(8,128)(2,1)S(1)}, u32[]{:S(2)}, u32[]{:S(2)}) collective-permute-start(bf16[32,4096]{1,0:T(8,128)(2,1)S(1)} %get-tuple-element.32), channel_id=1, source_target_pairs={{0,6},{1,7},{2,4},{3,5},{4,2},{5,3},{6,0},{7,1},{8,14},{9,15},{10,... | collective-permute-start | bytes 786440 | tf_op jit(solution)/shard_map/ppermute | solution.py:232
  141.4 15.6 %collective-permute-start.13 = (bf16[32,4096]{1,0:T(8,128)(2,1)S(1)}, bf16[32,4096]{1,0:T(8,128)(2,1)S(1)}, u32[]{:S(2)}, u32[]{:S(2)}) collective-permute-start(bf16[32,4096]{1,0:T(8,128)(2,1)S(1)} %get-tuple-element.25), channel_id=1, source_target_pairs={{0,2},{1,3},{2,0},{3,1},{4,6},{5,7},{6,4},{7,5},{8,10},{9,11},{10,... | collective-permute-start | bytes 786440 | tf_op jit(solution)/shard_map/ppermute | solution.py:232
  142.9 20.6 %collective-permute-start.14 = (bf16[32,4096]{1,0:T(8,128)(2,1)S(1)}, bf16[32,4096]{1,0:T(8,128)(2,1)S(1)}, u32[]{:S(2)}, u32[]{:S(2)}) collective-permute-start(bf16[32,4096]{1,0:T(8,128)(2,1)S(1)} %get-tuple-element.27), channel_id=1, source_target_pairs={{0,4},{1,5},{2,6},{3,7},{4,0},{5,1},{6,2},{7,3},{8,12},{9,13},{10,... | collective-permute-start | bytes 786440 | tf_op jit(solution)/shard_map/ppermute | solution.py:232
  145.7 17.8 %collective-permute-start.15 = (bf16[32,4096]{1,0:T(8,128)(2,1)S(1)}, bf16[32,4096]{1,0:T(8,128)(2,1)S(1)}, u32[]{:S(2)}, u32[]{:S(2)}) collective-permute-start(bf16[32,4096]{1,0:T(8,128)(2,1)S(1)} %get-tuple-element.26), channel_id=1, source_target_pairs={{0,6},{1,7},{2,4},{3,5},{4,2},{5,3},{6,0},{7,1},{8,14},{9,15},{10,... | collective-permute-start | bytes 786440 | tf_op jit(solution)/shard_map/ppermute | solution.py:232
  (31 other events, 299.0 us)
where the time goes:
time: 170 us; the launch traced here: 169 us
  waiting for transfers between devices  72 us (42%)
  starting transfers between devices  47.5 us (28%)
  Pallas kernels  27.4 us (16%)
  other arithmetic  18.2 us (11%)
  local copies, waits for them, and re-layouts  2.87 us (2%)
    ppermute x16, waiting for transfers between devices, send(): return lax.ppermute(value, 'row', pairs)  51 us
    ppermute x16, starting transfers between devices, send(): return lax.ppermute(value, 'row', pairs)  29.2 us
    pallas_call x4, Pallas kernels, tile_products(): pl.pallas_call(functools.partial(tile_kernel, pieces, group), in_specs=[s...  22.7 us
    ppermute x12, waiting for transfers between devices, reduce_parts(): terms.append(lax.ppermute(paired[half], 'col', flip(cols, 2 * half)))  21 us
    ppermute x12, starting transfers between devices, reduce_parts(): terms.append(lax.ppermute(paired[half], 'col', flip(cols, 2 * half)))  18.1 us
    convert_element_type x4, other arithmetic, reduce_parts(): (keep[half].astype(jnp.float32) + arrived[half].astype(jnp.float32)).asty...  7.24 us
    pallas_call x2, Pallas kernels, flip_tiles(): pl.pallas_call(functools.partial(flip_kernel, group, first), in_specs=[pl...  4.73 us
  transfers between devices with their start and end apart: 32, of which 15 were waited for; matrix products, arithmetic and copies ran while one was open for 7% of the time, Pallas kernels for 13%

commit v1 on v0

v1 whole, which is shorter than its diff:
```python
import functools

import jax
import jax.numpy as jnp
from jax import lax
from jax.experimental import pallas as pl
from jax.experimental.pallas import tpu as pltpu
from jax.sharding import PartitionSpec as P


SCALES = 8
TILE_SIZE = 128
CHUNKS = 2
GROUP = 64
FLIP_GROUP = 32
FLIP_DEPTH = 8
FLIP_VMEM = 28 * 2**20
SPARE_VMEM = 24 * 2**20


def bessel_pair(times):
    halved = times / 2.0
    square = halved * halved
    term_zero = jnp.ones_like(times)
    term_one = halved
    sum_zero = term_zero
    sum_one = term_one
    for degree in range(1, 24):
        term_zero = term_zero * square / float(degree * degree)
        term_one = term_one * square / float(degree * (degree + 1))
        sum_zero = sum_zero + term_zero
        sum_one = sum_one + term_one
    damping = jnp.exp(-times)
    return (damping * sum_zero, damping * sum_one)


def coefficients():
    times = 0.25 * 2.0 ** (jnp.arange(SCALES).astype(jnp.float32) / 2.0)
    bessel_zero, bessel_one = bessel_pair(times)
    return (bessel_zero, -2.0 * bessel_one, 2.0 * (bessel_zero - 2.0 * bessel_one / times))


def flip_kernel(group, depth, count_ref, tiles_hbm, flipped_ref, tiles_ref, sems):
    live_groups = lax.div(count_ref[0] + (group - 1), group)

    def load(index):
        slot = lax.rem(index, depth)
        source = tiles_hbm.at[pl.ds(index * group, group)]
        return pltpu.make_async_copy(source, tiles_ref.at[slot], sems.at[slot])

    for index in range(depth):

        @pl.when(index < live_groups)
        def _():
            load(index).start()

    @pl.loop(0, live_groups)
    def _(index):
        load(index).wait()
        for g in range(group):
            flipped_ref[index * group + g] = tiles_ref[lax.rem(index, depth), g].T

        @pl.when(index + depth < live_groups)
        def _():
            load(index + depth).start()


def flip_tiles(live, slot_data):
    slots = slot_data.shape[0]
    group = min(FLIP_GROUP, slots)
    depth = min(FLIP_DEPTH, slots // group)
    return pl.pallas_call(
        functools.partial(flip_kernel, group, depth),
        in_specs=[pl.BlockSpec(memory_space=pltpu.SMEM), pl.BlockSpec(memory_space=pl.ANY)],
        out_specs=pl.BlockSpec(memory_space=pltpu.VMEM),
        scratch_shapes=[
            pltpu.VMEM((depth, group, TILE_SIZE, TILE_SIZE), jnp.bfloat16),
            pltpu.SemaphoreType.DMA((depth,)),
        ],
        out_shape=jax.ShapeDtypeStruct(slot_data.shape, jnp.bfloat16),
        compiler_params=pltpu.CompilerParams(vmem_limit_bytes=FLIP_VMEM),
        cost_estimate=pl.CostEstimate(
            flops=slots * TILE_SIZE**3,
            bytes_accessed=slots * TILE_SIZE * TILE_SIZE * 2,
            transcendentals=0,
        ),
    )(live, slot_data)


def tile_kernel(pieces, group, count_ref, rows_ref, cols_ref, tiles_ref, *refs):
    piece_refs = refs[:pieces]
    keep_ref, send_ref = refs[pieces : pieces + 2]
    panel_ref, acc_ref, piece_sems = refs[pieces + 2 :]
    halves = keep_ref.shape[0]
    per_dev = panel_ref.shape[2] // TILE_SIZE
    count = count_ref[0]
    row_at = lax.axis_index("row")
    col_at = lax.axis_index("col")
    trash = acc_ref.shape[0] - 1
    shifted = pieces - 1 if pieces != lax.axis_size("row") else None
    at_end = (row_at == 0) | (row_at == lax.axis_size("row") - 1)

    copies = [
        pltpu.make_async_copy(piece_refs[i], panel_ref.at[i], piece_sems.at[i])
        for i in range(pieces)
    ]
    for copy in copies:
        copy.start()

    @pl.loop(0, acc_ref.shape[0] // 8)
    def _(index):
        acc_ref[pl.ds(index * 8, 8)] = jnp.zeros((8,) + acc_ref.shape[1:], jnp.float32)

    for copy in copies:
        copy.wait()

    @pl.loop(0, lax.div(count + (group - 1), group))
    def _(index):
        for g in range(group):
            slot = index * group + g
            col = cols_ref[slot]
            row = jnp.where(slot < count, rows_ref[slot], trash)
            source = lax.div(col, per_dev) ^ row_at
            if shifted is not None:
                source = jnp.where(at_end & (source == shifted - 1), shifted, source)
            offset = pl.multiple_of((col & (per_dev - 1)) * TILE_SIZE, TILE_SIZE)
            picked = panel_ref[source, :, pl.ds(offset, TILE_SIZE)]
            acc_ref[row] += jnp.dot(picked, tiles_ref[slot], preferred_element_type=jnp.float32)

    pair = lax.div(col_at, 2)
    core = col_at & 1

    @pl.loop(0, halves)
    def _(h):
        base = (pair ^ h) * 2
        for ref, side in ((send_ref, 1 - core), (keep_ref, core)):
            start = (base + side) * per_dev
            for j in range(per_dev):
                ref[h, :, j * TILE_SIZE : (j + 1) * TILE_SIZE] = acc_ref[start + j].astype(
                    jnp.bfloat16
                )


def tile_products(parts, live, slot_rows, slot_cols, tiles, block_rows, halves):
    channels, nodes = parts[0].shape
    slots = slot_rows.shape[0]
    group = min(GROUP, slots)
    pieces = len(parts)
    out = jax.ShapeDtypeStruct((halves, channels, nodes), jnp.bfloat16)
    scalars = pl.BlockSpec(memory_space=pltpu.SMEM)
    vectors = pl.BlockSpec(memory_space=pltpu.VMEM)
    scratch = channels * (4 * (block_rows + 8) * TILE_SIZE + 2 * pieces * nodes)
    return pl.pallas_call(
        functools.partial(tile_kernel, pieces, group),
        in_specs=[scalars] * 3 + [vectors] + [pl.BlockSpec(memory_space=pl.ANY)] * pieces,
        out_specs=[vectors] * 2,
        scratch_shapes=[
            pltpu.VMEM((pieces, channels, nodes), jnp.bfloat16),
            pltpu.VMEM((block_rows + 8, channels, TILE_SIZE), jnp.float32),
            pltpu.SemaphoreType.DMA((pieces,)),
        ],
        out_shape=[out, out],
        compiler_params=pltpu.CompilerParams(vmem_limit_bytes=scratch + SPARE_VMEM),
        cost_estimate=pl.CostEstimate(
            flops=2 * slots * channels * TILE_SIZE * TILE_SIZE * 8,
            bytes_accessed=slots * TILE_SIZE * TILE_SIZE * 2,
            transcendentals=0,
        ),
    )(live, slot_rows, slot_cols, tiles, *parts)


def flip(size, mask):
    return [(i, i ^ mask) for i in range(size)]


def gather_parts(own, rows):
    def send(value, pairs):
        return lax.ppermute(value, "row", pairs)

    if rows == 4:
        far = send(own, flip(rows, 2))
        near = send(own, flip(rows, 1))
        inner = send(own, [(1, 2), (2, 1)])
        outer = send(far, [(2, 3), (1, 0)])
        return [own, near, far, inner, outer]
    return [own] + [send(own, flip(rows, mask)) for mask in range(1, rows)]


def reduce_parts(keep, send, cols):
    arrived = lax.ppermute(send, "col", flip(cols, 1))
    paired = [
        (keep[half].astype(jnp.float32) + arrived[half].astype(jnp.float32)).astype(jnp.bfloat16)
        for half in range(cols // 2)
    ]
    terms = [paired[0]]
    for half in range(1, cols // 2):
        terms.append(lax.ppermute(paired[half], "col", flip(cols, 2 * half)))
    total = terms[0].astype(jnp.float32)
    for term in terms[1:]:
        total = total + term.astype(jnp.float32)
    return total.astype(jnp.bfloat16)


def filter_bank(features, tile_rows, tile_cols, tile_count, tile_data):
    cols = lax.axis_size("col")
    rows = lax.axis_size("row")
    channels, nodes = features.shape
    per_dev = nodes // TILE_SIZE
    block_rows = per_dev * cols
    slot_data = tile_data.reshape(-1, TILE_SIZE, TILE_SIZE)
    live = tile_count.reshape(-1)
    slot_rows = tile_rows.reshape(-1)
    slot_cols = tile_cols.reshape(-1)

    tiles = flip_tiles(live, slot_data)

    def apply_operator(field):
        parts = gather_parts(field, rows)
        keep, send = tile_products(parts, live, slot_rows, slot_cols, tiles, block_rows, cols // 2)
        return reduce_parts(keep, send, cols)

    width = channels // CHUNKS
    coef_zero, coef_one, coef_two = coefficients()
    fields = [features[i * width : (i + 1) * width] for i in range(CHUNKS)]
    firsts = [apply_operator(field) for field in fields]
    seconds = [apply_operator(first) for first in firsts]
    filtered = jnp.zeros((SCALES, channels, nodes), jnp.bfloat16)
    for chunk, (field, first, second) in enumerate(zip(fields, firsts, seconds)):
        base = field.astype(jnp.float32)
        first_wide = first.astype(jnp.float32)
        second_wide = second.astype(jnp.float32)
        block = (
            coef_zero[:, None, None] * base[None]
            + coef_one[:, None, None] * first_wide[None]
            + coef_two[:, None, None] * (2.0 * second_wide - base)[None]
        ).astype(jnp.bfloat16)
        filtered = lax.dynamic_update_slice(filtered, block, (0, chunk * width, 0))
    return filtered.reshape(-1, nodes)


def solution(mesh):
    return jax.shard_map(
        filter_bank,
        mesh=mesh,
        in_specs=(
            P(None, ("row", "col")),
            P("row", "col", None),
            P("row", "col", None),
            P("row", "col"),
            P("row", "col", None, None, None),
        ),
        out_specs=P(None, ("row", "col")),
        check_vma=False,
    )
```

time: 170 us -> 153 us (0.900)
  Pallas kernels: 27.4 us -> 13.3 us
  waiting for transfers between devices: 72 us -> 84.8 us
  other arithmetic: 18.2 us -> 6.99 us
  local copies, waits for them, and re-layouts: 2.87 us -> 0.02 us
    pallas_call x4, Pallas kernels: 22.7 us -> 11 us  [tile_products(): pl.pallas_call(functools.partial(tile_kernel, pieces, group), in_specs=[s...]
    ppermute x16, waiting for transfers between devices: 51 us -> 57.7 us  [send(): return lax.ppermute(value, 'row', pairs)]
    convert_element_type x4, other arithmetic: 7.24 us -> 0.77 us  [reduce_parts(): (keep[half].astype(jnp.float32) + arrived[half].astype(jnp.float32)).asty...]
    ppermute x12, waiting for transfers between devices: 21 us -> 27.1 us  [reduce_parts(): terms.append(lax.ppermute(paired[half], 'col', flip(cols, 2 * half)))]
    unnamed x46 -> x6, local copies, waits for them, and re-layouts: 2.87 us -> 0.02 us
    dynamic_update_slice x0 -> x1, other arithmetic: none -> 2.51 us  [filter_bank(): filtered = lax.dynamic_update_slice(filtered, block, (0, chunk * width, 0))]
    concatenate x1 -> x0, other arithmetic: 2.51 us -> none  [filter_bank(): return jnp.concatenate(outs, axis=1).reshape(-1, nodes)]
    convert_element_type x2, other arithmetic: 2.79 us -> 0.33 us  [filter_bank(): first_wide = first.astype(jnp.float32)]
  transfers between devices with their start and end apart: 32 -> 32, of which waited for: 15 -> 15; matrix products, arithmetic and copies ran while one was open for 7% -> 1% of each run, Pallas kernels for 13% -> 7%
where the time goes in v1:
time: 153 us; the launch traced here: 152 us
  waiting for transfers between devices  84.8 us (55%)
  starting transfers between devices  46.2 us (30%)
  Pallas kernels  13.3 us (9%)
  other arithmetic  6.99 us (5%)
    ppermute x16, waiting for transfers between devices, send(): return lax.ppermute(value, 'row', pairs)  57.7 us
    ppermute x16, starting transfers between devices, send(): return lax.ppermute(value, 'row', pairs)  28.1 us
    ppermute x12, waiting for transfers between devices, reduce_parts(): terms.append(lax.ppermute(paired[half], 'col', flip(cols, 2 * half)))  27.1 us
    ppermute x12, starting transfers between devices, reduce_parts(): terms.append(lax.ppermute(paired[half], 'col', flip(cols, 2 * half)))  17.9 us
    pallas_call x4, Pallas kernels, tile_products(): pl.pallas_call(functools.partial(tile_kernel, pieces, group), in_specs=[s...  11 us
  transfers between devices with their start and end apart: 32, of which 15 were waited for; matrix products, arithmetic and copies ran while one was open for 1% of the time, Pallas kernels for 7%

profile of v1, /device:TPU:0, one launch (start us, length us, event | category | flops | bytes accessed | tf_op | source)
XLA Modules:
  0.0 152.2 jit_solution(13099089721474751246)
XLA Ops:
  1.2 4.1 %collective-permute-start.17 = (bf16[32,4096]{1,0:T(8,128)(2,1)S(1)}, bf16[32,4096]{1,0:T(8,128)(2,1)S(1)}, u32[]{:S(2)}, u32[]{:S(2)}) collective-permute-start(bf16[32,4096]{1,0:T(8,128)(2,1)S(1)} %get-tuple-element.39.refs_0_), channel_id=1, source_target_pairs={{0,16},{8,24},{16,0},{24,8},{1,17},{9,25},{17,1},{25,9},{2,18},{10... | collective-permute-start | bytes 786440 | tf_op jit(solution)/shard_map/ppermute | solution.py:178
  7.5 10.6 %collective-permute-done.17.refs_2_ = bf16[32,4096]{1,0:T(8,128)(2,1)S(1)} collective-permute-done((bf16[32,4096]{1,0:T(8,128)(2,1)S(1)}, bf16[32,4096]{1,0:T(8,128)(2,1)S(1)}, u32[]{:S(2)}, u32[]{:S(2)}) %collective-permute-start.17) | collective-permute-done | bytes 262176 | tf_op jit(solution)/shard_map/ppermute | solution.py:178
  20.1 2.3 %shard_map.55.tiles_ref = bf16[512,128,128]{2,1,0:T(8,128)(2,1)S(1)} custom-call(s32[1]{0:T(128)} %bitcast.55.count_ref, bf16[512,128,128]{2,1,0:T(8,128)(2,1)} %bitcast.68), custom_call_target="tpu_custom_call" | custom-call | flops 1073741824 | bytes 16777216 | tf_op jit(solution)/shard_map/pallas_call | solution.py:72
  22.4 4.2 %collective-permute-done.19.refs_4_ = bf16[32,4096]{1,0:T(8,128)(2,1)S(1)} collective-permute-done((bf16[32,4096]{1,0:T(8,128)(2,1)S(1)}, bf16[32,4096]{1,0:T(8,128)(2,1)S(1)}, u32[]{:S(2)}, u32[]{:S(2)}) %collective-permute-start.19) | collective-permute-done | bytes 262176 | tf_op jit(solution)/shard_map/ppermute | solution.py:178
  26.6 2.8 %shard_map.58 = (bf16[4,32,4096]{2,1,0:T(8,128)(2,1)S(1)}, bf16[4,32,4096]{2,1,0:T(8,128)(2,1)S(1)}) custom-call(s32[1]{0:T(128)} %bitcast.58.count_ref, s32[512]{0:T(512)S(1)} %bitcast.60, s32[512]{0:T(512)S(1)} %bitcast.64, bf16[512,128,128]{2,1,0:T(8,128)(2,1)S(1)} %shard_map.55.tiles_ref, bf16[32,4096]{1,0:T(8,128)(2,1)S(1)} %get-tuple-element.39.refs_0_, ...), custom_call_target="tpu_custom_call" | custom-call | flops 4294967296 | bytes 16777216 | tf_op jit(solution)/shard_map/pallas_call | solution.py:153
  29.5 3.7 %collective-permute-start.1 = (bf16[32,4096]{1,0:T(8,128)(2,1)S(1)}, bf16[32,4096]{1,0:T(8,128)(2,1)S(1)}, u32[]{:S(2)}, u32[]{:S(2)}) collective-permute-start(bf16[32,4096]{1,0:T(8,128)(2,1)S(1)} %get-tuple-element.40.refs_0_), channel_id=1, source_target_pairs={{0,16},{8,24},{16,0},{24,8},{1,17},{9,25},{17,1},{25,9},{2,18},{10... | collective-permute-start | bytes 786440 | tf_op jit(solution)/shard_map/ppermute | solution.py:178
  35.6 10.4 %collective-permute-done.1.refs_2_ = bf16[32,4096]{1,0:T(8,128)(2,1)S(1)} collective-permute-done((bf16[32,4096]{1,0:T(8,128)(2,1)S(1)}, bf16[32,4096]{1,0:T(8,128)(2,1)S(1)}, u32[]{:S(2)}, u32[]{:S(2)}) %collective-permute-start.1) | collective-permute-done | bytes 262176 | tf_op jit(solution)/shard_map/ppermute | solution.py:178
  51.0 3.5 %collective-permute-start.23 = (bf16[32,4096]{1,0:T(8,128)(2,1)S(1)}, bf16[32,4096]{1,0:T(8,128)(2,1)S(1)}, u32[]{:S(2)}, u32[]{:S(2)}) collective-permute-start(bf16[32,4096]{1,0:T(8,128)(2,1)S(1)} %get-tuple-element.35), channel_id=1, source_target_pairs={{0,6},{1,7},{2,4},{3,5},{4,2},{5,3},{6,0},{7,1},{8,14},{9,15},{10,... | collective-permute-start | bytes 786440 | tf_op jit(solution)/shard_map/ppermute | solution.py:197
  55.7 2.8 %shard_map.56 = (bf16[4,32,4096]{2,1,0:T(8,128)(2,1)S(1)}, bf16[4,32,4096]{2,1,0:T(8,128)(2,1)S(1)}) custom-call(s32[1]{0:T(128)} %bitcast.56.count_ref, s32[512]{0:T(512)S(1)} %bitcast.61, s32[512]{0:T(512)S(1)} %bitcast.65, bf16[512,128,128]{2,1,0:T(8,128)(2,1)S(1)} %shard_map.55.tiles_ref, bf16[32,4096]{1,0:T(8,128)(2,1)S(1)} %get-tuple-element.40.refs_0_, ...), custom_call_target="tpu_custom_call" | custom-call | flops 4294967296 | bytes 16777216 | tf_op jit(solution)/shard_map/pallas_call | solution.py:153
  58.5 4.2 %collective-permute-done.22 = bf16[32,4096]{1,0:T(8,128)(2,1)S(1)} collective-permute-done((bf16[32,4096]{1,0:T(8,128)(2,1)S(1)}, bf16[32,4096]{1,0:T(8,128)(2,1)S(1)}, u32[]{:S(2)}, u32[]{:S(2)}) %collective-permute-start.22) | collective-permute-done | bytes 262176 | tf_op jit(solution)/shard_map/ppermute | solution.py:197
  63.0 3.1 %collective-permute-start.25 = (bf16[32,4096]{1,0:T(8,128)(2,1)S(1)}, bf16[32,4096]{1,0:T(8,128)(2,1)S(1)}, u32[]{:S(2)}, u32[]{:S(2)}) collective-permute-start(bf16[32,4096]{1,0:T(8,128)(2,1)S(1)} %get-tuple-element.24.refs_0_), channel_id=1, source_target_pairs={{0,16},{8,24},{16,0},{24,8},{1,17},{9,25},{17,1},{25,9},{2,18},{10... | collective-permute-start | bytes 786440 | tf_op jit(solution)/shard_map/ppermute | solution.py:178
  66.8 11.3 %collective-permute-done.25.refs_2_ = bf16[32,4096]{1,0:T(8,128)(2,1)S(1)} collective-permute-done((bf16[32,4096]{1,0:T(8,128)(2,1)S(1)}, bf16[32,4096]{1,0:T(8,128)(2,1)S(1)}, u32[]{:S(2)}, u32[]{:S(2)}) %collective-permute-start.25) | collective-permute-done | bytes 262176 | tf_op jit(solution)/shard_map/ppermute | solution.py:178
  83.1 3.2 %collective-permute-done.27.refs_4_ = bf16[32,4096]{1,0:T(8,128)(2,1)S(1)} collective-permute-done((bf16[32,4096]{1,0:T(8,128)(2,1)S(1)}, bf16[32,4096]{1,0:T(8,128)(2,1)S(1)}, u32[]{:S(2)}, u32[]{:S(2)}) %collective-permute-start.27) | collective-permute-done | bytes 262176 | tf_op jit(solution)/shard_map/ppermute | solution.py:178
  86.3 2.8 %shard_map.59 = (bf16[4,32,4096]{2,1,0:T(8,128)(2,1)S(1)}, bf16[4,32,4096]{2,1,0:T(8,128)(2,1)S(1)}) custom-call(s32[1]{0:T(128)} %bitcast.59.count_ref, s32[512]{0:T(512)S(1)} %bitcast.62, s32[512]{0:T(512)S(1)} %bitcast.66, bf16[512,128,128]{2,1,0:T(8,128)(2,1)S(1)} %shard_map.55.tiles_ref, bf16[32,4096]{1,0:T(8,128)(2,1)S(1)} %get-tuple-element.24.refs_0_, ...), custom_call_target="tpu_custom_call" | custom-call | flops 4294967296 | bytes 16777216 | tf_op jit(solution)/shard_map/pallas_call | solution.py:153
  89.2 3.1 %collective-permute-done.6 = bf16[32,4096]{1,0:T(8,128)(2,1)S(1)} collective-permute-done((bf16[32,4096]{1,0:T(8,128)(2,1)S(1)}, bf16[32,4096]{1,0:T(8,128)(2,1)S(1)}, u32[]{:S(2)}, u32[]{:S(2)}) %collective-permute-start.6) | collective-permute-done | bytes 262176 | tf_op jit(solution)/shard_map/ppermute | solution.py:197
  92.4 4.1 %collective-permute-start.9 = (bf16[32,4096]{1,0:T(8,128)(2,1)S(1)}, bf16[32,4096]{1,0:T(8,128)(2,1)S(1)}, u32[]{:S(2)}, u32[]{:S(2)}) collective-permute-start(bf16[32,4096]{1,0:T(8,128)(2,1)S(1)} %get-tuple-element.22.refs_0_), channel_id=1, source_target_pairs={{0,16},{8,24},{16,0},{24,8},{1,17},{9,25},{17,1},{25,9},{2,18},{10... | collective-permute-start | bytes 786440 | tf_op jit(solution)/shard_map/ppermute | solution.py:178
  99.1 8.0 %collective-permute-done.9.refs_2_ = bf16[32,4096]{1,0:T(8,128)(2,1)S(1)} collective-permute-done((bf16[32,4096]{1,0:T(8,128)(2,1)S(1)}, bf16[32,4096]{1,0:T(8,128)(2,1)S(1)}, u32[]{:S(2)}, u32[]{:S(2)}) %collective-permute-start.9) | collective-permute-done | bytes 262176 | tf_op jit(solution)/shard_map/ppermute | solution.py:178
  109.7 7.5 %collective-permute-done.11.refs_4_ = bf16[32,4096]{1,0:T(8,128)(2,1)S(1)} collective-permute-done((bf16[32,4096]{1,0:T(8,128)(2,1)S(1)}, bf16[32,4096]{1,0:T(8,128)(2,1)S(1)}, u32[]{:S(2)}, u32[]{:S(2)}) %collective-permute-start.11) | collective-permute-done | bytes 262176 | tf_op jit(solution)/shard_map/ppermute | solution.py:178
  117.1 2.8 %shard_map.57 = (bf16[4,32,4096]{2,1,0:T(8,128)(2,1)S(1)}, bf16[4,32,4096]{2,1,0:T(8,128)(2,1)S(1)}) custom-call(s32[1]{0:T(128)} %bitcast.57.count_ref, s32[512]{0:T(512)S(1)} %bitcast.63, s32[512]{0:T(512)S(1)} %bitcast.67, bf16[512,128,128]{2,1,0:T(8,128)(2,1)S(1)} %shard_map.55.tiles_ref, bf16[32,4096]{1,0:T(8,128)(2,1)S(1)} %get-tuple-element.22.refs_0_, ...), custom_call_target="tpu_custom_call" | custom-call | flops 4294967296 | bytes 16777216 | tf_op jit(solution)/shard_map/pallas_call | solution.py:153
  126.2 3.3 %collective-permute-done.29 = bf16[32,4096]{1,0:T(8,128)(2,1)S(1)} collective-permute-done((bf16[32,4096]{1,0:T(8,128)(2,1)S(1)}, bf16[32,4096]{1,0:T(8,128)(2,1)S(1)}, u32[]{:S(2)}, u32[]{:S(2)}) %collective-permute-start.29) | collective-permute-done | bytes 262176 | tf_op jit(solution)/shard_map/ppermute | solution.py:197
  131.1 6.0 %collective-permute-done.30 = bf16[32,4096]{1,0:T(8,128)(2,1)S(1)} collective-permute-done((bf16[32,4096]{1,0:T(8,128)(2,1)S(1)}, bf16[32,4096]{1,0:T(8,128)(2,1)S(1)}, u32[]{:S(2)}, u32[]{:S(2)}) %collective-permute-start.30) | collective-permute-done | bytes 262176 | tf_op jit(solution)/shard_map/ppermute | solution.py:197
  137.1 3.6 %collective-permute-done.13 = bf16[32,4096]{1,0:T(8,128)(2,1)S(1)} collective-permute-done((bf16[32,4096]{1,0:T(8,128)(2,1)S(1)}, bf16[32,4096]{1,0:T(8,128)(2,1)S(1)}, u32[]{:S(2)}, u32[]{:S(2)}) %collective-permute-start.13) | collective-permute-done | bytes 262176 | tf_op jit(solution)/shard_map/ppermute | solution.py:197
  140.8 6.8 %collective-permute-done.14 = bf16[32,4096]{1,0:T(8,128)(2,1)S(1)} collective-permute-done((bf16[32,4096]{1,0:T(8,128)(2,1)S(1)}, bf16[32,4096]{1,0:T(8,128)(2,1)S(1)}, u32[]{:S(2)}, u32[]{:S(2)}) %collective-permute-start.14) | collective-permute-done | bytes 262176 | tf_op jit(solution)/shard_map/ppermute | solution.py:197
  149.7 2.5 %pad_maximum_fusion = bf16[8,64,4096]{2,1,0:T(8,128)(2,1)} fusion(bf16[8,32,4096]{2,1,0:T(8,128)(2,1)S(1)} %get-tuple-element.44, bf16[8,32,4096]{2,1,0:T(8,128)(2,1)S(1)} %get-tuple-element.43), kind=kLoop, calls=%fused_computation | loop fusion | flops 8388608 | bytes 8388608 | tf_op jit(solution)/shard_map/dynamic_update_slice | solution.py:237
  (63 shorter events, 34.8 us)
Async XLA Ops:
  1.2 16.9 %collective-permute-start.17 = (bf16[32,4096]{1,0:T(8,128)(2,1)S(1)}, bf16[32,4096]{1,0:T(8,128)(2,1)S(1)}, u32[]{:S(2)}, u32[]{:S(2)}) collective-permute-start(bf16[32,4096]{1,0:T(8,128)(2,1)S(1)} %get-tuple-element.39.refs_0_), channel_id=1, source_target_pairs={{0,16},{8,24},{16,0},{24,8},{1,17},{9,25},{17,1},{25,9},{2,18},{10... | collective-permute-start | bytes 786440 | tf_op jit(solution)/shard_map/ppermute | solution.py:178
  5.3 17.1 %collective-permute-start.16 = (bf16[32,4096]{1,0:T(8,128)(2,1)S(1)}, bf16[32,4096]{1,0:T(8,128)(2,1)S(1)}, u32[]{:S(2)}, u32[]{:S(2)}) collective-permute-start(bf16[32,4096]{1,0:T(8,128)(2,1)S(1)} %get-tuple-element.39.refs_0_), channel_id=1, source_target_pairs={{0,8},{8,0},{16,24},{24,16},{1,9},{9,1},{17,25},{25,17},{2,10},{10... | collective-permute-start | bytes 786440 | tf_op jit(solution)/shard_map/ppermute | solution.py:178
  6.9 15.5 %collective-permute-start.18 = (bf16[32,4096]{1,0:T(8,128)(2,1)S(1)}, bf16[32,4096]{1,0:T(8,128)(2,1)S(1)}, u32[]{:S(2)}, u32[]{:S(2)}) collective-permute-start(bf16[32,4096]{1,0:T(8,128)(2,1)S(1)} %get-tuple-element.39.refs_0_), channel_id=1, source_target_pairs={{8,16},{16,8},{9,17},{17,9},{10,18},{18,10},{11,19},{19,11},{12,20... | collective-permute-start | bytes 786440 | tf_op jit(solution)/shard_map/ppermute | solution.py:178
  29.4 17.9 %collective-permute-start.20 = (bf16[4,32,4096]{2,1,0:T(8,128)(2,1)S(1)}, bf16[4,32,4096]{2,1,0:T(8,128)(2,1)S(1)}, u32[]{:S(2)}, u32[]{:S(2)}) collective-permute-start(bf16[4,32,4096]{2,1,0:T(8,128)(2,1)S(1)} %get-tuple-element.18), channel_id=1, source_target_pairs={{0,1},{1,0},{2,3},{3,2},{4,5},{5,4},{6,7},{7,6},{8,9},{9,8},{10,11... | collective-permute-start | bytes 3145736 | tf_op jit(solution)/shard_map/ppermute | solution.py:190
  29.5 16.6 %collective-permute-start.1 = (bf16[32,4096]{1,0:T(8,128)(2,1)S(1)}, bf16[32,4096]{1,0:T(8,128)(2,1)S(1)}, u32[]{:S(2)}, u32[]{:S(2)}) collective-permute-start(bf16[32,4096]{1,0:T(8,128)(2,1)S(1)} %get-tuple-element.40.refs_0_), channel_id=1, source_target_pairs={{0,16},{8,24},{16,0},{24,8},{1,17},{9,25},{17,1},{25,9},{2,18},{10... | collective-permute-start | bytes 786440 | tf_op jit(solution)/shard_map/ppermute | solution.py:178
  33.2 17.8 %collective-permute-start = (bf16[32,4096]{1,0:T(8,128)(2,1)S(1)}, bf16[32,4096]{1,0:T(8,128)(2,1)S(1)}, u32[]{:S(2)}, u32[]{:S(2)}) collective-permute-start(bf16[32,4096]{1,0:T(8,128)(2,1)S(1)} %get-tuple-element.40.refs_0_), channel_id=1, source_target_pairs={{0,8},{8,0},{16,24},{24,16},{1,9},{9,1},{17,25},{25,17},{2,10},{10... | collective-permute-start | bytes 786440 | tf_op jit(solution)/shard_map/ppermute | solution.py:178
  35.0 19.5 %collective-permute-start.2 = (bf16[32,4096]{1,0:T(8,128)(2,1)S(1)}, bf16[32,4096]{1,0:T(8,128)(2,1)S(1)}, u32[]{:S(2)}, u32[]{:S(2)}) collective-permute-start(bf16[32,4096]{1,0:T(8,128)(2,1)S(1)} %get-tuple-element.40.refs_0_), channel_id=1, source_target_pairs={{8,16},{16,8},{9,17},{17,9},{10,18},{18,10},{11,19},{19,11},{12,20... | collective-permute-start | bytes 786440 | tf_op jit(solution)/shard_map/ppermute | solution.py:178
  47.5 11.0 %collective-permute-start.21 = (bf16[32,4096]{1,0:T(8,128)(2,1)S(1)}, bf16[32,4096]{1,0:T(8,128)(2,1)S(1)}, u32[]{:S(2)}, u32[]{:S(2)}) collective-permute-start(bf16[32,4096]{1,0:T(8,128)(2,1)S(1)} %get-tuple-element.34), channel_id=1, source_target_pairs={{0,2},{1,3},{2,0},{3,1},{4,6},{5,7},{6,4},{7,5},{8,10},{9,11},{10,... | collective-permute-start | bytes 786440 | tf_op jit(solution)/shard_map/ppermute | solution.py:197
  49.7 13.1 %collective-permute-start.22 = (bf16[32,4096]{1,0:T(8,128)(2,1)S(1)}, bf16[32,4096]{1,0:T(8,128)(2,1)S(1)}, u32[]{:S(2)}, u32[]{:S(2)}) collective-permute-start(bf16[32,4096]{1,0:T(8,128)(2,1)S(1)} %get-tuple-element.36), channel_id=1, source_target_pairs={{0,4},{1,5},{2,6},{3,7},{4,0},{5,1},{6,2},{7,3},{8,12},{9,13},{10,... | collective-permute-start | bytes 786440 | tf_op jit(solution)/shard_map/ppermute | solution.py:197
  51.0 11.8 %collective-permute-start.23 = (bf16[32,4096]{1,0:T(8,128)(2,1)S(1)}, bf16[32,4096]{1,0:T(8,128)(2,1)S(1)}, u32[]{:S(2)}, u32[]{:S(2)}) collective-permute-start(bf16[32,4096]{1,0:T(8,128)(2,1)S(1)} %get-tuple-element.35), channel_id=1, source_target_pairs={{0,6},{1,7},{2,4},{3,5},{4,2},{5,3},{6,0},{7,1},{8,14},{9,15},{10,... | collective-permute-start | bytes 786440 | tf_op jit(solution)/shard_map/ppermute | solution.py:197
  58.5 20.9 %collective-permute-start.4 = (bf16[4,32,4096]{2,1,0:T(8,128)(2,1)S(1)}, bf16[4,32,4096]{2,1,0:T(8,128)(2,1)S(1)}, u32[]{:S(2)}, u32[]{:S(2)}) collective-permute-start(bf16[4,32,4096]{2,1,0:T(8,128)(2,1)S(1)} %get-tuple-element.14), channel_id=1, source_target_pairs={{0,1},{1,0},{2,3},{3,2},{4,5},{5,4},{6,7},{7,6},{8,9},{9,8},{10,11... | collective-permute-start | bytes 3145736 | tf_op jit(solution)/shard_map/ppermute | solution.py:190
  63.0 15.1 %collective-permute-start.25 = (bf16[32,4096]{1,0:T(8,128)(2,1)S(1)}, bf16[32,4096]{1,0:T(8,128)(2,1)S(1)}, u32[]{:S(2)}, u32[]{:S(2)}) collective-permute-start(bf16[32,4096]{1,0:T(8,128)(2,1)S(1)} %get-tuple-element.24.refs_0_), channel_id=1, source_target_pairs={{0,16},{8,24},{16,0},{24,8},{1,17},{9,25},{17,1},{25,9},{2,18},{10... | collective-permute-start | bytes 786440 | tf_op jit(solution)/shard_map/ppermute | solution.py:178
  66.1 15.6 %collective-permute-start.24 = (bf16[32,4096]{1,0:T(8,128)(2,1)S(1)}, bf16[32,4096]{1,0:T(8,128)(2,1)S(1)}, u32[]{:S(2)}, u32[]{:S(2)}) collective-permute-start(bf16[32,4096]{1,0:T(8,128)(2,1)S(1)} %get-tuple-element.24.refs_0_), channel_id=1, source_target_pairs={{0,8},{8,0},{16,24},{24,16},{1,9},{9,1},{17,25},{25,17},{2,10},{10... | collective-permute-start | bytes 786440 | tf_op jit(solution)/shard_map/ppermute | solution.py:178
  66.1 17.0 %collective-permute-start.26 = (bf16[32,4096]{1,0:T(8,128)(2,1)S(1)}, bf16[32,4096]{1,0:T(8,128)(2,1)S(1)}, u32[]{:S(2)}, u32[]{:S(2)}) collective-permute-start(bf16[32,4096]{1,0:T(8,128)(2,1)S(1)} %get-tuple-element.24.refs_0_), channel_id=1, source_target_pairs={{8,16},{16,8},{9,17},{17,9},{10,18},{18,10},{11,19},{19,11},{12,20... | collective-permute-start | bytes 786440 | tf_op jit(solution)/shard_map/ppermute | solution.py:178
  81.6 10.7 %collective-permute-start.6 = (bf16[32,4096]{1,0:T(8,128)(2,1)S(1)}, bf16[32,4096]{1,0:T(8,128)(2,1)S(1)}, u32[]{:S(2)}, u32[]{:S(2)}) collective-permute-start(bf16[32,4096]{1,0:T(8,128)(2,1)S(1)} %get-tuple-element.30), channel_id=1, source_target_pairs={{0,4},{1,5},{2,6},{3,7},{4,0},{5,1},{6,2},{7,3},{8,12},{9,13},{10,... | collective-permute-start | bytes 786440 | tf_op jit(solution)/shard_map/ppermute | solution.py:197
  89.1 30.9 %collective-permute-start.28 = (bf16[4,32,4096]{2,1,0:T(8,128)(2,1)S(1)}, bf16[4,32,4096]{2,1,0:T(8,128)(2,1)S(1)}, u32[]{:S(2)}, u32[]{:S(2)}) collective-permute-start(bf16[4,32,4096]{2,1,0:T(8,128)(2,1)S(1)} %get-tuple-element.20), channel_id=1, source_target_pairs={{0,1},{1,0},{2,3},{3,2},{4,5},{5,4},{6,7},{7,6},{8,9},{9,8},{10,11... | collective-permute-start | bytes 3145736 | tf_op jit(solution)/shard_map/ppermute | solution.py:190
  92.4 14.7 %collective-permute-start.9 = (bf16[32,4096]{1,0:T(8,128)(2,1)S(1)}, bf16[32,4096]{1,0:T(8,128)(2,1)S(1)}, u32[]{:S(2)}, u32[]{:S(2)}) collective-permute-start(bf16[32,4096]{1,0:T(8,128)(2,1)S(1)} %get-tuple-element.22.refs_0_), channel_id=1, source_target_pairs={{0,16},{8,24},{16,0},{24,8},{1,17},{9,25},{17,1},{25,9},{2,18},{10... | collective-permute-start | bytes 786440 | tf_op jit(solution)/shard_map/ppermute | solution.py:178
  96.5 11.9 %collective-permute-start.10 = (bf16[32,4096]{1,0:T(8,128)(2,1)S(1)}, bf16[32,4096]{1,0:T(8,128)(2,1)S(1)}, u32[]{:S(2)}, u32[]{:S(2)}) collective-permute-start(bf16[32,4096]{1,0:T(8,128)(2,1)S(1)} %get-tuple-element.22.refs_0_), channel_id=1, source_target_pairs={{8,16},{16,8},{9,17},{17,9},{10,18},{18,10},{11,19},{19,11},{12,20... | collective-permute-start | bytes 786440 | tf_op jit(solution)/shard_map/ppermute | solution.py:178
  97.2 12.5 %collective-permute-start.8 = (bf16[32,4096]{1,0:T(8,128)(2,1)S(1)}, bf16[32,4096]{1,0:T(8,128)(2,1)S(1)}, u32[]{:S(2)}, u32[]{:S(2)}) collective-permute-start(bf16[32,4096]{1,0:T(8,128)(2,1)S(1)} %get-tuple-element.22.refs_0_), channel_id=1, source_target_pairs={{0,8},{8,0},{16,24},{24,16},{1,9},{9,1},{17,25},{25,17},{2,10},{10... | collective-permute-start | bytes 786440 | tf_op jit(solution)/shard_map/ppermute | solution.py:178
  122.3 14.8 %collective-permute-start.30 = (bf16[32,4096]{1,0:T(8,128)(2,1)S(1)}, bf16[32,4096]{1,0:T(8,128)(2,1)S(1)}, u32[]{:S(2)}, u32[]{:S(2)}) collective-permute-start(bf16[32,4096]{1,0:T(8,128)(2,1)S(1)} %get-tuple-element.33), channel_id=1, source_target_pairs={{0,4},{1,5},{2,6},{3,7},{4,0},{5,1},{6,2},{7,3},{8,12},{9,13},{10,... | collective-permute-start | bytes 786440 | tf_op jit(solution)/shard_map/ppermute | solution.py:197
  122.5 14.7 %collective-permute-start.31 = (bf16[32,4096]{1,0:T(8,128)(2,1)S(1)}, bf16[32,4096]{1,0:T(8,128)(2,1)S(1)}, u32[]{:S(2)}, u32[]{:S(2)}) collective-permute-start(bf16[32,4096]{1,0:T(8,128)(2,1)S(1)} %get-tuple-element.32), channel_id=1, source_target_pairs={{0,6},{1,7},{2,4},{3,5},{4,2},{5,3},{6,0},{7,1},{8,14},{9,15},{10,... | collective-permute-start | bytes 786440 | tf_op jit(solution)/shard_map/ppermute | solution.py:197
  124.1 16.7 %collective-permute-start.13 = (bf16[32,4096]{1,0:T(8,128)(2,1)S(1)}, bf16[32,4096]{1,0:T(8,128)(2,1)S(1)}, u32[]{:S(2)}, u32[]{:S(2)}) collective-permute-start(bf16[32,4096]{1,0:T(8,128)(2,1)S(1)} %get-tuple-element.25), channel_id=1, source_target_pairs={{0,2},{1,3},{2,0},{3,1},{4,6},{5,7},{6,4},{7,5},{8,10},{9,11},{10,... | collective-permute-start | bytes 786440 | tf_op jit(solution)/shard_map/ppermute | solution.py:197
  126.1 21.5 %collective-permute-start.14 = (bf16[32,4096]{1,0:T(8,128)(2,1)S(1)}, bf16[32,4096]{1,0:T(8,128)(2,1)S(1)}, u32[]{:S(2)}, u32[]{:S(2)}) collective-permute-start(bf16[32,4096]{1,0:T(8,128)(2,1)S(1)} %get-tuple-element.27), channel_id=1, source_target_pairs={{0,4},{1,5},{2,6},{3,7},{4,0},{5,1},{6,2},{7,3},{8,12},{9,13},{10,... | collective-permute-start | bytes 786440 | tf_op jit(solution)/shard_map/ppermute | solution.py:197
  129.5 18.1 %collective-permute-start.15 = (bf16[32,4096]{1,0:T(8,128)(2,1)S(1)}, bf16[32,4096]{1,0:T(8,128)(2,1)S(1)}, u32[]{:S(2)}, u32[]{:S(2)}) collective-permute-start(bf16[32,4096]{1,0:T(8,128)(2,1)S(1)} %get-tuple-element.26), channel_id=1, source_target_pairs={{0,6},{1,7},{2,4},{3,5},{4,2},{5,3},{6,0},{7,1},{8,14},{9,15},{10,... | collective-permute-start | bytes 786440 | tf_op jit(solution)/shard_map/ppermute | solution.py:197
  (11 other events, 110.8 us)

commit v2 on v1

--- a/solution.py
+++ b/solution.py
@@ -16,6 +16,7 @@
 FLIP_DEPTH = 8
 FLIP_VMEM = 28 * 2**20
 SPARE_VMEM = 24 * 2**20
+FILTER_VMEM = 16 * 2**20
 
 
 def bessel_pair(times):
@@ -97,8 +98,6 @@
     row_at = lax.axis_index("row")
     col_at = lax.axis_index("col")
     trash = acc_ref.shape[0] - 1
-    shifted = pieces - 1 if pieces != lax.axis_size("row") else None
-    at_end = (row_at == 0) | (row_at == lax.axis_size("row") - 1)
 
     copies = [
         pltpu.make_async_copy(piece_refs[i], panel_ref.at[i], piece_sems.at[i])
@@ -121,8 +120,6 @@
             col = cols_ref[slot]
             row = jnp.where(slot < count, rows_ref[slot], trash)
             source = lax.div(col, per_dev) ^ row_at
-            if shifted is not None:
-                source = jnp.where(at_end & (source == shifted - 1), shifted, source)
             offset = pl.multiple_of((col & (per_dev - 1)) * TILE_SIZE, TILE_SIZE)
             picked = panel_ref[source, :, pl.ds(offset, TILE_SIZE)]
             acc_ref[row] += jnp.dot(picked, tiles_ref[slot], preferred_element_type=jnp.float32)
@@ -173,17 +170,22 @@
     return [(i, i ^ mask) for i in range(size)]
 
 
+def gather_masks(rows):
+    masks = []
+    held = [0]
+    step = rows // 2
+    while step:
+        masks += [(mask ^ step, mask, step) for mask in reversed(held)]
+        held += [mask ^ step for mask in held]
+        step //= 2
+    return masks
+
+
 def gather_parts(own, rows):
-    def send(value, pairs):
-        return lax.ppermute(value, "row", pairs)
-
-    if rows == 4:
-        far = send(own, flip(rows, 2))
-        near = send(own, flip(rows, 1))
-        inner = send(own, [(1, 2), (2, 1)])
-        outer = send(far, [(2, 3), (1, 0)])
-        return [own, near, far, inner, outer]
-    return [own] + [send(own, flip(rows, mask)) for mask in range(1, rows)]
+    parts = {0: own}
+    for mask, source, step in gather_masks(rows):
+        parts[mask] = lax.ppermute(parts[source], "row", flip(rows, step))
+    return [parts[mask] for mask in range(rows)]
 
 
 def reduce_parts(keep, send, cols):
@@ -195,10 +197,72 @@
     terms = [paired[0]]
     for half in range(1, cols // 2):
         terms.append(lax.ppermute(paired[half], "col", flip(cols, 2 * half)))
+    return terms
+
+
+def add_terms(terms):
     total = terms[0].astype(jnp.float32)
     for term in terms[1:]:
         total = total + term.astype(jnp.float32)
     return total.astype(jnp.bfloat16)
+
+
+def filter_kernel(begin, count, coef_ref, base_ref, first_ref, *refs):
+    out_hbm, stage_ref, sems = refs[-3:]
+    width, nodes = base_ref.shape
+    strip = min(nodes, 512)
+
+    def save(scale):
+        target = out_hbm.at[scale, pl.ds(begin, width)]
+        return pltpu.make_async_copy(stage_ref.at[scale], target, sems.at[scale])
+
+    for half in range(2):
+        scales = range(half * SCALES // 2, (half + 1) * SCALES // 2)
+
+        @pl.loop(0, nodes // strip)
+        def _(index):
+            span = pl.ds(pl.multiple_of(index * strip, strip), strip)
+            base = base_ref[:, span].astype(jnp.float32)
+            first = first_ref[:, span].astype(jnp.float32)
+            second = add_terms([ref[:, span] for ref in refs[:count]]).astype(jnp.float32)
+            bend = 2.0 * second - base
+            for scale in scales:
+                stage_ref[scale, :, span] = (
+                    coef_ref[0, scale] * base
+                    + coef_ref[1, scale] * first
+                    + coef_ref[2, scale] * bend
+                ).astype(jnp.bfloat16)
+
+        for scale in scales:
+            save(scale).start()
+    for scale in range(SCALES):
+        save(scale).wait()
+
+
+def write_filtered(coefs, base, first, terms, begin, channels, filtered):
+    width, nodes = base.shape
+    vectors = pl.BlockSpec(memory_space=pltpu.VMEM)
+    anywhere = pl.BlockSpec(memory_space=pl.ANY)
+    rest = [] if filtered is None else [filtered]
+    return pl.pallas_call(
+        functools.partial(filter_kernel, begin, len(terms)),
+        in_specs=[pl.BlockSpec(memory_space=pltpu.SMEM)]
+        + [vectors] * (2 + len(terms))
+        + [anywhere] * len(rest),
+        out_specs=anywhere,
+        scratch_shapes=[
+            pltpu.VMEM((SCALES, width, nodes), jnp.bfloat16),
+            pltpu.SemaphoreType.DMA((SCALES,)),
+        ],
+        out_shape=jax.ShapeDtypeStruct((SCALES, channels, nodes), jnp.bfloat16),
+        input_output_aliases={3 + len(terms): 0} if rest else {},
+        compiler_params=pltpu.CompilerParams(vmem_limit_bytes=FILTER_VMEM),
+        cost_estimate=pl.CostEstimate(
+            flops=8 * SCALES * width * nodes,
+            bytes_accessed=2 * SCALES * width * nodes,
+            transcendentals=0,
+        ),
+    )(coefs, base, first, *terms, *rest)
 
 
 def filter_bank(features, tile_rows, tile_cols, tile_count, tile_data):
@@ -220,21 +284,16 @@
         return reduce_parts(keep, send, cols)
 
     width = channels // CHUNKS
-    coef_zero, coef_one, coef_two = coefficients()
+    coefs = jnp.stack(coefficients())
     fields = [features[i * width : (i + 1) * width] for i in range(CHUNKS)]
-    firsts = [apply_operator(field) for field in fields]
+    firsts = []
+    for field in fields:
+        terms = apply_operator(field)
+        firsts.append(add_terms(terms))
     seconds = [apply_operator(first) for first in firsts]
-    filtered = jnp.zeros((SCALES, channels, nodes), jnp.bfloat16)
-    for chunk, (field, first, second) in enumerate(zip(fields, firsts, seconds)):
-        base = field.astype(jnp.float32)
-        first_wide = first.astype(jnp.float32)
-        second_wide = second.astype(jnp.float32)
-        block = (
-            coef_zero[:, None, None] * base[None]
-            + coef_one[:, None, None] * first_wide[None]
-            + coef_two[:, None, None] * (2.0 * second_wide - base)[None]
-        ).astype(jnp.bfloat16)
-        filtered = lax.dynamic_update_slice(filtered, block, (0, chunk * width, 0))
+    filtered = None
+    for chunk, (field, first, terms) in enumerate(zip(fields, firsts, seconds)):
+        filtered = write_filtered(coefs, field, first, terms, chunk * width, channels, filtered)
     return filtered.reshape(-1, nodes)
 
 

time: 153 us -> 145 us (0.948)
  starting transfers between devices: 46.2 us -> 31.1 us
  waiting for transfers between devices: 84.8 us -> 92 us
  Pallas kernels: 13.3 us -> 19 us
  other arithmetic: 6.99 us -> 1.35 us
    ppermute x16 -> x12, starting transfers between devices: 28.1 us -> 16.4 us  [gather_parts(): parts[mask] = lax.ppermute(parts[source], 'row', flip(rows, step))]
    pallas_call x0 -> x2, Pallas kernels: none -> 5.77 us  [write_filtered(): pl.pallas_call(functools.partial(filter_kernel, begin, len(terms)), in_sp...]
    ppermute x16 -> x12, waiting for transfers between devices: 57.7 us -> 63.2 us  [gather_parts(): parts[mask] = lax.ppermute(parts[source], 'row', flip(rows, step))]
    ppermute x12, starting transfers between devices: 17.9 us -> 14.5 us  [reduce_parts(): terms.append(lax.ppermute(paired[half], 'col', flip(cols, 2 * half)))]
    convert_element_type x4 -> x2, other arithmetic: 3.15 us -> 0.33 us  [add_terms(): return total.astype(jnp.bfloat16)]
    dynamic_update_slice x1 -> x0, other arithmetic: 2.51 us -> none  [filter_bank(): filtered = lax.dynamic_update_slice(filtered, block, (0, chunk * width, 0))]
    ppermute x12, waiting for transfers between devices: 27.1 us -> 28.8 us  [reduce_parts(): terms.append(lax.ppermute(paired[half], 'col', flip(cols, 2 * half)))]
  transfers between devices with their start and end apart: 32 -> 28, of which waited for: 15 -> 16; matrix products, arithmetic and copies ran while one was open for 1% -> 1% of each run, Pallas kernels for 7% -> 9%
where the time goes in v2:
time: 145 us
  waiting for transfers between devices  92 us (63%)
  starting transfers between devices  31.1 us (21%)
  Pallas kernels  19 us (13%)
    ppermute x12, waiting for transfers between devices, gather_parts(): parts[mask] = lax.ppermute(parts[source], 'row', flip(rows, step))  63.2 us
    ppermute x12, waiting for transfers between devices, reduce_parts(): terms.append(lax.ppermute(paired[half], 'col', flip(cols, 2 * half)))  28.8 us
    ppermute x12, starting transfers between devices, gather_parts(): parts[mask] = lax.ppermute(parts[source], 'row', flip(rows, step))  16.4 us
    ppermute x12, starting transfers between devices, reduce_parts(): terms.append(lax.ppermute(paired[half], 'col', flip(cols, 2 * half)))  14.5 us
    pallas_call x4, Pallas kernels, tile_products(): pl.pallas_call(functools.partial(tile_kernel, pieces, group), in_specs=[s...  10.9 us
    pallas_call x2, Pallas kernels, write_filtered(): pl.pallas_call(functools.partial(filter_kernel, begin, len(terms)), in_sp...  5.77 us
  transfers between devices with their start and end apart: 28, of which 16 were waited for; matrix products, arithmetic and copies ran while one was open for 1% of the time, Pallas kernels for 9%

profile of v2, /device:TPU:0, one launch (start us, length us, event | category | flops | bytes accessed | tf_op | source)
XLA Modules:
  0.0 145.3 jit_solution(11155134049955161250)
XLA Ops:
  1.1 4.1 %collective-permute-start.15 = (bf16[32,4096]{1,0:T(8,128)(2,1)S(1)}, bf16[32,4096]{1,0:T(8,128)(2,1)S(1)}, u32[]{:S(2)}, u32[]{:S(2)}) collective-permute-start(bf16[32,4096]{1,0:T(8,128)(2,1)S(1)} %get-tuple-element.35.refs_0_.base_ref), channel_id=1, source_target_pairs={{0,16},{8,24},{16,0},{24,8},{1,17},{9,25},{17,1},{25,9},{2,18},{10... | collective-permute-start | bytes 786440 | tf_op jit(solution)/shard_map/ppermute | solution.py:187
  6.8 10.4 %collective-permute-done.15.refs_2_ = bf16[32,4096]{1,0:T(8,128)(2,1)S(1)} collective-permute-done((bf16[32,4096]{1,0:T(8,128)(2,1)S(1)}, bf16[32,4096]{1,0:T(8,128)(2,1)S(1)}, u32[]{:S(2)}, u32[]{:S(2)}) %collective-permute-start.15) | collective-permute-done | bytes 262176 | tf_op jit(solution)/shard_map/ppermute | solution.py:187
  18.5 2.3 %shard_map.55.tiles_ref = bf16[512,128,128]{2,1,0:T(8,128)(2,1)S(1)} custom-call(s32[1]{0:T(128)} %bitcast.43.count_ref, bf16[512,128,128]{2,1,0:T(8,128)(2,1)} %bitcast.56), custom_call_target="tpu_custom_call" | custom-call | flops 1073741824 | bytes 16777216 | tf_op jit(solution)/shard_map/pallas_call | solution.py:73
  20.8 3.8 %collective-permute-done.16.refs_3_ = bf16[32,4096]{1,0:T(8,128)(2,1)S(1)} collective-permute-done((bf16[32,4096]{1,0:T(8,128)(2,1)S(1)}, bf16[32,4096]{1,0:T(8,128)(2,1)S(1)}, u32[]{:S(2)}, u32[]{:S(2)}) %collective-permute-start.16) | collective-permute-done | bytes 262176 | tf_op jit(solution)/shard_map/ppermute | solution.py:187
  24.6 2.7 %shard_map.58 = (bf16[4,32,4096]{2,1,0:T(8,128)(2,1)S(1)}, bf16[4,32,4096]{2,1,0:T(8,128)(2,1)S(1)}) custom-call(s32[1]{0:T(128)} %bitcast.46.count_ref, s32[512]{0:T(512)S(1)} %bitcast.48, s32[512]{0:T(512)S(1)} %bitcast.52, bf16[512,128,128]{2,1,0:T(8,128)(2,1)S(1)} %shard_map.55.tiles_ref, bf16[32,4096]{1,0:T(8,128)(2,1)S(1)} %get-tuple-element.35.refs_0_.base_ref, ...), custom_call_target="tpu_custom_call" | custom-call | flops 4294967296 | bytes 16777216 | tf_op jit(solution)/shard_map/pallas_call | solution.py:150
  27.5 4.5 %collective-permute-start.1 = (bf16[32,4096]{1,0:T(8,128)(2,1)S(1)}, bf16[32,4096]{1,0:T(8,128)(2,1)S(1)}, u32[]{:S(2)}, u32[]{:S(2)}) collective-permute-start(bf16[32,4096]{1,0:T(8,128)(2,1)S(1)} %get-tuple-element.36.refs_0_.base_ref), channel_id=1, source_target_pairs={{0,16},{8,24},{16,0},{24,8},{1,17},{9,25},{17,1},{25,9},{2,18},{10... | collective-permute-start | bytes 786440 | tf_op jit(solution)/shard_map/ppermute | solution.py:187
  33.0 11.6 %collective-permute-done.1.refs_2_ = bf16[32,4096]{1,0:T(8,128)(2,1)S(1)} collective-permute-done((bf16[32,4096]{1,0:T(8,128)(2,1)S(1)}, bf16[32,4096]{1,0:T(8,128)(2,1)S(1)}, u32[]{:S(2)}, u32[]{:S(2)}) %collective-permute-start.1) | collective-permute-done | bytes 262176 | tf_op jit(solution)/shard_map/ppermute | solution.py:187
  48.5 4.1 %collective-permute-done.2.refs_3_ = bf16[32,4096]{1,0:T(8,128)(2,1)S(1)} collective-permute-done((bf16[32,4096]{1,0:T(8,128)(2,1)S(1)}, bf16[32,4096]{1,0:T(8,128)(2,1)S(1)}, u32[]{:S(2)}, u32[]{:S(2)}) %collective-permute-start.2) | collective-permute-done | bytes 262176 | tf_op jit(solution)/shard_map/ppermute | solution.py:187
  52.6 2.7 %shard_map.56 = (bf16[4,32,4096]{2,1,0:T(8,128)(2,1)S(1)}, bf16[4,32,4096]{2,1,0:T(8,128)(2,1)S(1)}) custom-call(s32[1]{0:T(128)} %bitcast.44.count_ref, s32[512]{0:T(512)S(1)} %bitcast.49, s32[512]{0:T(512)S(1)} %bitcast.53, bf16[512,128,128]{2,1,0:T(8,128)(2,1)S(1)} %shard_map.55.tiles_ref, bf16[32,4096]{1,0:T(8,128)(2,1)S(1)} %get-tuple-element.36.refs_0_.base_ref, ...), custom_call_target="tpu_custom_call" | custom-call | flops 4294967296 | bytes 16777216 | tf_op jit(solution)/shard_map/pallas_call | solution.py:150
  55.4 4.3 %collective-permute-done.20 = bf16[32,4096]{1,0:T(8,128)(2,1)S(1)} collective-permute-done((bf16[32,4096]{1,0:T(8,128)(2,1)S(1)}, bf16[32,4096]{1,0:T(8,128)(2,1)S(1)}, u32[]{:S(2)}, u32[]{:S(2)}) %collective-permute-start.20) | collective-permute-done | bytes 262176 | tf_op jit(solution)/shard_map/ppermute | solution.py:199
  61.2 2.2 %collective-permute-start.22 = (bf16[32,4096]{1,0:T(8,128)(2,1)S(1)}, bf16[32,4096]{1,0:T(8,128)(2,1)S(1)}, u32[]{:S(2)}, u32[]{:S(2)}) collective-permute-start(bf16[32,4096]{1,0:T(8,128)(2,1)S(1)} %fusion.2.refs_0_.first_ref), channel_id=1, source_target_pairs={{0,16},{8,24},{16,0},{24,8},{1,17},{9,25},{17,1},{25,9},{2,18},{10... | collective-permute-start | bytes 786440 | tf_op jit(solution)/shard_map/ppermute | solution.py:187
  63.7 10.1 %collective-permute-done.22.refs_2_ = bf16[32,4096]{1,0:T(8,128)(2,1)S(1)} collective-permute-done((bf16[32,4096]{1,0:T(8,128)(2,1)S(1)}, bf16[32,4096]{1,0:T(8,128)(2,1)S(1)}, u32[]{:S(2)}, u32[]{:S(2)}) %collective-permute-start.22) | collective-permute-done | bytes 262176 | tf_op jit(solution)/shard_map/ppermute | solution.py:187
  77.9 3.2 %collective-permute-done.23.refs_3_ = bf16[32,4096]{1,0:T(8,128)(2,1)S(1)} collective-permute-done((bf16[32,4096]{1,0:T(8,128)(2,1)S(1)}, bf16[32,4096]{1,0:T(8,128)(2,1)S(1)}, u32[]{:S(2)}, u32[]{:S(2)}) %collective-permute-start.23) | collective-permute-done | bytes 262176 | tf_op jit(solution)/shard_map/ppermute | solution.py:187
  81.1 2.7 %shard_map.59 = (bf16[4,32,4096]{2,1,0:T(8,128)(2,1)S(1)}, bf16[4,32,4096]{2,1,0:T(8,128)(2,1)S(1)}) custom-call(s32[1]{0:T(128)} %bitcast.47.count_ref, s32[512]{0:T(512)S(1)} %bitcast.50, s32[512]{0:T(512)S(1)} %bitcast.54, bf16[512,128,128]{2,1,0:T(8,128)(2,1)S(1)} %shard_map.55.tiles_ref, bf16[32,4096]{1,0:T(8,128)(2,1)S(1)} %fusion.2.refs_0_.first_ref, ...), custom_call_target="tpu_custom_call" | custom-call | flops 4294967296 | bytes 16777216 | tf_op jit(solution)/shard_map/pallas_call | solution.py:150
  83.9 5.5 %collective-permute-done.6 = bf16[32,4096]{1,0:T(8,128)(2,1)S(1)} collective-permute-done((bf16[32,4096]{1,0:T(8,128)(2,1)S(1)}, bf16[32,4096]{1,0:T(8,128)(2,1)S(1)}, u32[]{:S(2)}, u32[]{:S(2)}) %collective-permute-start.6) | collective-permute-done | bytes 262176 | tf_op jit(solution)/shard_map/ppermute | solution.py:199
  92.9 11.7 %collective-permute-done.8.refs_2_ = bf16[32,4096]{1,0:T(8,128)(2,1)S(1)} collective-permute-done((bf16[32,4096]{1,0:T(8,128)(2,1)S(1)}, bf16[32,4096]{1,0:T(8,128)(2,1)S(1)}, u32[]{:S(2)}, u32[]{:S(2)}) %collective-permute-start.8) | collective-permute-done | bytes 262176 | tf_op jit(solution)/shard_map/ppermute | solution.py:187
  104.6 8.2 %collective-permute-done.9.refs_3_ = bf16[32,4096]{1,0:T(8,128)(2,1)S(1)} collective-permute-done((bf16[32,4096]{1,0:T(8,128)(2,1)S(1)}, bf16[32,4096]{1,0:T(8,128)(2,1)S(1)}, u32[]{:S(2)}, u32[]{:S(2)}) %collective-permute-start.9) | collective-permute-done | bytes 262176 | tf_op jit(solution)/shard_map/ppermute | solution.py:187
  112.9 2.7 %shard_map.57 = (bf16[4,32,4096]{2,1,0:T(8,128)(2,1)S(1)}, bf16[4,32,4096]{2,1,0:T(8,128)(2,1)S(1)}) custom-call(s32[1]{0:T(128)} %bitcast.45.count_ref, s32[512]{0:T(512)S(1)} %bitcast.51, s32[512]{0:T(512)S(1)} %bitcast.55, bf16[512,128,128]{2,1,0:T(8,128)(2,1)S(1)} %shard_map.55.tiles_ref, bf16[32,4096]{1,0:T(8,128)(2,1)S(1)} %fusion.5.refs_0_.first_ref, ...), custom_call_target="tpu_custom_call" | custom-call | flops 4294967296 | bytes 16777216 | tf_op jit(solution)/shard_map/pallas_call | solution.py:150
  122.3 3.9 %collective-permute-done.27.refs_3_ = bf16[32,4096]{1,0:T(8,128)(2,1)S(1)} collective-permute-done((bf16[32,4096]{1,0:T(8,128)(2,1)S(1)}, bf16[32,4096]{1,0:T(8,128)(2,1)S(1)}, u32[]{:S(2)}, u32[]{:S(2)}) %collective-permute-start.27) | collective-permute-done | bytes 262176 | tf_op jit(solution)/shard_map/ppermute | solution.py:199
  127.2 4.5 %collective-permute-done.26.refs_2_ = bf16[32,4096]{1,0:T(8,128)(2,1)S(1)} collective-permute-done((bf16[32,4096]{1,0:T(8,128)(2,1)S(1)}, bf16[32,4096]{1,0:T(8,128)(2,1)S(1)}, u32[]{:S(2)}, u32[]{:S(2)}) %collective-permute-start.26) | collective-permute-done | bytes 262176 | tf_op jit(solution)/shard_map/ppermute | solution.py:199
  131.8 2.9 %shard_map.60.refs_4_ = bf16[8,64,4096]{2,1,0:T(8,128)(2,1)} custom-call(f32[3,8]{1,0:T(4,128)S(1)} %pad_maximum_fusion.coef_ref, bf16[32,4096]{1,0:T(8,128)(2,1)S(1)} %get-tuple-element.35.refs_0_.base_ref, bf16[32,4096]{1,0:T(8,128)(2,1)S(1)} %fusion.2.refs_0_.first_ref, bf16[32,4096]{1,0:T(8,128)(2,1)S(1)} %get-tuple-element.24.refs_0_, ...), custom_call_target="tpu_custom_call" | custom-call | flops 8388608 | bytes 2097152 | tf_op jit(solution)/shard_map/pallas_call | solution.py:247
  134.7 2.7 %collective-permute-done.13.refs_3_ = bf16[32,4096]{1,0:T(8,128)(2,1)S(1)} collective-permute-done((bf16[32,4096]{1,0:T(8,128)(2,1)S(1)}, bf16[32,4096]{1,0:T(8,128)(2,1)S(1)}, u32[]{:S(2)}, u32[]{:S(2)}) %collective-permute-start.13) | collective-permute-done | bytes 262176 | tf_op jit(solution)/shard_map/ppermute | solution.py:199
  137.4 5.0 %collective-permute-done.12.refs_2_ = bf16[32,4096]{1,0:T(8,128)(2,1)S(1)} collective-permute-done((bf16[32,4096]{1,0:T(8,128)(2,1)S(1)}, bf16[32,4096]{1,0:T(8,128)(2,1)S(1)}, u32[]{:S(2)}, u32[]{:S(2)}) %collective-permute-start.12) | collective-permute-done | bytes 262176 | tf_op jit(solution)/shard_map/ppermute | solution.py:199
  142.5 2.9 %shard_map.61 = bf16[8,64,4096]{2,1,0:T(8,128)(2,1)} custom-call(f32[3,8]{1,0:T(4,128)S(1)} %pad_maximum_fusion.coef_ref, bf16[32,4096]{1,0:T(8,128)(2,1)S(1)} %get-tuple-element.36.refs_0_.base_ref, bf16[32,4096]{1,0:T(8,128)(2,1)S(1)} %fusion.5.refs_0_.first_ref, bf16[32,4096]{1,0:T(8,128)(2,1)S(1)} %get-tuple-element.31.refs_0_, ...), custom_call_target="tpu_custom_call", output_to_operand_aliasing={{}: (7, {})} | custom-call | flops 8388608 | bytes 2097152 | tf_op jit(solution)/shard_map/pallas_call | solution.py:247
  (53 shorter events, 25.6 us)
Async XLA Ops:
  1.1 16.2 %collective-permute-start.15 = (bf16[32,4096]{1,0:T(8,128)(2,1)S(1)}, bf16[32,4096]{1,0:T(8,128)(2,1)S(1)}, u32[]{:S(2)}, u32[]{:S(2)}) collective-permute-start(bf16[32,4096]{1,0:T(8,128)(2,1)S(1)} %get-tuple-element.35.refs_0_.base_ref), channel_id=1, source_target_pairs={{0,16},{8,24},{16,0},{24,8},{1,17},{9,25},{17,1},{25,9},{2,18},{10... | collective-permute-start | bytes 786440 | tf_op jit(solution)/shard_map/ppermute | solution.py:187
  5.2 15.6 %collective-permute-start.14 = (bf16[32,4096]{1,0:T(8,128)(2,1)S(1)}, bf16[32,4096]{1,0:T(8,128)(2,1)S(1)}, u32[]{:S(2)}, u32[]{:S(2)}) collective-permute-start(bf16[32,4096]{1,0:T(8,128)(2,1)S(1)} %get-tuple-element.35.refs_0_.base_ref), channel_id=1, source_target_pairs={{0,8},{8,0},{16,24},{24,16},{1,9},{9,1},{17,25},{25,17},{2,10},{10... | collective-permute-start | bytes 786440 | tf_op jit(solution)/shard_map/ppermute | solution.py:187
  27.4 17.4 %collective-permute-start.17 = (bf16[4,32,4096]{2,1,0:T(8,128)(2,1)S(1)}, bf16[4,32,4096]{2,1,0:T(8,128)(2,1)S(1)}, u32[]{:S(2)}, u32[]{:S(2)}) collective-permute-start(bf16[4,32,4096]{2,1,0:T(8,128)(2,1)S(1)} %get-tuple-element.18), channel_id=1, source_target_pairs={{0,1},{1,0},{2,3},{3,2},{4,5},{5,4},{6,7},{7,6},{8,9},{9,8},{10,11... | collective-permute-start | bytes 3145736 | tf_op jit(solution)/shard_map/ppermute | solution.py:192
  27.5 17.1 %collective-permute-start.1 = (bf16[32,4096]{1,0:T(8,128)(2,1)S(1)}, bf16[32,4096]{1,0:T(8,128)(2,1)S(1)}, u32[]{:S(2)}, u32[]{:S(2)}) collective-permute-start(bf16[32,4096]{1,0:T(8,128)(2,1)S(1)} %get-tuple-element.36.refs_0_.base_ref), channel_id=1, source_target_pairs={{0,16},{8,24},{16,0},{24,8},{1,17},{9,25},{17,1},{25,9},{2,18},{10... | collective-permute-start | bytes 786440 | tf_op jit(solution)/shard_map/ppermute | solution.py:187
  31.9 16.6 %collective-permute-start = (bf16[32,4096]{1,0:T(8,128)(2,1)S(1)}, bf16[32,4096]{1,0:T(8,128)(2,1)S(1)}, u32[]{:S(2)}, u32[]{:S(2)}) collective-permute-start(bf16[32,4096]{1,0:T(8,128)(2,1)S(1)} %get-tuple-element.36.refs_0_.base_ref), channel_id=1, source_target_pairs={{0,8},{8,0},{16,24},{24,16},{1,9},{9,1},{17,25},{25,17},{2,10},{10... | collective-permute-start | bytes 786440 | tf_op jit(solution)/shard_map/ppermute | solution.py:187
  44.9 10.4 %collective-permute-start.18 = (bf16[32,4096]{1,0:T(8,128)(2,1)S(1)}, bf16[32,4096]{1,0:T(8,128)(2,1)S(1)}, u32[]{:S(2)}, u32[]{:S(2)}) collective-permute-start(bf16[32,4096]{1,0:T(8,128)(2,1)S(1)} %get-tuple-element.25), channel_id=1, source_target_pairs={{0,2},{1,3},{2,0},{3,1},{4,6},{5,7},{6,4},{7,5},{8,10},{9,11},{10,... | collective-permute-start | bytes 786440 | tf_op jit(solution)/shard_map/ppermute | solution.py:199
  45.7 14.0 %collective-permute-start.20 = (bf16[32,4096]{1,0:T(8,128)(2,1)S(1)}, bf16[32,4096]{1,0:T(8,128)(2,1)S(1)}, u32[]{:S(2)}, u32[]{:S(2)}) collective-permute-start(bf16[32,4096]{1,0:T(8,128)(2,1)S(1)} %get-tuple-element.26), channel_id=1, source_target_pairs={{0,6},{1,7},{2,4},{3,5},{4,2},{5,3},{6,0},{7,1},{8,14},{9,15},{10,... | collective-permute-start | bytes 786440 | tf_op jit(solution)/shard_map/ppermute | solution.py:199
  47.7 13.3 %collective-permute-start.19 = (bf16[32,4096]{1,0:T(8,128)(2,1)S(1)}, bf16[32,4096]{1,0:T(8,128)(2,1)S(1)}, u32[]{:S(2)}, u32[]{:S(2)}) collective-permute-start(bf16[32,4096]{1,0:T(8,128)(2,1)S(1)} %get-tuple-element.27), channel_id=1, source_target_pairs={{0,4},{1,5},{2,6},{3,7},{4,0},{5,1},{6,2},{7,3},{8,12},{9,13},{10,... | collective-permute-start | bytes 786440 | tf_op jit(solution)/shard_map/ppermute | solution.py:199
  55.3 18.5 %collective-permute-start.3 = (bf16[4,32,4096]{2,1,0:T(8,128)(2,1)S(1)}, bf16[4,32,4096]{2,1,0:T(8,128)(2,1)S(1)}, u32[]{:S(2)}, u32[]{:S(2)}) collective-permute-start(bf16[4,32,4096]{2,1,0:T(8,128)(2,1)S(1)} %get-tuple-element.14), channel_id=1, source_target_pairs={{0,1},{1,0},{2,3},{3,2},{4,5},{5,4},{6,7},{7,6},{8,9},{9,8},{10,11... | collective-permute-start | bytes 3145736 | tf_op jit(solution)/shard_map/ppermute | solution.py:192
  61.2 12.6 %collective-permute-start.22 = (bf16[32,4096]{1,0:T(8,128)(2,1)S(1)}, bf16[32,4096]{1,0:T(8,128)(2,1)S(1)}, u32[]{:S(2)}, u32[]{:S(2)}) collective-permute-start(bf16[32,4096]{1,0:T(8,128)(2,1)S(1)} %fusion.2.refs_0_.first_ref), channel_id=1, source_target_pairs={{0,16},{8,24},{16,0},{24,8},{1,17},{9,25},{17,1},{25,9},{2,18},{10... | collective-permute-start | bytes 786440 | tf_op jit(solution)/shard_map/ppermute | solution.py:187
  63.4 14.5 %collective-permute-start.21 = (bf16[32,4096]{1,0:T(8,128)(2,1)S(1)}, bf16[32,4096]{1,0:T(8,128)(2,1)S(1)}, u32[]{:S(2)}, u32[]{:S(2)}) collective-permute-start(bf16[32,4096]{1,0:T(8,128)(2,1)S(1)} %fusion.2.refs_0_.first_ref), channel_id=1, source_target_pairs={{0,8},{8,0},{16,24},{24,16},{1,9},{9,1},{17,25},{25,17},{2,10},{10... | collective-permute-start | bytes 786440 | tf_op jit(solution)/shard_map/ppermute | solution.py:187
  74.0 9.9 %collective-permute-start.4 = (bf16[32,4096]{1,0:T(8,128)(2,1)S(1)}, bf16[32,4096]{1,0:T(8,128)(2,1)S(1)}, u32[]{:S(2)}, u32[]{:S(2)}) collective-permute-start(bf16[32,4096]{1,0:T(8,128)(2,1)S(1)} %get-tuple-element.32), channel_id=1, source_target_pairs={{0,2},{1,3},{2,0},{3,1},{4,6},{5,7},{6,4},{7,5},{8,10},{9,11},{10,... | collective-permute-start | bytes 786440 | tf_op jit(solution)/shard_map/ppermute | solution.py:199
  75.5 13.9 %collective-permute-start.6 = (bf16[32,4096]{1,0:T(8,128)(2,1)S(1)}, bf16[32,4096]{1,0:T(8,128)(2,1)S(1)}, u32[]{:S(2)}, u32[]{:S(2)}) collective-permute-start(bf16[32,4096]{1,0:T(8,128)(2,1)S(1)} %get-tuple-element.33), channel_id=1, source_target_pairs={{0,6},{1,7},{2,4},{3,5},{4,2},{5,3},{6,0},{7,1},{8,14},{9,15},{10,... | collective-permute-start | bytes 786440 | tf_op jit(solution)/shard_map/ppermute | solution.py:199
  77.4 13.5 %collective-permute-start.5 = (bf16[32,4096]{1,0:T(8,128)(2,1)S(1)}, bf16[32,4096]{1,0:T(8,128)(2,1)S(1)}, u32[]{:S(2)}, u32[]{:S(2)}) collective-permute-start(bf16[32,4096]{1,0:T(8,128)(2,1)S(1)} %get-tuple-element.34), channel_id=1, source_target_pairs={{0,4},{1,5},{2,6},{3,7},{4,0},{5,1},{6,2},{7,3},{8,12},{9,13},{10,... | collective-permute-start | bytes 786440 | tf_op jit(solution)/shard_map/ppermute | solution.py:199
  83.8 31.9 %collective-permute-start.24 = (bf16[4,32,4096]{2,1,0:T(8,128)(2,1)S(1)}, bf16[4,32,4096]{2,1,0:T(8,128)(2,1)S(1)}, u32[]{:S(2)}, u32[]{:S(2)}) collective-permute-start(bf16[4,32,4096]{2,1,0:T(8,128)(2,1)S(1)} %get-tuple-element.20), channel_id=1, source_target_pairs={{0,1},{1,0},{2,3},{3,2},{4,5},{5,4},{6,7},{7,6},{8,9},{9,8},{10,11... | collective-permute-start | bytes 3145736 | tf_op jit(solution)/shard_map/ppermute | solution.py:192
  91.0 13.6 %collective-permute-start.8 = (bf16[32,4096]{1,0:T(8,128)(2,1)S(1)}, bf16[32,4096]{1,0:T(8,128)(2,1)S(1)}, u32[]{:S(2)}, u32[]{:S(2)}) collective-permute-start(bf16[32,4096]{1,0:T(8,128)(2,1)S(1)} %fusion.5.refs_0_.first_ref), channel_id=1, source_target_pairs={{0,16},{8,24},{16,0},{24,8},{1,17},{9,25},{17,1},{25,9},{2,18},{10... | collective-permute-start | bytes 786440 | tf_op jit(solution)/shard_map/ppermute | solution.py:187
  91.3 13.3 %collective-permute-start.7 = (bf16[32,4096]{1,0:T(8,128)(2,1)S(1)}, bf16[32,4096]{1,0:T(8,128)(2,1)S(1)}, u32[]{:S(2)}, u32[]{:S(2)}) collective-permute-start(bf16[32,4096]{1,0:T(8,128)(2,1)S(1)} %fusion.5.refs_0_.first_ref), channel_id=1, source_target_pairs={{0,8},{8,0},{16,24},{24,16},{1,9},{9,1},{17,25},{25,17},{2,10},{10... | collective-permute-start | bytes 786440 | tf_op jit(solution)/shard_map/ppermute | solution.py:187
  104.6 8.2 %collective-permute-start.9 = (bf16[32,4096]{1,0:T(8,128)(2,1)S(1)}, bf16[32,4096]{1,0:T(8,128)(2,1)S(1)}, u32[]{:S(2)}, u32[]{:S(2)}) collective-permute-start(bf16[32,4096]{1,0:T(8,128)(2,1)S(1)} %collective-permute-done.8.refs_2_), channel_id=1, source_target_pairs={{0,8},{8,0},{16,24},{24,16},{1,9},{9,1},{17,25},{25,17},{2,10},{10... | collective-permute-start | bytes 786440 | tf_op jit(solution)/shard_map/ppermute | solution.py:187
  115.9 10.2 %collective-permute-start.27 = (bf16[32,4096]{1,0:T(8,128)(2,1)S(1)}, bf16[32,4096]{1,0:T(8,128)(2,1)S(1)}, u32[]{:S(2)}, u32[]{:S(2)}) collective-permute-start(bf16[32,4096]{1,0:T(8,128)(2,1)S(1)} %get-tuple-element.21), channel_id=1, source_target_pairs={{0,6},{1,7},{2,4},{3,5},{4,2},{5,3},{6,0},{7,1},{8,14},{9,15},{10,... | collective-permute-start | bytes 786440 | tf_op jit(solution)/shard_map/ppermute | solution.py:199
  117.9 13.8 %collective-permute-start.26 = (bf16[32,4096]{1,0:T(8,128)(2,1)S(1)}, bf16[32,4096]{1,0:T(8,128)(2,1)S(1)}, u32[]{:S(2)}, u32[]{:S(2)}) collective-permute-start(bf16[32,4096]{1,0:T(8,128)(2,1)S(1)} %get-tuple-element.22), channel_id=1, source_target_pairs={{0,4},{1,5},{2,6},{3,7},{4,0},{5,1},{6,2},{7,3},{8,12},{9,13},{10,... | collective-permute-start | bytes 786440 | tf_op jit(solution)/shard_map/ppermute | solution.py:199
  118.4 13.3 %collective-permute-start.25 = (bf16[32,4096]{1,0:T(8,128)(2,1)S(1)}, bf16[32,4096]{1,0:T(8,128)(2,1)S(1)}, u32[]{:S(2)}, u32[]{:S(2)}) collective-permute-start(bf16[32,4096]{1,0:T(8,128)(2,1)S(1)} %get-tuple-element.23), channel_id=1, source_target_pairs={{0,2},{1,3},{2,0},{3,1},{4,6},{5,7},{6,4},{7,5},{8,10},{9,11},{10,... | collective-permute-start | bytes 786440 | tf_op jit(solution)/shard_map/ppermute | solution.py:199
  119.8 17.6 %collective-permute-start.13 = (bf16[32,4096]{1,0:T(8,128)(2,1)S(1)}, bf16[32,4096]{1,0:T(8,128)(2,1)S(1)}, u32[]{:S(2)}, u32[]{:S(2)}) collective-permute-start(bf16[32,4096]{1,0:T(8,128)(2,1)S(1)} %get-tuple-element.28), channel_id=1, source_target_pairs={{0,6},{1,7},{2,4},{3,5},{4,2},{5,3},{6,0},{7,1},{8,14},{9,15},{10,... | collective-permute-start | bytes 786440 | tf_op jit(solution)/shard_map/ppermute | solution.py:199
  121.8 20.7 %collective-permute-start.12 = (bf16[32,4096]{1,0:T(8,128)(2,1)S(1)}, bf16[32,4096]{1,0:T(8,128)(2,1)S(1)}, u32[]{:S(2)}, u32[]{:S(2)}) collective-permute-start(bf16[32,4096]{1,0:T(8,128)(2,1)S(1)} %get-tuple-element.29), channel_id=1, source_target_pairs={{0,4},{1,5},{2,6},{3,7},{4,0},{5,1},{6,2},{7,3},{8,12},{9,13},{10,... | collective-permute-start | bytes 786440 | tf_op jit(solution)/shard_map/ppermute | solution.py:199
  126.1 16.3 %collective-permute-start.11 = (bf16[32,4096]{1,0:T(8,128)(2,1)S(1)}, bf16[32,4096]{1,0:T(8,128)(2,1)S(1)}, u32[]{:S(2)}, u32[]{:S(2)}) collective-permute-start(bf16[32,4096]{1,0:T(8,128)(2,1)S(1)} %get-tuple-element.30), channel_id=1, source_target_pairs={{0,2},{1,3},{2,0},{3,1},{4,6},{5,7},{6,4},{7,5},{8,10},{9,11},{10,... | collective-permute-start | bytes 786440 | tf_op jit(solution)/shard_map/ppermute | solution.py:199
  (6 other events, 38.9 us)

commit v3 on v2

--- a/solution.py
+++ b/solution.py
@@ -15,7 +15,7 @@
 FLIP_GROUP = 32
 FLIP_DEPTH = 8
 FLIP_VMEM = 28 * 2**20
-SPARE_VMEM = 24 * 2**20
+PRODUCT_VMEM = 16 * 2**20
 FILTER_VMEM = 16 * 2**20
 
 
@@ -41,8 +41,13 @@
     return (bessel_zero, -2.0 * bessel_one, 2.0 * (bessel_zero - 2.0 * bessel_one / times))
 
 
-def flip_kernel(group, depth, count_ref, tiles_hbm, flipped_ref, tiles_ref, sems):
-    live_groups = lax.div(count_ref[0] + (group - 1), group)
+def flip_kernel(group, depth, per_dev, count_ref, rows_ref, cols_ref, tiles_hbm, *refs):
+    flipped_ref, order_rows_ref, order_cols_ref, split_ref, tiles_ref, sems = refs
+    slots = flipped_ref.shape[0]
+    count = count_ref[0]
+    row_at = lax.axis_index("row")
+    last = lax.axis_size("row") - 1
+    live_groups = lax.div(count + (group - 1), group)
 
     def load(index):
         slot = lax.rem(index, depth)
@@ -55,53 +60,69 @@
         def _():
             load(index).start()
 
-    @pl.loop(0, live_groups)
-    def _(index):
+    def one_group(index, split):
+        front, back = split
         load(index).wait()
         for g in range(group):
-            flipped_ref[index * group + g] = tiles_ref[lax.rem(index, depth), g].T
+            slot = index * group + g
+            col = cols_ref[slot]
+            source = lax.div(col, per_dev) ^ row_at
+            to_back = (source == last) & (slot < count)
+            place = jnp.where(to_back, slots - 1 - back, front)
+            flipped_ref[place] = tiles_ref[lax.rem(index, depth), g].T
+            order_rows_ref[place] = rows_ref[slot]
+            order_cols_ref[place] = source * per_dev + (col & (per_dev - 1))
+            back = back + to_back.astype(jnp.int32)
+            front = front + ((source != last) & (slot < count)).astype(jnp.int32)
 
         @pl.when(index + depth < live_groups)
         def _():
             load(index + depth).start()
 
-
-def flip_tiles(live, slot_data):
+        return front, back
+
+    front, back = lax.fori_loop(0, live_groups, one_group, (jnp.int32(0), jnp.int32(0)))
+    split_ref[0] = front
+    split_ref[1] = back
+
+
+def flip_tiles(live, slot_rows, slot_cols, slot_data, per_dev):
     slots = slot_data.shape[0]
     group = min(FLIP_GROUP, slots)
     depth = min(FLIP_DEPTH, slots // group)
+    scalars = pl.BlockSpec(memory_space=pltpu.SMEM)
+    numbers = jax.ShapeDtypeStruct((slots,), jnp.int32)
     return pl.pallas_call(
-        functools.partial(flip_kernel, group, depth),
-        in_specs=[pl.BlockSpec(memory_space=pltpu.SMEM), pl.BlockSpec(memory_space=pl.ANY)],
-        out_specs=pl.BlockSpec(memory_space=pltpu.VMEM),
+        functools.partial(flip_kernel, group, depth, per_dev),
+        in_specs=[scalars] * 3 + [pl.BlockSpec(memory_space=pl.ANY)],
+        out_specs=[pl.BlockSpec(memory_space=pltpu.VMEM)] + [scalars] * 3,
         scratch_shapes=[
             pltpu.VMEM((depth, group, TILE_SIZE, TILE_SIZE), jnp.bfloat16),
             pltpu.SemaphoreType.DMA((depth,)),
         ],
-        out_shape=jax.ShapeDtypeStruct(slot_data.shape, jnp.bfloat16),
+        out_shape=[
+            jax.ShapeDtypeStruct(slot_data.shape, jnp.bfloat16),
+            numbers,
+            numbers,
+            jax.ShapeDtypeStruct((2,), jnp.int32),
+        ],
         compiler_params=pltpu.CompilerParams(vmem_limit_bytes=FLIP_VMEM),
         cost_estimate=pl.CostEstimate(
             flops=slots * TILE_SIZE**3,
             bytes_accessed=slots * TILE_SIZE * TILE_SIZE * 2,
             transcendentals=0,
         ),
-    )(live, slot_data)
-
-
-def tile_kernel(pieces, group, count_ref, rows_ref, cols_ref, tiles_ref, *refs):
-    piece_refs = refs[:pieces]
-    keep_ref, send_ref = refs[pieces : pieces + 2]
-    panel_ref, acc_ref, piece_sems = refs[pieces + 2 :]
-    halves = keep_ref.shape[0]
+    )(live, slot_rows, slot_cols, slot_data)
+
+
+def front_kernel(group, split_ref, rows_ref, cols_ref, tiles_ref, *refs):
+    acc_ref, panel_ref, sems = refs[-3:]
+    piece_refs = refs[:-3]
     per_dev = panel_ref.shape[2] // TILE_SIZE
-    count = count_ref[0]
-    row_at = lax.axis_index("row")
-    col_at = lax.axis_index("col")
     trash = acc_ref.shape[0] - 1
-
+    front = split_ref[0]
     copies = [
-        pltpu.make_async_copy(piece_refs[i], panel_ref.at[i], piece_sems.at[i])
-        for i in range(pieces)
+        pltpu.make_async_copy(ref, panel_ref.at[i], sems.at[i]) for i, ref in enumerate(piece_refs)
     ]
     for copy in copies:
         copy.start()
@@ -113,19 +134,39 @@
     for copy in copies:
         copy.wait()
 
-    @pl.loop(0, lax.div(count + (group - 1), group))
+    @pl.loop(0, lax.div(front + (group - 1), group))
     def _(index):
         for g in range(group):
             slot = index * group + g
-            col = cols_ref[slot]
-            row = jnp.where(slot < count, rows_ref[slot], trash)
-            source = lax.div(col, per_dev) ^ row_at
+            valid = slot < front
+            col = jnp.where(valid, cols_ref[slot], 0)
+            row = jnp.where(valid, rows_ref[slot], trash)
             offset = pl.multiple_of((col & (per_dev - 1)) * TILE_SIZE, TILE_SIZE)
-            picked = panel_ref[source, :, pl.ds(offset, TILE_SIZE)]
+            picked = panel_ref[lax.div(col, per_dev), :, pl.ds(offset, TILE_SIZE)]
             acc_ref[row] += jnp.dot(picked, tiles_ref[slot], preferred_element_type=jnp.float32)
 
+
+def back_kernel(group, split_ref, rows_ref, cols_ref, tiles_ref, piece_ref, acc_in, *refs):
+    acc_ref, keep_ref, send_ref = refs
+    halves = keep_ref.shape[0]
+    slots = tiles_ref.shape[0]
+    per_dev = piece_ref.shape[1] // TILE_SIZE
+    trash = acc_ref.shape[0] - 1
+    back = split_ref[1]
+    col_at = lax.axis_index("col")
     pair = lax.div(col_at, 2)
     core = col_at & 1
+
+    @pl.loop(0, lax.div(back + (group - 1), group))
+    def _(index):
+        for g in range(group):
+            slot = slots - group * (index + 1) + g
+            valid = slot >= slots - back
+            col = jnp.where(valid, cols_ref[slot], 0)
+            row = jnp.where(valid, rows_ref[slot], trash)
+            offset = pl.multiple_of((col & (per_dev - 1)) * TILE_SIZE, TILE_SIZE)
+            picked = piece_ref[:, pl.ds(offset, TILE_SIZE)]
+            acc_ref[row] += jnp.dot(picked, tiles_ref[slot], preferred_element_type=jnp.float32)
 
     @pl.loop(0, halves)
     def _(h):
@@ -138,32 +179,46 @@
                 )
 
 
-def tile_products(parts, live, slot_rows, slot_cols, tiles, block_rows, halves):
+def tile_products(parts, ordered, block_rows, halves):
+    tiles, slot_rows, slot_cols, split = ordered
     channels, nodes = parts[0].shape
-    slots = slot_rows.shape[0]
+    slots = tiles.shape[0]
     group = min(GROUP, slots)
-    pieces = len(parts)
-    out = jax.ShapeDtypeStruct((halves, channels, nodes), jnp.bfloat16)
+    pieces = len(parts) - 1
     scalars = pl.BlockSpec(memory_space=pltpu.SMEM)
     vectors = pl.BlockSpec(memory_space=pltpu.VMEM)
-    scratch = channels * (4 * (block_rows + 8) * TILE_SIZE + 2 * pieces * nodes)
-    return pl.pallas_call(
-        functools.partial(tile_kernel, pieces, group),
+    sums = jax.ShapeDtypeStruct((block_rows + 8, channels, TILE_SIZE), jnp.float32)
+    out = jax.ShapeDtypeStruct((halves, channels, nodes), jnp.bfloat16)
+
+    def cost(share):
+        return pl.CostEstimate(
+            flops=int(share * 16 * slots * channels * TILE_SIZE * TILE_SIZE),
+            bytes_accessed=int(share * slots * TILE_SIZE * TILE_SIZE * 2),
+            transcendentals=0,
+        )
+
+    front = pl.pallas_call(
+        functools.partial(front_kernel, group),
         in_specs=[scalars] * 3 + [vectors] + [pl.BlockSpec(memory_space=pl.ANY)] * pieces,
-        out_specs=[vectors] * 2,
+        out_specs=vectors,
         scratch_shapes=[
             pltpu.VMEM((pieces, channels, nodes), jnp.bfloat16),
-            pltpu.VMEM((block_rows + 8, channels, TILE_SIZE), jnp.float32),
             pltpu.SemaphoreType.DMA((pieces,)),
         ],
-        out_shape=[out, out],
-        compiler_params=pltpu.CompilerParams(vmem_limit_bytes=scratch + SPARE_VMEM),
-        cost_estimate=pl.CostEstimate(
-            flops=2 * slots * channels * TILE_SIZE * TILE_SIZE * 8,
-            bytes_accessed=slots * TILE_SIZE * TILE_SIZE * 2,
-            transcendentals=0,
-        ),
-    )(live, slot_rows, slot_cols, tiles, *parts)
+        out_shape=sums,
+        compiler_params=pltpu.CompilerParams(vmem_limit_bytes=PRODUCT_VMEM),
+        cost_estimate=cost(0.7),
+    )(split, slot_rows, slot_cols, tiles, *parts[:-1])
+    _, keep, send = pl.pallas_call(
+        functools.partial(back_kernel, group),
+        in_specs=[scalars] * 3 + [vectors] * 3,
+        out_specs=[vectors] * 3,
+        out_shape=[sums, out, out],
+        input_output_aliases={5: 0},
+        compiler_params=pltpu.CompilerParams(vmem_limit_bytes=PRODUCT_VMEM),
+        cost_estimate=cost(0.3),
+    )(split, slot_rows, slot_cols, tiles, parts[-1], front)
+    return keep, send
 
 
 def flip(size, mask):
@@ -276,11 +331,11 @@
     slot_rows = tile_rows.reshape(-1)
     slot_cols = tile_cols.reshape(-1)
 
-    tiles = flip_tiles(live, slot_data)
+    ordered = flip_tiles(live, slot_rows, slot_cols, slot_data, per_dev)
 
     def apply_operator(field):
         parts = gather_parts(field, rows)
-        keep, send = tile_products(parts, live, slot_rows, slot_cols, tiles, block_rows, cols // 2)
+        keep, send = tile_products(parts, ordered, block_rows, cols // 2)
         return reduce_parts(keep, send, cols)
 
     width = channels // CHUNKS

time: 145 us -> 144 us (level)
  waiting for transfers between devices: 92 us -> 80.9 us
  Pallas kernels: 19 us -> 23.2 us
  starting transfers between devices: 31.1 us -> 34.6 us
    ppermute x12, waiting for transfers between devices: 63.2 us -> 54.6 us  [gather_parts(): parts[mask] = lax.ppermute(parts[source], 'row', flip(rows, step))]
    pallas_call x5 -> x9, Pallas kernels: 13.2 us -> 17.4 us  [the longest x4 6.81 us: tile_products(): pl.pallas_call(functools.partial(front_kernel, group), in_specs=[scalars]...]
    ppermute x12, waiting for transfers between devices: 28.8 us -> 26 us  [reduce_parts(): terms.append(lax.ppermute(paired[half], 'col', flip(cols, 2 * half)))]
    ppermute x12, starting transfers between devices: 14.5 us -> 16.6 us  [reduce_parts(): terms.append(lax.ppermute(paired[half], 'col', flip(cols, 2 * half)))]
  transfers between devices with their start and end apart: 28 -> 28, of which waited for: 16 -> 14; matrix products, arithmetic and copies ran while one was open for 1% -> 1% of each run, Pallas kernels for 9% -> 13%
where the time goes in v3:
time: 144 us; the launch traced here: 143 us
  waiting for transfers between devices  80.9 us (56%)
  starting transfers between devices  34.6 us (24%)
  Pallas kernels  23.2 us (16%)
  local copies, waits for them, and re-layouts  2.42 us (2%)
    ppermute x12, waiting for transfers between devices, gather_parts(): parts[mask] = lax.ppermute(parts[source], 'row', flip(rows, step))  54.6 us
    ppermute x12, waiting for transfers between devices, reduce_parts(): terms.append(lax.ppermute(paired[half], 'col', flip(cols, 2 * half)))  26 us
    ppermute x12, starting transfers between devices, gather_parts(): parts[mask] = lax.ppermute(parts[source], 'row', flip(rows, step))  17.7 us
    ppermute x12, starting transfers between devices, reduce_parts(): terms.append(lax.ppermute(paired[half], 'col', flip(cols, 2 * half)))  16.6 us
    pallas_call x4, Pallas kernels, tile_products(): pl.pallas_call(functools.partial(front_kernel, group), in_specs=[scalars]...  6.81 us
    pallas_call x4, Pallas kernels, tile_products(): pl.pallas_call(functools.partial(back_kernel, group), in_specs=[scalars]...  6.6 us
    pallas_call x2, Pallas kernels, write_filtered(): pl.pallas_call(functools.partial(filter_kernel, begin, len(terms)), in_sp...  5.78 us
    pallas_call x1, Pallas kernels, flip_tiles(): pl.pallas_call(functools.partial(flip_kernel, group, depth, per_dev), in_...  4.05 us
  transfers between devices with their start and end apart: 28, of which 14 were waited for; matrix products, arithmetic and copies ran while one was open for 1% of the time, Pallas kernels for 13%

profile of v3, /device:TPU:0, one launch (start us, length us, event | category | flops | bytes accessed | tf_op | source)
XLA Modules:
  0.0 143.4 jit_solution(754752440897721033)
XLA Ops:
  1.1 4.1 %collective-permute-start.14 = (bf16[32,4096]{1,0:T(8,128)(2,1)S(1)}, bf16[32,4096]{1,0:T(8,128)(2,1)S(1)}, u32[]{:S(2)}, u32[]{:S(2)}) collective-permute-start(bf16[32,4096]{1,0:T(8,128)(2,1)S(1)} %get-tuple-element.43.refs_0_.base_ref), channel_id=1, source_target_pairs={{0,16},{8,24},{16,0},{24,8},{1,17},{9,25},{17,1},{25,9},{2,18},{10... | collective-permute-start | bytes 786440 | tf_op jit(solution)/shard_map/ppermute | solution.py:242
  8.8 4.0 %shard_map.55 = (bf16[512,128,128]{2,1,0:T(8,128)(2,1)S(1)}, s32[512]{0:T(512)S(1)}, s32[512]{0:T(512)S(1)}, s32[2]{0:T(128)S(1)}) custom-call(s32[1]{0:T(128)} %bitcast.43.count_ref, s32[512]{0:T(512)S(1)} %bitcast.44, s32[512]{0:T(512)S(1)} %bitcast.45, bf16[512,128,128]{2,1,0:T(8,128)(2,1)} %bitcast.46), custom_call_target="tpu_custom_call" | custom-call | flops 1073741824 | bytes 16777216 | tf_op jit(solution)/shard_map/pallas_call | solution.py:95
  12.8 4.4 %collective-permute-done.14.refs_2_ = bf16[32,4096]{1,0:T(8,128)(2,1)S(1)} collective-permute-done((bf16[32,4096]{1,0:T(8,128)(2,1)S(1)}, bf16[32,4096]{1,0:T(8,128)(2,1)S(1)}, u32[]{:S(2)}, u32[]{:S(2)}) %collective-permute-start.14) | collective-permute-done | bytes 262176 | tf_op jit(solution)/shard_map/ppermute | solution.py:242
  19.6 5.1 %collective-permute-done.15.piece_ref = bf16[32,4096]{1,0:T(8,128)(2,1)S(1)} collective-permute-done((bf16[32,4096]{1,0:T(8,128)(2,1)S(1)}, bf16[32,4096]{1,0:T(8,128)(2,1)S(1)}, u32[]{:S(2)}, u32[]{:S(2)}) %collective-permute-start.15) | collective-permute-done | bytes 262176 | tf_op jit(solution)/shard_map/ppermute | solution.py:242
  26.4 3.1 %collective-permute-start = (bf16[32,4096]{1,0:T(8,128)(2,1)S(1)}, bf16[32,4096]{1,0:T(8,128)(2,1)S(1)}, u32[]{:S(2)}, u32[]{:S(2)}) collective-permute-start(bf16[32,4096]{1,0:T(8,128)(2,1)S(1)} %get-tuple-element.44.refs_0_.base_ref), channel_id=1, source_target_pairs={{0,16},{8,24},{16,0},{24,8},{1,17},{9,25},{17,1},{25,9},{2,18},{10... | collective-permute-start | bytes 786440 | tf_op jit(solution)/shard_map/ppermute | solution.py:242
  29.5 1.8 %collective-permute-start.2 = (bf16[32,4096]{1,0:T(8,128)(2,1)S(1)}, bf16[32,4096]{1,0:T(8,128)(2,1)S(1)}, u32[]{:S(2)}, u32[]{:S(2)}) collective-permute-start(bf16[32,4096]{1,0:T(8,128)(2,1)S(1)} %get-tuple-element.44.refs_0_.base_ref), channel_id=1, source_target_pairs={{0,8},{8,0},{16,24},{24,16},{1,9},{9,1},{17,25},{25,17},{2,10},{10... | collective-permute-start | bytes 786440 | tf_op jit(solution)/shard_map/ppermute | solution.py:242
  31.2 10.9 %collective-permute-done.refs_2_ = bf16[32,4096]{1,0:T(8,128)(2,1)S(1)} collective-permute-done((bf16[32,4096]{1,0:T(8,128)(2,1)S(1)}, bf16[32,4096]{1,0:T(8,128)(2,1)S(1)}, u32[]{:S(2)}, u32[]{:S(2)}) %collective-permute-start) | collective-permute-done | bytes 262176 | tf_op jit(solution)/shard_map/ppermute | solution.py:242
  42.9 3.1 %collective-permute-start.20 = (bf16[32,4096]{1,0:T(8,128)(2,1)S(1)}, bf16[32,4096]{1,0:T(8,128)(2,1)S(1)}, u32[]{:S(2)}, u32[]{:S(2)}) collective-permute-start(bf16[32,4096]{1,0:T(8,128)(2,1)S(1)} %get-tuple-element.34), channel_id=1, source_target_pairs={{0,6},{1,7},{2,4},{3,5},{4,2},{5,3},{6,0},{7,1},{8,14},{9,15},{10,... | collective-permute-start | bytes 786440 | tf_op jit(solution)/shard_map/ppermute | solution.py:254
  48.4 1.7 %collective-permute-done.1.piece_ref = bf16[32,4096]{1,0:T(8,128)(2,1)S(1)} collective-permute-done((bf16[32,4096]{1,0:T(8,128)(2,1)S(1)}, bf16[32,4096]{1,0:T(8,128)(2,1)S(1)}, u32[]{:S(2)}, u32[]{:S(2)}) %collective-permute-start.1) | collective-permute-done | bytes 262176 | tf_op jit(solution)/shard_map/ppermute | solution.py:242
  53.2 4.9 %collective-permute-done.19 = bf16[32,4096]{1,0:T(8,128)(2,1)S(1)} collective-permute-done((bf16[32,4096]{1,0:T(8,128)(2,1)S(1)}, bf16[32,4096]{1,0:T(8,128)(2,1)S(1)}, u32[]{:S(2)}, u32[]{:S(2)}) %collective-permute-start.19) | collective-permute-done | bytes 262176 | tf_op jit(solution)/shard_map/ppermute | solution.py:254
  58.3 2.9 %collective-permute-start.21 = (bf16[32,4096]{1,0:T(8,128)(2,1)S(1)}, bf16[32,4096]{1,0:T(8,128)(2,1)S(1)}, u32[]{:S(2)}, u32[]{:S(2)}) collective-permute-start(bf16[32,4096]{1,0:T(8,128)(2,1)S(1)} %fusion.2.refs_0_.first_ref), channel_id=1, source_target_pairs={{0,16},{8,24},{16,0},{24,8},{1,17},{9,25},{17,1},{25,9},{2,18},{10... | collective-permute-start | bytes 786440 | tf_op jit(solution)/shard_map/ppermute | solution.py:242
  61.7 1.7 %collective-permute-start.6 = (bf16[32,4096]{1,0:T(8,128)(2,1)S(1)}, bf16[32,4096]{1,0:T(8,128)(2,1)S(1)}, u32[]{:S(2)}, u32[]{:S(2)}) collective-permute-start(bf16[32,4096]{1,0:T(8,128)(2,1)S(1)} %get-tuple-element.41), channel_id=1, source_target_pairs={{0,6},{1,7},{2,4},{3,5},{4,2},{5,3},{6,0},{7,1},{8,14},{9,15},{10,... | collective-permute-start | bytes 786440 | tf_op jit(solution)/shard_map/ppermute | solution.py:254
  65.2 8.1 %collective-permute-done.21.refs_2_ = bf16[32,4096]{1,0:T(8,128)(2,1)S(1)} collective-permute-done((bf16[32,4096]{1,0:T(8,128)(2,1)S(1)}, bf16[32,4096]{1,0:T(8,128)(2,1)S(1)}, u32[]{:S(2)}, u32[]{:S(2)}) %collective-permute-start.21) | collective-permute-done | bytes 262176 | tf_op jit(solution)/shard_map/ppermute | solution.py:242
  75.2 5.5 %collective-permute-done.22.piece_ref = bf16[32,4096]{1,0:T(8,128)(2,1)S(1)} collective-permute-done((bf16[32,4096]{1,0:T(8,128)(2,1)S(1)}, bf16[32,4096]{1,0:T(8,128)(2,1)S(1)}, u32[]{:S(2)}, u32[]{:S(2)}) %collective-permute-start.22) | collective-permute-done | bytes 262176 | tf_op jit(solution)/shard_map/ppermute | solution.py:242
  83.6 1.8 %collective-permute-start.9 = (bf16[32,4096]{1,0:T(8,128)(2,1)S(1)}, bf16[32,4096]{1,0:T(8,128)(2,1)S(1)}, u32[]{:S(2)}, u32[]{:S(2)}) collective-permute-start(bf16[32,4096]{1,0:T(8,128)(2,1)S(1)} %fusion.5.refs_0_.first_ref), channel_id=1, source_target_pairs={{0,8},{8,0},{16,24},{24,16},{1,9},{9,1},{17,25},{25,17},{2,10},{10... | collective-permute-start | bytes 786440 | tf_op jit(solution)/shard_map/ppermute | solution.py:242
  85.4 12.3 %collective-permute-done.7.refs_2_ = bf16[32,4096]{1,0:T(8,128)(2,1)S(1)} collective-permute-done((bf16[32,4096]{1,0:T(8,128)(2,1)S(1)}, bf16[32,4096]{1,0:T(8,128)(2,1)S(1)}, u32[]{:S(2)}, u32[]{:S(2)}) %collective-permute-start.7) | collective-permute-done | bytes 262176 | tf_op jit(solution)/shard_map/ppermute | solution.py:242
  97.7 1.7 %shard_map.58.acc_in = f32[264,32,128]{2,1,0:T(8,128)S(1)} custom-call(s32[2]{0:T(128)S(1)} %get-tuple-element.17.split_ref, s32[512]{0:T(512)S(1)} %get-tuple-element.18.rows_ref, s32[512]{0:T(512)S(1)} %get-tuple-element.19.cols_ref, bf16[512,128,128]{2,1,0:T(8,128)(2,1)S(1)} %get-tuple-element.20.tiles_ref, bf16[32,4096]{1,0:T(8,128)(2,1)S(1)} %fusion.5.refs_0_.first_ref, ...), custom_call_target="tpu_custom_call" | custom-call | flops 3006477056 | bytes 11744051 | tf_op jit(solution)/shard_map/pallas_call | solution.py:200
  99.4 6.5 %collective-permute-done.8.piece_ref = bf16[32,4096]{1,0:T(8,128)(2,1)S(1)} collective-permute-done((bf16[32,4096]{1,0:T(8,128)(2,1)S(1)}, bf16[32,4096]{1,0:T(8,128)(2,1)S(1)}, u32[]{:S(2)}, u32[]{:S(2)}) %collective-permute-start.8) | collective-permute-done | bytes 262176 | tf_op jit(solution)/shard_map/ppermute | solution.py:242
  107.9 2.1 %collective-permute-start.25 = (bf16[32,4096]{1,0:T(8,128)(2,1)S(1)}, bf16[32,4096]{1,0:T(8,128)(2,1)S(1)}, u32[]{:S(2)}, u32[]{:S(2)}) collective-permute-start(bf16[32,4096]{1,0:T(8,128)(2,1)S(1)} %get-tuple-element.31), channel_id=1, source_target_pairs={{0,2},{1,3},{2,0},{3,1},{4,6},{5,7},{6,4},{7,5},{8,10},{9,11},{10,... | collective-permute-start | bytes 786440 | tf_op jit(solution)/shard_map/ppermute | solution.py:254
  110.6 2.1 %collective-permute-start.11 = (bf16[32,4096]{1,0:T(8,128)(2,1)S(1)}, bf16[32,4096]{1,0:T(8,128)(2,1)S(1)}, u32[]{:S(2)}, u32[]{:S(2)}) collective-permute-start(bf16[32,4096]{1,0:T(8,128)(2,1)S(1)} %get-tuple-element.38), channel_id=1, source_target_pairs={{0,2},{1,3},{2,0},{3,1},{4,6},{5,7},{6,4},{7,5},{8,10},{9,11},{10,... | collective-permute-start | bytes 786440 | tf_op jit(solution)/shard_map/ppermute | solution.py:254
  114.2 2.0 %collective-permute-start.26 = (bf16[32,4096]{1,0:T(8,128)(2,1)S(1)}, bf16[32,4096]{1,0:T(8,128)(2,1)S(1)}, u32[]{:S(2)}, u32[]{:S(2)}) collective-permute-start(bf16[32,4096]{1,0:T(8,128)(2,1)S(1)} %get-tuple-element.30), channel_id=1, source_target_pairs={{0,4},{1,5},{2,6},{3,7},{4,0},{5,1},{6,2},{7,3},{8,12},{9,13},{10,... | collective-permute-start | bytes 786440 | tf_op jit(solution)/shard_map/ppermute | solution.py:254
  118.9 18.7 %collective-permute-done.26.refs_2_ = bf16[32,4096]{1,0:T(8,128)(2,1)S(1)} collective-permute-done((bf16[32,4096]{1,0:T(8,128)(2,1)S(1)}, bf16[32,4096]{1,0:T(8,128)(2,1)S(1)}, u32[]{:S(2)}, u32[]{:S(2)}) %collective-permute-start.26) | collective-permute-done | bytes 262176 | tf_op jit(solution)/shard_map/ppermute | solution.py:254
  137.5 2.9 %shard_map.64.refs_4_ = bf16[8,64,4096]{2,1,0:T(8,128)(2,1)} custom-call(f32[3,8]{1,0:T(4,128)S(1)} %pad_maximum_fusion.coef_ref, bf16[32,4096]{1,0:T(8,128)(2,1)S(1)} %get-tuple-element.43.refs_0_.base_ref, bf16[32,4096]{1,0:T(8,128)(2,1)S(1)} %fusion.2.refs_0_.first_ref, bf16[32,4096]{1,0:T(8,128)(2,1)S(1)} %get-tuple-element.32.refs_0_, ...), custom_call_target="tpu_custom_call" | custom-call | flops 8388608 | bytes 2097152 | tf_op jit(solution)/shard_map/pallas_call | solution.py:302
  140.5 2.9 %shard_map.65 = bf16[8,64,4096]{2,1,0:T(8,128)(2,1)} custom-call(f32[3,8]{1,0:T(4,128)S(1)} %pad_maximum_fusion.coef_ref, bf16[32,4096]{1,0:T(8,128)(2,1)S(1)} %get-tuple-element.44.refs_0_.base_ref, bf16[32,4096]{1,0:T(8,128)(2,1)S(1)} %fusion.5.refs_0_.first_ref, bf16[32,4096]{1,0:T(8,128)(2,1)S(1)} %get-tuple-element.39.refs_0_, ...), custom_call_target="tpu_custom_call", output_to_operand_aliasing={{}: (7, {})} | custom-call | flops 8388608 | bytes 2097152 | tf_op jit(solution)/shard_map/pallas_call | solution.py:302
  (57 shorter events, 28.3 us)
Async XLA Ops:
  1.1 16.2 %collective-permute-start.14 = (bf16[32,4096]{1,0:T(8,128)(2,1)S(1)}, bf16[32,4096]{1,0:T(8,128)(2,1)S(1)}, u32[]{:S(2)}, u32[]{:S(2)}) collective-permute-start(bf16[32,4096]{1,0:T(8,128)(2,1)S(1)} %get-tuple-element.43.refs_0_.base_ref), channel_id=1, source_target_pairs={{0,16},{8,24},{16,0},{24,8},{1,17},{9,25},{17,1},{25,9},{2,18},{10... | collective-permute-start | bytes 786440 | tf_op jit(solution)/shard_map/ppermute | solution.py:242
  5.2 12.6 %collective-permute-start.16 = (bf16[32,4096]{1,0:T(8,128)(2,1)S(1)}, bf16[32,4096]{1,0:T(8,128)(2,1)S(1)}, u32[]{:S(2)}, u32[]{:S(2)}) collective-permute-start(bf16[32,4096]{1,0:T(8,128)(2,1)S(1)} %get-tuple-element.43.refs_0_.base_ref), channel_id=1, source_target_pairs={{0,8},{8,0},{16,24},{24,16},{1,9},{9,1},{17,25},{25,17},{2,10},{10... | collective-permute-start | bytes 786440 | tf_op jit(solution)/shard_map/ppermute | solution.py:242
  26.3 16.4 %collective-permute-start.17 = (bf16[4,32,4096]{2,1,0:T(8,128)(2,1)S(1)}, bf16[4,32,4096]{2,1,0:T(8,128)(2,1)S(1)}, u32[]{:S(2)}, u32[]{:S(2)}) collective-permute-start(bf16[4,32,4096]{2,1,0:T(8,128)(2,1)S(1)} %get-tuple-element.26), channel_id=1, source_target_pairs={{0,1},{1,0},{2,3},{3,2},{4,5},{5,4},{6,7},{7,6},{8,9},{9,8},{10,11... | collective-permute-start | bytes 3145736 | tf_op jit(solution)/shard_map/ppermute | solution.py:247
  26.4 15.7 %collective-permute-start = (bf16[32,4096]{1,0:T(8,128)(2,1)S(1)}, bf16[32,4096]{1,0:T(8,128)(2,1)S(1)}, u32[]{:S(2)}, u32[]{:S(2)}) collective-permute-start(bf16[32,4096]{1,0:T(8,128)(2,1)S(1)} %get-tuple-element.44.refs_0_.base_ref), channel_id=1, source_target_pairs={{0,16},{8,24},{16,0},{24,8},{1,17},{9,25},{17,1},{25,9},{2,18},{10... | collective-permute-start | bytes 786440 | tf_op jit(solution)/shard_map/ppermute | solution.py:242
  29.5 17.2 %collective-permute-start.2 = (bf16[32,4096]{1,0:T(8,128)(2,1)S(1)}, bf16[32,4096]{1,0:T(8,128)(2,1)S(1)}, u32[]{:S(2)}, u32[]{:S(2)}) collective-permute-start(bf16[32,4096]{1,0:T(8,128)(2,1)S(1)} %get-tuple-element.44.refs_0_.base_ref), channel_id=1, source_target_pairs={{0,8},{8,0},{16,24},{24,16},{1,9},{9,1},{17,25},{25,17},{2,10},{10... | collective-permute-start | bytes 786440 | tf_op jit(solution)/shard_map/ppermute | solution.py:242
  42.9 10.3 %collective-permute-start.20 = (bf16[32,4096]{1,0:T(8,128)(2,1)S(1)}, bf16[32,4096]{1,0:T(8,128)(2,1)S(1)}, u32[]{:S(2)}, u32[]{:S(2)}) collective-permute-start(bf16[32,4096]{1,0:T(8,128)(2,1)S(1)} %get-tuple-element.34), channel_id=1, source_target_pairs={{0,6},{1,7},{2,4},{3,5},{4,2},{5,3},{6,0},{7,1},{8,14},{9,15},{10,... | collective-permute-start | bytes 786440 | tf_op jit(solution)/shard_map/ppermute | solution.py:254
  46.0 12.1 %collective-permute-start.19 = (bf16[32,4096]{1,0:T(8,128)(2,1)S(1)}, bf16[32,4096]{1,0:T(8,128)(2,1)S(1)}, u32[]{:S(2)}, u32[]{:S(2)}) collective-permute-start(bf16[32,4096]{1,0:T(8,128)(2,1)S(1)} %get-tuple-element.35), channel_id=1, source_target_pairs={{0,4},{1,5},{2,6},{3,7},{4,0},{5,1},{6,2},{7,3},{8,12},{9,13},{10,... | collective-permute-start | bytes 786440 | tf_op jit(solution)/shard_map/ppermute | solution.py:254
  46.0 12.1 %collective-permute-start.18 = (bf16[32,4096]{1,0:T(8,128)(2,1)S(1)}, bf16[32,4096]{1,0:T(8,128)(2,1)S(1)}, u32[]{:S(2)}, u32[]{:S(2)}) collective-permute-start(bf16[32,4096]{1,0:T(8,128)(2,1)S(1)} %get-tuple-element.33), channel_id=1, source_target_pairs={{0,2},{1,3},{2,0},{3,1},{4,6},{5,7},{6,4},{7,5},{8,10},{9,11},{10,... | collective-permute-start | bytes 786440 | tf_op jit(solution)/shard_map/ppermute | solution.py:254
  51.7 9.7 %collective-permute-start.3 = (bf16[4,32,4096]{2,1,0:T(8,128)(2,1)S(1)}, bf16[4,32,4096]{2,1,0:T(8,128)(2,1)S(1)}, u32[]{:S(2)}, u32[]{:S(2)}) collective-permute-start(bf16[4,32,4096]{2,1,0:T(8,128)(2,1)S(1)} %get-tuple-element.22), channel_id=1, source_target_pairs={{0,1},{1,0},{2,3},{3,2},{4,5},{5,4},{6,7},{7,6},{8,9},{9,8},{10,11... | collective-permute-start | bytes 3145736 | tf_op jit(solution)/shard_map/ppermute | solution.py:247
  58.3 15.0 %collective-permute-start.21 = (bf16[32,4096]{1,0:T(8,128)(2,1)S(1)}, bf16[32,4096]{1,0:T(8,128)(2,1)S(1)}, u32[]{:S(2)}, u32[]{:S(2)}) collective-permute-start(bf16[32,4096]{1,0:T(8,128)(2,1)S(1)} %fusion.2.refs_0_.first_ref), channel_id=1, source_target_pairs={{0,16},{8,24},{16,0},{24,8},{1,17},{9,25},{17,1},{25,9},{2,18},{10... | collective-permute-start | bytes 786440 | tf_op jit(solution)/shard_map/ppermute | solution.py:242
  61.2 12.3 %collective-permute-start.23 = (bf16[32,4096]{1,0:T(8,128)(2,1)S(1)}, bf16[32,4096]{1,0:T(8,128)(2,1)S(1)}, u32[]{:S(2)}, u32[]{:S(2)}) collective-permute-start(bf16[32,4096]{1,0:T(8,128)(2,1)S(1)} %fusion.2.refs_0_.first_ref), channel_id=1, source_target_pairs={{0,8},{8,0},{16,24},{24,16},{1,9},{9,1},{17,25},{25,17},{2,10},{10... | collective-permute-start | bytes 786440 | tf_op jit(solution)/shard_map/ppermute | solution.py:242
  61.7 20.8 %collective-permute-start.6 = (bf16[32,4096]{1,0:T(8,128)(2,1)S(1)}, bf16[32,4096]{1,0:T(8,128)(2,1)S(1)}, u32[]{:S(2)}, u32[]{:S(2)}) collective-permute-start(bf16[32,4096]{1,0:T(8,128)(2,1)S(1)} %get-tuple-element.41), channel_id=1, source_target_pairs={{0,6},{1,7},{2,4},{3,5},{4,2},{5,3},{6,0},{7,1},{8,14},{9,15},{10,... | collective-permute-start | bytes 786440 | tf_op jit(solution)/shard_map/ppermute | solution.py:254
  63.4 19.0 %collective-permute-start.5 = (bf16[32,4096]{1,0:T(8,128)(2,1)S(1)}, bf16[32,4096]{1,0:T(8,128)(2,1)S(1)}, u32[]{:S(2)}, u32[]{:S(2)}) collective-permute-start(bf16[32,4096]{1,0:T(8,128)(2,1)S(1)} %get-tuple-element.42), channel_id=1, source_target_pairs={{0,4},{1,5},{2,6},{3,7},{4,0},{5,1},{6,2},{7,3},{8,12},{9,13},{10,... | collective-permute-start | bytes 786440 | tf_op jit(solution)/shard_map/ppermute | solution.py:254
  64.7 17.8 %collective-permute-start.4 = (bf16[32,4096]{1,0:T(8,128)(2,1)S(1)}, bf16[32,4096]{1,0:T(8,128)(2,1)S(1)}, u32[]{:S(2)}, u32[]{:S(2)}) collective-permute-start(bf16[32,4096]{1,0:T(8,128)(2,1)S(1)} %get-tuple-element.40), channel_id=1, source_target_pairs={{0,2},{1,3},{2,0},{3,1},{4,6},{5,7},{6,4},{7,5},{8,10},{9,11},{10,... | collective-permute-start | bytes 786440 | tf_op jit(solution)/shard_map/ppermute | solution.py:254
  82.4 25.3 %collective-permute-start.24 = (bf16[4,32,4096]{2,1,0:T(8,128)(2,1)S(1)}, bf16[4,32,4096]{2,1,0:T(8,128)(2,1)S(1)}, u32[]{:S(2)}, u32[]{:S(2)}) collective-permute-start(bf16[4,32,4096]{2,1,0:T(8,128)(2,1)S(1)} %get-tuple-element.28), channel_id=1, source_target_pairs={{0,1},{1,0},{2,3},{3,2},{4,5},{5,4},{6,7},{7,6},{8,9},{9,8},{10,11... | collective-permute-start | bytes 3145736 | tf_op jit(solution)/shard_map/ppermute | solution.py:247
  82.6 15.0 %collective-permute-start.7 = (bf16[32,4096]{1,0:T(8,128)(2,1)S(1)}, bf16[32,4096]{1,0:T(8,128)(2,1)S(1)}, u32[]{:S(2)}, u32[]{:S(2)}) collective-permute-start(bf16[32,4096]{1,0:T(8,128)(2,1)S(1)} %fusion.5.refs_0_.first_ref), channel_id=1, source_target_pairs={{0,16},{8,24},{16,0},{24,8},{1,17},{9,25},{17,1},{25,9},{2,18},{10... | collective-permute-start | bytes 786440 | tf_op jit(solution)/shard_map/ppermute | solution.py:242
  83.6 14.1 %collective-permute-start.9 = (bf16[32,4096]{1,0:T(8,128)(2,1)S(1)}, bf16[32,4096]{1,0:T(8,128)(2,1)S(1)}, u32[]{:S(2)}, u32[]{:S(2)}) collective-permute-start(bf16[32,4096]{1,0:T(8,128)(2,1)S(1)} %fusion.5.refs_0_.first_ref), channel_id=1, source_target_pairs={{0,8},{8,0},{16,24},{24,16},{1,9},{9,1},{17,25},{25,17},{2,10},{10... | collective-permute-start | bytes 786440 | tf_op jit(solution)/shard_map/ppermute | solution.py:242
  97.7 8.2 %collective-permute-start.8 = (bf16[32,4096]{1,0:T(8,128)(2,1)S(1)}, bf16[32,4096]{1,0:T(8,128)(2,1)S(1)}, u32[]{:S(2)}, u32[]{:S(2)}) collective-permute-start(bf16[32,4096]{1,0:T(8,128)(2,1)S(1)} %collective-permute-done.7.refs_2_), channel_id=1, source_target_pairs={{0,8},{8,0},{16,24},{24,16},{1,9},{9,1},{17,25},{25,17},{2,10},{10... | collective-permute-start | bytes 786440 | tf_op jit(solution)/shard_map/ppermute | solution.py:242
  107.9 9.2 %collective-permute-start.25 = (bf16[32,4096]{1,0:T(8,128)(2,1)S(1)}, bf16[32,4096]{1,0:T(8,128)(2,1)S(1)}, u32[]{:S(2)}, u32[]{:S(2)}) collective-permute-start(bf16[32,4096]{1,0:T(8,128)(2,1)S(1)} %get-tuple-element.31), channel_id=1, source_target_pairs={{0,2},{1,3},{2,0},{3,1},{4,6},{5,7},{6,4},{7,5},{8,10},{9,11},{10,... | collective-permute-start | bytes 786440 | tf_op jit(solution)/shard_map/ppermute | solution.py:254
  110.6 29.9 %collective-permute-start.11 = (bf16[32,4096]{1,0:T(8,128)(2,1)S(1)}, bf16[32,4096]{1,0:T(8,128)(2,1)S(1)}, u32[]{:S(2)}, u32[]{:S(2)}) collective-permute-start(bf16[32,4096]{1,0:T(8,128)(2,1)S(1)} %get-tuple-element.38), channel_id=1, source_target_pairs={{0,2},{1,3},{2,0},{3,1},{4,6},{5,7},{6,4},{7,5},{8,10},{9,11},{10,... | collective-permute-start | bytes 786440 | tf_op jit(solution)/shard_map/ppermute | solution.py:254
  112.6 27.8 %collective-permute-start.12 = (bf16[32,4096]{1,0:T(8,128)(2,1)S(1)}, bf16[32,4096]{1,0:T(8,128)(2,1)S(1)}, u32[]{:S(2)}, u32[]{:S(2)}) collective-permute-start(bf16[32,4096]{1,0:T(8,128)(2,1)S(1)} %get-tuple-element.37), channel_id=1, source_target_pairs={{0,4},{1,5},{2,6},{3,7},{4,0},{5,1},{6,2},{7,3},{8,12},{9,13},{10,... | collective-permute-start | bytes 786440 | tf_op jit(solution)/shard_map/ppermute | solution.py:254
  112.8 27.6 %collective-permute-start.13 = (bf16[32,4096]{1,0:T(8,128)(2,1)S(1)}, bf16[32,4096]{1,0:T(8,128)(2,1)S(1)}, u32[]{:S(2)}, u32[]{:S(2)}) collective-permute-start(bf16[32,4096]{1,0:T(8,128)(2,1)S(1)} %get-tuple-element.36), channel_id=1, source_target_pairs={{0,6},{1,7},{2,4},{3,5},{4,2},{5,3},{6,0},{7,1},{8,14},{9,15},{10,... | collective-permute-start | bytes 786440 | tf_op jit(solution)/shard_map/ppermute | solution.py:254
  114.2 23.3 %collective-permute-start.26 = (bf16[32,4096]{1,0:T(8,128)(2,1)S(1)}, bf16[32,4096]{1,0:T(8,128)(2,1)S(1)}, u32[]{:S(2)}, u32[]{:S(2)}) collective-permute-start(bf16[32,4096]{1,0:T(8,128)(2,1)S(1)} %get-tuple-element.30), channel_id=1, source_target_pairs={{0,4},{1,5},{2,6},{3,7},{4,0},{5,1},{6,2},{7,3},{8,12},{9,13},{10,... | collective-permute-start | bytes 786440 | tf_op jit(solution)/shard_map/ppermute | solution.py:254
  117.2 20.4 %collective-permute-start.27 = (bf16[32,4096]{1,0:T(8,128)(2,1)S(1)}, bf16[32,4096]{1,0:T(8,128)(2,1)S(1)}, u32[]{:S(2)}, u32[]{:S(2)}) collective-permute-start(bf16[32,4096]{1,0:T(8,128)(2,1)S(1)} %get-tuple-element.29), channel_id=1, source_target_pairs={{0,6},{1,7},{2,4},{3,5},{4,2},{5,3},{6,0},{7,1},{8,14},{9,15},{10,... | collective-permute-start | bytes 786440 | tf_op jit(solution)/shard_map/ppermute | solution.py:254
  (6 other events, 26.9 us)

commit v4 on v3

--- a/solution.py
+++ b/solution.py
@@ -12,11 +12,14 @@
 TILE_SIZE = 128
 CHUNKS = 2
 GROUP = 64
+COL_BITS = 16
+COL_MASK = 2**COL_BITS - 1
 FLIP_GROUP = 32
 FLIP_DEPTH = 8
 FLIP_VMEM = 28 * 2**20
 PRODUCT_VMEM = 16 * 2**20
 FILTER_VMEM = 16 * 2**20
+PLAIN_VMEM = 8 * 2**20
 
 
 def bessel_pair(times):
@@ -41,12 +44,9 @@
     return (bessel_zero, -2.0 * bessel_one, 2.0 * (bessel_zero - 2.0 * bessel_one / times))
 
 
-def flip_kernel(group, depth, per_dev, count_ref, rows_ref, cols_ref, tiles_hbm, *refs):
-    flipped_ref, order_rows_ref, order_cols_ref, split_ref, tiles_ref, sems = refs
+def flip_kernel(group, depth, edge, codes_ref, tiles_hbm, flipped_ref, order_ref, tiles_ref, sems):
     slots = flipped_ref.shape[0]
-    count = count_ref[0]
-    row_at = lax.axis_index("row")
-    last = lax.axis_size("row") - 1
+    count = codes_ref[slots]
     live_groups = lax.div(count + (group - 1), group)
 
     def load(index):
@@ -65,15 +65,14 @@
         load(index).wait()
         for g in range(group):
             slot = index * group + g
-            col = cols_ref[slot]
-            source = lax.div(col, per_dev) ^ row_at
-            to_back = (source == last) & (slot < count)
-            place = jnp.where(to_back, slots - 1 - back, front)
+            code = codes_ref[slot]
+            late = (code & COL_MASK) >= edge
+            to_back = (late & (slot < count)).astype(jnp.int32)
+            place = jnp.where(to_back == 1, slots - 1 - back, front)
             flipped_ref[place] = tiles_ref[lax.rem(index, depth), g].T
-            order_rows_ref[place] = rows_ref[slot]
-            order_cols_ref[place] = source * per_dev + (col & (per_dev - 1))
-            back = back + to_back.astype(jnp.int32)
-            front = front + ((source != last) & (slot < count)).astype(jnp.int32)
+            order_ref[place] = code
+            back = back + to_back
+            front = front + (1 - to_back)
 
         @pl.when(index + depth < live_groups)
         def _():
@@ -81,30 +80,27 @@
 
         return front, back
 
-    front, back = lax.fori_loop(0, live_groups, one_group, (jnp.int32(0), jnp.int32(0)))
-    split_ref[0] = front
-    split_ref[1] = back
-
-
-def flip_tiles(live, slot_rows, slot_cols, slot_data, per_dev):
+    _, back = lax.fori_loop(0, live_groups, one_group, (jnp.int32(0), jnp.int32(0)))
+    order_ref[slots] = count - back
+    order_ref[slots + 1] = back
+
+
+def flip_tiles(codes, slot_data, edge):
     slots = slot_data.shape[0]
     group = min(FLIP_GROUP, slots)
     depth = min(FLIP_DEPTH, slots // group)
     scalars = pl.BlockSpec(memory_space=pltpu.SMEM)
-    numbers = jax.ShapeDtypeStruct((slots,), jnp.int32)
     return pl.pallas_call(
-        functools.partial(flip_kernel, group, depth, per_dev),
-        in_specs=[scalars] * 3 + [pl.BlockSpec(memory_space=pl.ANY)],
-        out_specs=[pl.BlockSpec(memory_space=pltpu.VMEM)] + [scalars] * 3,
+        functools.partial(flip_kernel, group, depth, edge),
+        in_specs=[scalars, pl.BlockSpec(memory_space=pl.ANY)],
+        out_specs=[pl.BlockSpec(memory_space=pltpu.VMEM), scalars],
         scratch_shapes=[
             pltpu.VMEM((depth, group, TILE_SIZE, TILE_SIZE), jnp.bfloat16),
             pltpu.SemaphoreType.DMA((depth,)),
         ],
         out_shape=[
             jax.ShapeDtypeStruct(slot_data.shape, jnp.bfloat16),
-            numbers,
-            numbers,
-            jax.ShapeDtypeStruct((2,), jnp.int32),
+            jax.ShapeDtypeStruct((slots + 2,), jnp.int32),
         ],
         compiler_params=pltpu.CompilerParams(vmem_limit_bytes=FLIP_VMEM),
         cost_estimate=pl.CostEstimate(
@@ -112,15 +108,15 @@
             bytes_accessed=slots * TILE_SIZE * TILE_SIZE * 2,
             transcendentals=0,
         ),
-    )(live, slot_rows, slot_cols, slot_data)
-
-
-def front_kernel(group, split_ref, rows_ref, cols_ref, tiles_ref, *refs):
+    )(codes, slot_data)
+
+
+def front_kernel(group, order_ref, tiles_ref, *refs):
     acc_ref, panel_ref, sems = refs[-3:]
     piece_refs = refs[:-3]
     per_dev = panel_ref.shape[2] // TILE_SIZE
     trash = acc_ref.shape[0] - 1
-    front = split_ref[0]
+    front = order_ref[tiles_ref.shape[0]]
     copies = [
         pltpu.make_async_copy(ref, panel_ref.at[i], sems.at[i]) for i, ref in enumerate(piece_refs)
     ]
@@ -139,20 +135,21 @@
         for g in range(group):
             slot = index * group + g
             valid = slot < front
-            col = jnp.where(valid, cols_ref[slot], 0)
-            row = jnp.where(valid, rows_ref[slot], trash)
+            code = jnp.where(valid, order_ref[slot], trash * (COL_MASK + 1))
+            col = code & COL_MASK
+            row = lax.shift_right_logical(code, COL_BITS)
             offset = pl.multiple_of((col & (per_dev - 1)) * TILE_SIZE, TILE_SIZE)
             picked = panel_ref[lax.div(col, per_dev), :, pl.ds(offset, TILE_SIZE)]
             acc_ref[row] += jnp.dot(picked, tiles_ref[slot], preferred_element_type=jnp.float32)
 
 
-def back_kernel(group, split_ref, rows_ref, cols_ref, tiles_ref, piece_ref, acc_in, *refs):
+def back_kernel(group, order_ref, tiles_ref, piece_ref, acc_in, *refs):
     acc_ref, keep_ref, send_ref = refs
     halves = keep_ref.shape[0]
     slots = tiles_ref.shape[0]
     per_dev = piece_ref.shape[1] // TILE_SIZE
     trash = acc_ref.shape[0] - 1
-    back = split_ref[1]
+    back = order_ref[slots + 1]
     col_at = lax.axis_index("col")
     pair = lax.div(col_at, 2)
     core = col_at & 1
@@ -162,8 +159,9 @@
         for g in range(group):
             slot = slots - group * (index + 1) + g
             valid = slot >= slots - back
-            col = jnp.where(valid, cols_ref[slot], 0)
-            row = jnp.where(valid, rows_ref[slot], trash)
+            code = jnp.where(valid, order_ref[slot], trash * (COL_MASK + 1))
+            col = code & COL_MASK
+            row = lax.shift_right_logical(code, COL_BITS)
             offset = pl.multiple_of((col & (per_dev - 1)) * TILE_SIZE, TILE_SIZE)
             picked = piece_ref[:, pl.ds(offset, TILE_SIZE)]
             acc_ref[row] += jnp.dot(picked, tiles_ref[slot], preferred_element_type=jnp.float32)
@@ -180,7 +178,7 @@
 
 
 def tile_products(parts, ordered, block_rows, halves):
-    tiles, slot_rows, slot_cols, split = ordered
+    tiles, order = ordered
     channels, nodes = parts[0].shape
     slots = tiles.shape[0]
     group = min(GROUP, slots)
@@ -199,7 +197,7 @@
 
     front = pl.pallas_call(
         functools.partial(front_kernel, group),
-        in_specs=[scalars] * 3 + [vectors] + [pl.BlockSpec(memory_space=pl.ANY)] * pieces,
+        in_specs=[scalars, vectors] + [pl.BlockSpec(memory_space=pl.ANY)] * pieces,
         out_specs=vectors,
         scratch_shapes=[
             pltpu.VMEM((pieces, channels, nodes), jnp.bfloat16),
@@ -208,16 +206,16 @@
         out_shape=sums,
         compiler_params=pltpu.CompilerParams(vmem_limit_bytes=PRODUCT_VMEM),
         cost_estimate=cost(0.7),
-    )(split, slot_rows, slot_cols, tiles, *parts[:-1])
+    )(order, tiles, *parts[:-1])
     _, keep, send = pl.pallas_call(
         functools.partial(back_kernel, group),
-        in_specs=[scalars] * 3 + [vectors] * 3,
+        in_specs=[scalars] + [vectors] * 3,
         out_specs=[vectors] * 3,
         out_shape=[sums, out, out],
-        input_output_aliases={5: 0},
+        input_output_aliases={3: 0},
         compiler_params=pltpu.CompilerParams(vmem_limit_bytes=PRODUCT_VMEM),
         cost_estimate=cost(0.3),
-    )(split, slot_rows, slot_cols, tiles, parts[-1], front)
+    )(order, tiles, parts[-1], front)
     return keep, send
 
 
@@ -262,9 +260,9 @@
     return total.astype(jnp.bfloat16)
 
 
-def filter_kernel(begin, count, coef_ref, base_ref, first_ref, *refs):
+def filter_kernel(begin, count, coef_ref, plain_ref, *refs):
     out_hbm, stage_ref, sems = refs[-3:]
-    width, nodes = base_ref.shape
+    width, nodes = refs[0].shape
     strip = min(nodes, 512)
 
     def save(scale):
@@ -277,15 +275,11 @@
         @pl.loop(0, nodes // strip)
         def _(index):
             span = pl.ds(pl.multiple_of(index * strip, strip), strip)
-            base = base_ref[:, span].astype(jnp.float32)
-            first = first_ref[:, span].astype(jnp.float32)
             second = add_terms([ref[:, span] for ref in refs[:count]]).astype(jnp.float32)
-            bend = 2.0 * second - base
+            twice = 2.0 * second
             for scale in scales:
                 stage_ref[scale, :, span] = (
-                    coef_ref[0, scale] * base
-                    + coef_ref[1, scale] * first
-                    + coef_ref[2, scale] * bend
+                    plain_ref[scale, :, span] + coef_ref[2, scale] * twice
                 ).astype(jnp.bfloat16)
 
         for scale in scales:
@@ -294,15 +288,46 @@
         save(scale).wait()
 
 
-def write_filtered(coefs, base, first, terms, begin, channels, filtered):
+def plain_kernel(coef_ref, base_ref, first_ref, plain_ref):
+    strip = min(base_ref.shape[1], 512)
+
+    @pl.loop(0, base_ref.shape[1] // strip)
+    def _(index):
+        span = pl.ds(pl.multiple_of(index * strip, strip), strip)
+        base = base_ref[:, span].astype(jnp.float32)
+        first = first_ref[:, span].astype(jnp.float32)
+        for scale in range(SCALES):
+            plain_ref[scale, :, span] = (
+                coef_ref[0, scale] - coef_ref[2, scale]
+            ) * base + coef_ref[1, scale] * first
+
+
+def plain_part(coefs, base, first):
     width, nodes = base.shape
+    vectors = pl.BlockSpec(memory_space=pltpu.VMEM)
+    return pl.pallas_call(
+        plain_kernel,
+        in_specs=[pl.BlockSpec(memory_space=pltpu.SMEM)] + [vectors] * 2,
+        out_specs=vectors,
+        out_shape=jax.ShapeDtypeStruct((SCALES, width, nodes), jnp.float32),
+        compiler_params=pltpu.CompilerParams(vmem_limit_bytes=PLAIN_VMEM),
+        cost_estimate=pl.CostEstimate(
+            flops=4 * SCALES * width * nodes,
+            bytes_accessed=4 * SCALES * width * nodes,
+            transcendentals=0,
+        ),
+    )(coefs, base, first)
+
+
+def write_filtered(coefs, plain, terms, begin, channels, filtered):
+    width, nodes = terms[0].shape
     vectors = pl.BlockSpec(memory_space=pltpu.VMEM)
     anywhere = pl.BlockSpec(memory_space=pl.ANY)
     rest = [] if filtered is None else [filtered]
     return pl.pallas_call(
         functools.partial(filter_kernel, begin, len(terms)),
         in_specs=[pl.BlockSpec(memory_space=pltpu.SMEM)]
-        + [vectors] * (2 + len(terms))
+        + [vectors] * (1 + len(terms))
         + [anywhere] * len(rest),
         out_specs=anywhere,
         scratch_shapes=[
@@ -310,14 +335,14 @@
             pltpu.SemaphoreType.DMA((SCALES,)),
         ],
         out_shape=jax.ShapeDtypeStruct((SCALES, channels, nodes), jnp.bfloat16),
-        input_output_aliases={3 + len(terms): 0} if rest else {},
+        input_output_aliases={2 + len(terms): 0} if rest else {},
         compiler_params=pltpu.CompilerParams(vmem_limit_bytes=FILTER_VMEM),
         cost_estimate=pl.CostEstimate(
             flops=8 * SCALES * width * nodes,
             bytes_accessed=2 * SCALES * width * nodes,
             transcendentals=0,
         ),
-    )(coefs, base, first, *terms, *rest)
+    )(coefs, plain, *terms, *rest)
 
 
 def filter_bank(features, tile_rows, tile_cols, tile_count, tile_data):
@@ -327,11 +352,12 @@
     per_dev = nodes // TILE_SIZE
     block_rows = per_dev * cols
     slot_data = tile_data.reshape(-1, TILE_SIZE, TILE_SIZE)
-    live = tile_count.reshape(-1)
-    slot_rows = tile_rows.reshape(-1)
     slot_cols = tile_cols.reshape(-1)
-
-    ordered = flip_tiles(live, slot_rows, slot_cols, slot_data, per_dev)
+    source = (slot_cols // per_dev) ^ lax.axis_index("row")
+    codes = tile_rows.reshape(-1) * (COL_MASK + 1) + source * per_dev + slot_cols % per_dev
+    codes = jnp.concatenate([codes, tile_count.reshape(-1)])
+
+    ordered = flip_tiles(codes, slot_data, (rows - 1) * per_dev)
 
     def apply_operator(field):
         parts = gather_parts(field, rows)
@@ -348,7 +374,8 @@
     seconds = [apply_operator(first) for first in firsts]
     filtered = None
     for chunk, (field, first, terms) in enumerate(zip(fields, firsts, seconds)):
-        filtered = write_filtered(coefs, field, first, terms, chunk * width, channels, filtered)
+        plain = plain_part(coefs, field, first)
+        filtered = write_filtered(coefs, plain, terms, chunk * width, channels, filtered)
     return filtered.reshape(-1, nodes)
 
 

time: 144 us -> 136 us (0.944)
  starting transfers between devices: 34.6 us -> 28.6 us
  waiting for transfers between devices: 80.9 us -> 78.5 us
    ppermute x12, starting transfers between devices: 17.7 us -> 13 us  [gather_parts(): parts[mask] = lax.ppermute(parts[source], 'row', flip(rows, step))]
    ppermute x12, waiting for transfers between devices: 26 us -> 21.5 us  [reduce_parts(): terms.append(lax.ppermute(paired[half], 'col', flip(cols, 2 * half)))]
    ppermute x12, waiting for transfers between devices: 54.6 us -> 57 us  [gather_parts(): parts[mask] = lax.ppermute(parts[source], 'row', flip(rows, step))]
    pallas_call x5 -> x7, Pallas kernels: 10.9 us -> 12.5 us  [the longest x4 6.65 us: tile_products(): pl.pallas_call(functools.partial(front_kernel, group), in_specs=[scalars,...]
  transfers between devices with their start and end apart: 28 -> 28, of which waited for: 14 -> 17; matrix products, arithmetic and copies ran while one was open for 1% -> 2% of each run, Pallas kernels for 13% -> 15%
where the time goes in v4:
time: 136 us
  waiting for transfers between devices  78.5 us (58%)
  starting transfers between devices  28.6 us (21%)
  Pallas kernels  23.8 us (18%)
  other arithmetic  2.73 us (2%)
    ppermute x12, waiting for transfers between devices, gather_parts(): parts[mask] = lax.ppermute(parts[source], 'row', flip(rows, step))  57 us
    ppermute x12, waiting for transfers between devices, reduce_parts(): terms.append(lax.ppermute(paired[half], 'col', flip(cols, 2 * half)))  21.5 us
    ppermute x12, starting transfers between devices, reduce_parts(): terms.append(lax.ppermute(paired[half], 'col', flip(cols, 2 * half)))  15.3 us
    ppermute x12, starting transfers between devices, gather_parts(): parts[mask] = lax.ppermute(parts[source], 'row', flip(rows, step))  13 us
    pallas_call x4, Pallas kernels, tile_products(): pl.pallas_call(functools.partial(front_kernel, group), in_specs=[scalars,...  6.65 us
    pallas_call x4, Pallas kernels, tile_products(): pl.pallas_call(functools.partial(back_kernel, group), in_specs=[scalars]...  6.51 us
    pallas_call x2, Pallas kernels, write_filtered(): pl.pallas_call(functools.partial(filter_kernel, begin, len(terms)), in_sp...  4.71 us
    pallas_call x1, Pallas kernels, flip_tiles(): pl.pallas_call(functools.partial(flip_kernel, group, depth, edge), in_spe...  3.74 us
  transfers between devices with their start and end apart: 28, of which 17 were waited for; matrix products, arithmetic and copies ran while one was open for 2% of the time, Pallas kernels for 15%

profile of v4, /device:TPU:0, one launch (start us, length us, event | category | flops | bytes accessed | tf_op | source)
XLA Modules:
  0.0 135.6 jit_solution(5986370808298689694)
XLA Ops:
  1.1 3.1 %collective-permute-start.16 = (bf16[32,4096]{1,0:T(8,128)(2,1)S(1)}, bf16[32,4096]{1,0:T(8,128)(2,1)S(1)}, u32[]{:S(2)}, u32[]{:S(2)}) collective-permute-start(bf16[32,4096]{1,0:T(8,128)(2,1)S(1)} %get-tuple-element.39.refs_0_.base_ref), channel_id=1, source_target_pairs={{0,8},{8,0},{16,24},{24,16},{1,9},{9,1},{17,25},{25,17},{2,10},{10... | collective-permute-start | bytes 786440 | tf_op jit(solution)/shard_map/ppermute | solution.py:240
  4.2 2.6 %collective-permute-start.14 = (bf16[32,4096]{1,0:T(8,128)(2,1)S(1)}, bf16[32,4096]{1,0:T(8,128)(2,1)S(1)}, u32[]{:S(2)}, u32[]{:S(2)}) collective-permute-start(bf16[32,4096]{1,0:T(8,128)(2,1)S(1)} %get-tuple-element.39.refs_0_.base_ref), channel_id=1, source_target_pairs={{0,16},{8,24},{16,0},{24,8},{1,17},{9,25},{17,1},{25,9},{2,18},{10... | collective-permute-start | bytes 786440 | tf_op jit(solution)/shard_map/ppermute | solution.py:240
  8.8 3.7 %shard_map.55 = (bf16[512,128,128]{2,1,0:T(8,128)(2,1)S(1)}, s32[514]{0:T(1024)S(1)}) custom-call(s32[513]{0:T(1024)S(1)} %pad_add_fusion.codes_ref, bf16[512,128,128]{2,1,0:T(8,128)(2,1)} %bitcast.44), custom_call_target="tpu_custom_call" | custom-call | flops 1073741824 | bytes 16777216 | tf_op jit(solution)/shard_map/pallas_call | solution.py:93
  12.6 5.9 %collective-permute-done.14.refs_2_ = bf16[32,4096]{1,0:T(8,128)(2,1)S(1)} collective-permute-done((bf16[32,4096]{1,0:T(8,128)(2,1)S(1)}, bf16[32,4096]{1,0:T(8,128)(2,1)S(1)}, u32[]{:S(2)}, u32[]{:S(2)}) %collective-permute-start.14) | collective-permute-done | bytes 262176 | tf_op jit(solution)/shard_map/ppermute | solution.py:240
  20.6 4.2 %collective-permute-done.15.piece_ref = bf16[32,4096]{1,0:T(8,128)(2,1)S(1)} collective-permute-done((bf16[32,4096]{1,0:T(8,128)(2,1)S(1)}, bf16[32,4096]{1,0:T(8,128)(2,1)S(1)}, u32[]{:S(2)}, u32[]{:S(2)}) %collective-permute-start.15) | collective-permute-done | bytes 262176 | tf_op jit(solution)/shard_map/ppermute | solution.py:240
  27.7 2.0 %collective-permute-start.2 = (bf16[32,4096]{1,0:T(8,128)(2,1)S(1)}, bf16[32,4096]{1,0:T(8,128)(2,1)S(1)}, u32[]{:S(2)}, u32[]{:S(2)}) collective-permute-start(bf16[32,4096]{1,0:T(8,128)(2,1)S(1)} %get-tuple-element.40.refs_0_.base_ref), channel_id=1, source_target_pairs={{0,8},{8,0},{16,24},{24,16},{1,9},{9,1},{17,25},{25,17},{2,10},{10... | collective-permute-start | bytes 786440 | tf_op jit(solution)/shard_map/ppermute | solution.py:240
  29.8 12.1 %collective-permute-done.refs_2_ = bf16[32,4096]{1,0:T(8,128)(2,1)S(1)} collective-permute-done((bf16[32,4096]{1,0:T(8,128)(2,1)S(1)}, bf16[32,4096]{1,0:T(8,128)(2,1)S(1)}, u32[]{:S(2)}, u32[]{:S(2)}) %collective-permute-start) | collective-permute-done | bytes 262176 | tf_op jit(solution)/shard_map/ppermute | solution.py:240
  43.5 1.8 %collective-permute-start.20 = (bf16[32,4096]{1,0:T(8,128)(2,1)S(1)}, bf16[32,4096]{1,0:T(8,128)(2,1)S(1)}, u32[]{:S(2)}, u32[]{:S(2)}) collective-permute-start(bf16[32,4096]{1,0:T(8,128)(2,1)S(1)} %get-tuple-element.30), channel_id=1, source_target_pairs={{0,6},{1,7},{2,4},{3,5},{4,2},{5,3},{6,0},{7,1},{8,14},{9,15},{10,... | collective-permute-start | bytes 786440 | tf_op jit(solution)/shard_map/ppermute | solution.py:252
  47.4 2.2 %collective-permute-done.1.piece_ref = bf16[32,4096]{1,0:T(8,128)(2,1)S(1)} collective-permute-done((bf16[32,4096]{1,0:T(8,128)(2,1)S(1)}, bf16[32,4096]{1,0:T(8,128)(2,1)S(1)}, u32[]{:S(2)}, u32[]{:S(2)}) %collective-permute-start.1) | collective-permute-done | bytes 262176 | tf_op jit(solution)/shard_map/ppermute | solution.py:240
  51.3 5.9 %collective-permute-done.20 = bf16[32,4096]{1,0:T(8,128)(2,1)S(1)} collective-permute-done((bf16[32,4096]{1,0:T(8,128)(2,1)S(1)}, bf16[32,4096]{1,0:T(8,128)(2,1)S(1)}, u32[]{:S(2)}, u32[]{:S(2)}) %collective-permute-start.20) | collective-permute-done | bytes 262176 | tf_op jit(solution)/shard_map/ppermute | solution.py:252
  58.9 1.8 %collective-permute-start.23 = (bf16[32,4096]{1,0:T(8,128)(2,1)S(1)}, bf16[32,4096]{1,0:T(8,128)(2,1)S(1)}, u32[]{:S(2)}, u32[]{:S(2)}) collective-permute-start(bf16[32,4096]{1,0:T(8,128)(2,1)S(1)} %fusion.2.first_ref.refs_0_), channel_id=1, source_target_pairs={{0,8},{8,0},{16,24},{24,16},{1,9},{9,1},{17,25},{25,17},{2,10},{10... | collective-permute-start | bytes 786440 | tf_op jit(solution)/shard_map/ppermute | solution.py:240
  61.4 1.7 %collective-permute-start.4 = (bf16[32,4096]{1,0:T(8,128)(2,1)S(1)}, bf16[32,4096]{1,0:T(8,128)(2,1)S(1)}, u32[]{:S(2)}, u32[]{:S(2)}) collective-permute-start(bf16[32,4096]{1,0:T(8,128)(2,1)S(1)} %get-tuple-element.36), channel_id=1, source_target_pairs={{0,2},{1,3},{2,0},{3,1},{4,6},{5,7},{6,4},{7,5},{8,10},{9,11},{10,... | collective-permute-start | bytes 786440 | tf_op jit(solution)/shard_map/ppermute | solution.py:252
  65.0 7.9 %collective-permute-done.21.refs_2_ = bf16[32,4096]{1,0:T(8,128)(2,1)S(1)} collective-permute-done((bf16[32,4096]{1,0:T(8,128)(2,1)S(1)}, bf16[32,4096]{1,0:T(8,128)(2,1)S(1)}, u32[]{:S(2)}, u32[]{:S(2)}) %collective-permute-start.21) | collective-permute-done | bytes 262176 | tf_op jit(solution)/shard_map/ppermute | solution.py:240
  74.5 4.7 %collective-permute-done.22.piece_ref = bf16[32,4096]{1,0:T(8,128)(2,1)S(1)} collective-permute-done((bf16[32,4096]{1,0:T(8,128)(2,1)S(1)}, bf16[32,4096]{1,0:T(8,128)(2,1)S(1)}, u32[]{:S(2)}, u32[]{:S(2)}) %collective-permute-start.22) | collective-permute-done | bytes 262176 | tf_op jit(solution)/shard_map/ppermute | solution.py:240
  82.5 13.4 %collective-permute-done.7.refs_2_ = bf16[32,4096]{1,0:T(8,128)(2,1)S(1)} collective-permute-done((bf16[32,4096]{1,0:T(8,128)(2,1)S(1)}, bf16[32,4096]{1,0:T(8,128)(2,1)S(1)}, u32[]{:S(2)}, u32[]{:S(2)}) %collective-permute-start.7) | collective-permute-done | bytes 262176 | tf_op jit(solution)/shard_map/ppermute | solution.py:240
  98.1 6.0 %collective-permute-done.8.piece_ref = bf16[32,4096]{1,0:T(8,128)(2,1)S(1)} collective-permute-done((bf16[32,4096]{1,0:T(8,128)(2,1)S(1)}, bf16[32,4096]{1,0:T(8,128)(2,1)S(1)}, u32[]{:S(2)}, u32[]{:S(2)}) %collective-permute-start.8) | collective-permute-done | bytes 262176 | tf_op jit(solution)/shard_map/ppermute | solution.py:240
  106.1 2.3 %collective-permute-start.27 = (bf16[32,4096]{1,0:T(8,128)(2,1)S(1)}, bf16[32,4096]{1,0:T(8,128)(2,1)S(1)}, u32[]{:S(2)}, u32[]{:S(2)}) collective-permute-start(bf16[32,4096]{1,0:T(8,128)(2,1)S(1)} %get-tuple-element.25), channel_id=1, source_target_pairs={{0,6},{1,7},{2,4},{3,5},{4,2},{5,3},{6,0},{7,1},{8,14},{9,15},{10,... | collective-permute-start | bytes 786440 | tf_op jit(solution)/shard_map/ppermute | solution.py:252
  109.9 2.3 %collective-permute-start.13 = (bf16[32,4096]{1,0:T(8,128)(2,1)S(1)}, bf16[32,4096]{1,0:T(8,128)(2,1)S(1)}, u32[]{:S(2)}, u32[]{:S(2)}) collective-permute-start(bf16[32,4096]{1,0:T(8,128)(2,1)S(1)} %get-tuple-element.32), channel_id=1, source_target_pairs={{0,6},{1,7},{2,4},{3,5},{4,2},{5,3},{6,0},{7,1},{8,14},{9,15},{10,... | collective-permute-start | bytes 786440 | tf_op jit(solution)/shard_map/ppermute | solution.py:252
  112.9 3.4 %collective-permute-done.27.refs_3_ = bf16[32,4096]{1,0:T(8,128)(2,1)S(1)} collective-permute-done((bf16[32,4096]{1,0:T(8,128)(2,1)S(1)}, bf16[32,4096]{1,0:T(8,128)(2,1)S(1)}, u32[]{:S(2)}, u32[]{:S(2)}) %collective-permute-start.27) | collective-permute-done | bytes 262176 | tf_op jit(solution)/shard_map/ppermute | solution.py:252
  120.1 1.9 %collective-permute-done.26.refs_2_ = bf16[32,4096]{1,0:T(8,128)(2,1)S(1)} collective-permute-done((bf16[32,4096]{1,0:T(8,128)(2,1)S(1)}, bf16[32,4096]{1,0:T(8,128)(2,1)S(1)}, u32[]{:S(2)}, u32[]{:S(2)}) %collective-permute-start.26) | collective-permute-done | bytes 262176 | tf_op jit(solution)/shard_map/ppermute | solution.py:252
  122.4 2.4 %shard_map.66.refs_4_ = bf16[8,64,4096]{2,1,0:T(8,128)(2,1)} custom-call(f32[3,8]{1,0:T(4,128)S(1)} %pad_maximum_fusion.coef_ref, f32[8,32,4096]{2,1,0:T(8,128)S(1)} %shard_map.63.plain_ref, bf16[32,4096]{1,0:T(8,128)(2,1)S(1)} %get-tuple-element.28.refs_0_, bf16[32,4096]{1,0:T(8,128)(2,1)S(1)} %collective-permute-done.25.refs_1_, ...), custom_call_target="tpu_custom_call" | custom-call | flops 8388608 | bytes 2097152 | tf_op jit(solution)/shard_map/pallas_call | solution.py:327
  124.8 2.8 %collective-permute-done.13.refs_3_ = bf16[32,4096]{1,0:T(8,128)(2,1)S(1)} collective-permute-done((bf16[32,4096]{1,0:T(8,128)(2,1)S(1)}, bf16[32,4096]{1,0:T(8,128)(2,1)S(1)}, u32[]{:S(2)}, u32[]{:S(2)}) %collective-permute-start.13) | collective-permute-done | bytes 262176 | tf_op jit(solution)/shard_map/ppermute | solution.py:252
  127.6 5.0 %collective-permute-done.12.refs_2_ = bf16[32,4096]{1,0:T(8,128)(2,1)S(1)} collective-permute-done((bf16[32,4096]{1,0:T(8,128)(2,1)S(1)}, bf16[32,4096]{1,0:T(8,128)(2,1)S(1)}, u32[]{:S(2)}, u32[]{:S(2)}) %collective-permute-start.12) | collective-permute-done | bytes 262176 | tf_op jit(solution)/shard_map/ppermute | solution.py:252
  133.2 2.4 %shard_map.67 = bf16[8,64,4096]{2,1,0:T(8,128)(2,1)} custom-call(f32[3,8]{1,0:T(4,128)S(1)} %pad_maximum_fusion.coef_ref, f32[8,32,4096]{2,1,0:T(8,128)S(1)} %shard_map.58.plain_ref, bf16[32,4096]{1,0:T(8,128)(2,1)S(1)} %get-tuple-element.35.refs_0_, bf16[32,4096]{1,0:T(8,128)(2,1)S(1)} %collective-permute-done.11.refs_1_, ...), custom_call_target="tpu_custom_call", output_to_operand_aliasing={{}: (6, {})} | custom-call | flops 8388608 | bytes 2097152 | tf_op jit(solution)/shard_map/pallas_call | solution.py:327
  (58 shorter events, 33.0 us)
Async XLA Ops:
  1.1 17.9 %collective-permute-start.16 = (bf16[32,4096]{1,0:T(8,128)(2,1)S(1)}, bf16[32,4096]{1,0:T(8,128)(2,1)S(1)}, u32[]{:S(2)}, u32[]{:S(2)}) collective-permute-start(bf16[32,4096]{1,0:T(8,128)(2,1)S(1)} %get-tuple-element.39.refs_0_.base_ref), channel_id=1, source_target_pairs={{0,8},{8,0},{16,24},{24,16},{1,9},{9,1},{17,25},{25,17},{2,10},{10... | collective-permute-start | bytes 786440 | tf_op jit(solution)/shard_map/ppermute | solution.py:240
  4.2 14.3 %collective-permute-start.14 = (bf16[32,4096]{1,0:T(8,128)(2,1)S(1)}, bf16[32,4096]{1,0:T(8,128)(2,1)S(1)}, u32[]{:S(2)}, u32[]{:S(2)}) collective-permute-start(bf16[32,4096]{1,0:T(8,128)(2,1)S(1)} %get-tuple-element.39.refs_0_.base_ref), channel_id=1, source_target_pairs={{0,16},{8,24},{16,0},{24,8},{1,17},{9,25},{17,1},{25,9},{2,18},{10... | collective-permute-start | bytes 786440 | tf_op jit(solution)/shard_map/ppermute | solution.py:240
  26.5 15.3 %collective-permute-start.17 = (bf16[4,32,4096]{2,1,0:T(8,128)(2,1)S(1)}, bf16[4,32,4096]{2,1,0:T(8,128)(2,1)S(1)}, u32[]{:S(2)}, u32[]{:S(2)}) collective-permute-start(bf16[4,32,4096]{2,1,0:T(8,128)(2,1)S(1)} %get-tuple-element.22), channel_id=1, source_target_pairs={{0,1},{1,0},{2,3},{3,2},{4,5},{5,4},{6,7},{7,6},{8,9},{9,8},{10,11... | collective-permute-start | bytes 3145736 | tf_op jit(solution)/shard_map/ppermute | solution.py:245
  26.6 15.2 %collective-permute-start = (bf16[32,4096]{1,0:T(8,128)(2,1)S(1)}, bf16[32,4096]{1,0:T(8,128)(2,1)S(1)}, u32[]{:S(2)}, u32[]{:S(2)}) collective-permute-start(bf16[32,4096]{1,0:T(8,128)(2,1)S(1)} %get-tuple-element.40.refs_0_.base_ref), channel_id=1, source_target_pairs={{0,16},{8,24},{16,0},{24,8},{1,17},{9,25},{17,1},{25,9},{2,18},{10... | collective-permute-start | bytes 786440 | tf_op jit(solution)/shard_map/ppermute | solution.py:240
  27.7 18.0 %collective-permute-start.2 = (bf16[32,4096]{1,0:T(8,128)(2,1)S(1)}, bf16[32,4096]{1,0:T(8,128)(2,1)S(1)}, u32[]{:S(2)}, u32[]{:S(2)}) collective-permute-start(bf16[32,4096]{1,0:T(8,128)(2,1)S(1)} %get-tuple-element.40.refs_0_.base_ref), channel_id=1, source_target_pairs={{0,8},{8,0},{16,24},{24,16},{1,9},{9,1},{17,25},{25,17},{2,10},{10... | collective-permute-start | bytes 786440 | tf_op jit(solution)/shard_map/ppermute | solution.py:240
  42.0 9.3 %collective-permute-start.18 = (bf16[32,4096]{1,0:T(8,128)(2,1)S(1)}, bf16[32,4096]{1,0:T(8,128)(2,1)S(1)}, u32[]{:S(2)}, u32[]{:S(2)}) collective-permute-start(bf16[32,4096]{1,0:T(8,128)(2,1)S(1)} %get-tuple-element.29), channel_id=1, source_target_pairs={{0,2},{1,3},{2,0},{3,1},{4,6},{5,7},{6,4},{7,5},{8,10},{9,11},{10,... | collective-permute-start | bytes 786440 | tf_op jit(solution)/shard_map/ppermute | solution.py:252
  43.5 13.8 %collective-permute-start.20 = (bf16[32,4096]{1,0:T(8,128)(2,1)S(1)}, bf16[32,4096]{1,0:T(8,128)(2,1)S(1)}, u32[]{:S(2)}, u32[]{:S(2)}) collective-permute-start(bf16[32,4096]{1,0:T(8,128)(2,1)S(1)} %get-tuple-element.30), channel_id=1, source_target_pairs={{0,6},{1,7},{2,4},{3,5},{4,2},{5,3},{6,0},{7,1},{8,14},{9,15},{10,... | collective-permute-start | bytes 786440 | tf_op jit(solution)/shard_map/ppermute | solution.py:252
  45.3 13.4 %collective-permute-start.19 = (bf16[32,4096]{1,0:T(8,128)(2,1)S(1)}, bf16[32,4096]{1,0:T(8,128)(2,1)S(1)}, u32[]{:S(2)}, u32[]{:S(2)}) collective-permute-start(bf16[32,4096]{1,0:T(8,128)(2,1)S(1)} %get-tuple-element.31), channel_id=1, source_target_pairs={{0,4},{1,5},{2,6},{3,7},{4,0},{5,1},{6,2},{7,3},{8,12},{9,13},{10,... | collective-permute-start | bytes 786440 | tf_op jit(solution)/shard_map/ppermute | solution.py:252
  51.2 9.9 %collective-permute-start.3 = (bf16[4,32,4096]{2,1,0:T(8,128)(2,1)S(1)}, bf16[4,32,4096]{2,1,0:T(8,128)(2,1)S(1)}, u32[]{:S(2)}, u32[]{:S(2)}) collective-permute-start(bf16[4,32,4096]{2,1,0:T(8,128)(2,1)S(1)} %get-tuple-element.18), channel_id=1, source_target_pairs={{0,1},{1,0},{2,3},{3,2},{4,5},{5,4},{6,7},{7,6},{8,9},{9,8},{10,11... | collective-permute-start | bytes 3145736 | tf_op jit(solution)/shard_map/ppermute | solution.py:245
  58.9 13.9 %collective-permute-start.23 = (bf16[32,4096]{1,0:T(8,128)(2,1)S(1)}, bf16[32,4096]{1,0:T(8,128)(2,1)S(1)}, u32[]{:S(2)}, u32[]{:S(2)}) collective-permute-start(bf16[32,4096]{1,0:T(8,128)(2,1)S(1)} %fusion.2.first_ref.refs_0_), channel_id=1, source_target_pairs={{0,8},{8,0},{16,24},{24,16},{1,9},{9,1},{17,25},{25,17},{2,10},{10... | collective-permute-start | bytes 786440 | tf_op jit(solution)/shard_map/ppermute | solution.py:240
  60.7 12.1 %collective-permute-start.21 = (bf16[32,4096]{1,0:T(8,128)(2,1)S(1)}, bf16[32,4096]{1,0:T(8,128)(2,1)S(1)}, u32[]{:S(2)}, u32[]{:S(2)}) collective-permute-start(bf16[32,4096]{1,0:T(8,128)(2,1)S(1)} %fusion.2.first_ref.refs_0_), channel_id=1, source_target_pairs={{0,16},{8,24},{16,0},{24,8},{1,17},{9,25},{17,1},{25,9},{2,18},{10... | collective-permute-start | bytes 786440 | tf_op jit(solution)/shard_map/ppermute | solution.py:240
  61.4 19.5 %collective-permute-start.4 = (bf16[32,4096]{1,0:T(8,128)(2,1)S(1)}, bf16[32,4096]{1,0:T(8,128)(2,1)S(1)}, u32[]{:S(2)}, u32[]{:S(2)}) collective-permute-start(bf16[32,4096]{1,0:T(8,128)(2,1)S(1)} %get-tuple-element.36), channel_id=1, source_target_pairs={{0,2},{1,3},{2,0},{3,1},{4,6},{5,7},{6,4},{7,5},{8,10},{9,11},{10,... | collective-permute-start | bytes 786440 | tf_op jit(solution)/shard_map/ppermute | solution.py:252
  63.1 17.8 %collective-permute-start.6 = (bf16[32,4096]{1,0:T(8,128)(2,1)S(1)}, bf16[32,4096]{1,0:T(8,128)(2,1)S(1)}, u32[]{:S(2)}, u32[]{:S(2)}) collective-permute-start(bf16[32,4096]{1,0:T(8,128)(2,1)S(1)} %get-tuple-element.37), channel_id=1, source_target_pairs={{0,6},{1,7},{2,4},{3,5},{4,2},{5,3},{6,0},{7,1},{8,14},{9,15},{10,... | collective-permute-start | bytes 786440 | tf_op jit(solution)/shard_map/ppermute | solution.py:252
  63.4 17.5 %collective-permute-start.5 = (bf16[32,4096]{1,0:T(8,128)(2,1)S(1)}, bf16[32,4096]{1,0:T(8,128)(2,1)S(1)}, u32[]{:S(2)}, u32[]{:S(2)}) collective-permute-start(bf16[32,4096]{1,0:T(8,128)(2,1)S(1)} %get-tuple-element.38), channel_id=1, source_target_pairs={{0,4},{1,5},{2,6},{3,7},{4,0},{5,1},{6,2},{7,3},{8,12},{9,13},{10,... | collective-permute-start | bytes 786440 | tf_op jit(solution)/shard_map/ppermute | solution.py:252
  80.8 25.0 %collective-permute-start.24 = (bf16[4,32,4096]{2,1,0:T(8,128)(2,1)S(1)}, bf16[4,32,4096]{2,1,0:T(8,128)(2,1)S(1)}, u32[]{:S(2)}, u32[]{:S(2)}) collective-permute-start(bf16[4,32,4096]{2,1,0:T(8,128)(2,1)S(1)} %get-tuple-element.24), channel_id=1, source_target_pairs={{0,1},{1,0},{2,3},{3,2},{4,5},{5,4},{6,7},{7,6},{8,9},{9,8},{10,11... | collective-permute-start | bytes 3145736 | tf_op jit(solution)/shard_map/ppermute | solution.py:245
  81.1 14.8 %collective-permute-start.7 = (bf16[32,4096]{1,0:T(8,128)(2,1)S(1)}, bf16[32,4096]{1,0:T(8,128)(2,1)S(1)}, u32[]{:S(2)}, u32[]{:S(2)}) collective-permute-start(bf16[32,4096]{1,0:T(8,128)(2,1)S(1)} %fusion.5.first_ref.refs_0_), channel_id=1, source_target_pairs={{0,16},{8,24},{16,0},{24,8},{1,17},{9,25},{17,1},{25,9},{2,18},{10... | collective-permute-start | bytes 786440 | tf_op jit(solution)/shard_map/ppermute | solution.py:240
  82.4 14.0 %collective-permute-start.9 = (bf16[32,4096]{1,0:T(8,128)(2,1)S(1)}, bf16[32,4096]{1,0:T(8,128)(2,1)S(1)}, u32[]{:S(2)}, u32[]{:S(2)}) collective-permute-start(bf16[32,4096]{1,0:T(8,128)(2,1)S(1)} %fusion.5.first_ref.refs_0_), channel_id=1, source_target_pairs={{0,8},{8,0},{16,24},{24,16},{1,9},{9,1},{17,25},{25,17},{2,10},{10... | collective-permute-start | bytes 786440 | tf_op jit(solution)/shard_map/ppermute | solution.py:240
  95.9 8.2 %collective-permute-start.8 = (bf16[32,4096]{1,0:T(8,128)(2,1)S(1)}, bf16[32,4096]{1,0:T(8,128)(2,1)S(1)}, u32[]{:S(2)}, u32[]{:S(2)}) collective-permute-start(bf16[32,4096]{1,0:T(8,128)(2,1)S(1)} %collective-permute-done.7.refs_2_), channel_id=1, source_target_pairs={{0,8},{8,0},{16,24},{24,16},{1,9},{9,1},{17,25},{25,17},{2,10},{10... | collective-permute-start | bytes 786440 | tf_op jit(solution)/shard_map/ppermute | solution.py:240
  106.1 10.2 %collective-permute-start.27 = (bf16[32,4096]{1,0:T(8,128)(2,1)S(1)}, bf16[32,4096]{1,0:T(8,128)(2,1)S(1)}, u32[]{:S(2)}, u32[]{:S(2)}) collective-permute-start(bf16[32,4096]{1,0:T(8,128)(2,1)S(1)} %get-tuple-element.25), channel_id=1, source_target_pairs={{0,6},{1,7},{2,4},{3,5},{4,2},{5,3},{6,0},{7,1},{8,14},{9,15},{10,... | collective-permute-start | bytes 786440 | tf_op jit(solution)/shard_map/ppermute | solution.py:252
  108.4 13.5 %collective-permute-start.26 = (bf16[32,4096]{1,0:T(8,128)(2,1)S(1)}, bf16[32,4096]{1,0:T(8,128)(2,1)S(1)}, u32[]{:S(2)}, u32[]{:S(2)}) collective-permute-start(bf16[32,4096]{1,0:T(8,128)(2,1)S(1)} %get-tuple-element.26), channel_id=1, source_target_pairs={{0,4},{1,5},{2,6},{3,7},{4,0},{5,1},{6,2},{7,3},{8,12},{9,13},{10,... | collective-permute-start | bytes 786440 | tf_op jit(solution)/shard_map/ppermute | solution.py:252
  109.1 13.3 %collective-permute-start.25 = (bf16[32,4096]{1,0:T(8,128)(2,1)S(1)}, bf16[32,4096]{1,0:T(8,128)(2,1)S(1)}, u32[]{:S(2)}, u32[]{:S(2)}) collective-permute-start(bf16[32,4096]{1,0:T(8,128)(2,1)S(1)} %get-tuple-element.27), channel_id=1, source_target_pairs={{0,2},{1,3},{2,0},{3,1},{4,6},{5,7},{6,4},{7,5},{8,10},{9,11},{10,... | collective-permute-start | bytes 786440 | tf_op jit(solution)/shard_map/ppermute | solution.py:252
  109.9 17.6 %collective-permute-start.13 = (bf16[32,4096]{1,0:T(8,128)(2,1)S(1)}, bf16[32,4096]{1,0:T(8,128)(2,1)S(1)}, u32[]{:S(2)}, u32[]{:S(2)}) collective-permute-start(bf16[32,4096]{1,0:T(8,128)(2,1)S(1)} %get-tuple-element.32), channel_id=1, source_target_pairs={{0,6},{1,7},{2,4},{3,5},{4,2},{5,3},{6,0},{7,1},{8,14},{9,15},{10,... | collective-permute-start | bytes 786440 | tf_op jit(solution)/shard_map/ppermute | solution.py:252
  112.3 20.4 %collective-permute-start.12 = (bf16[32,4096]{1,0:T(8,128)(2,1)S(1)}, bf16[32,4096]{1,0:T(8,128)(2,1)S(1)}, u32[]{:S(2)}, u32[]{:S(2)}) collective-permute-start(bf16[32,4096]{1,0:T(8,128)(2,1)S(1)} %get-tuple-element.33), channel_id=1, source_target_pairs={{0,4},{1,5},{2,6},{3,7},{4,0},{5,1},{6,2},{7,3},{8,12},{9,13},{10,... | collective-permute-start | bytes 786440 | tf_op jit(solution)/shard_map/ppermute | solution.py:252
  116.3 16.9 %collective-permute-start.11 = (bf16[32,4096]{1,0:T(8,128)(2,1)S(1)}, bf16[32,4096]{1,0:T(8,128)(2,1)S(1)}, u32[]{:S(2)}, u32[]{:S(2)}) collective-permute-start(bf16[32,4096]{1,0:T(8,128)(2,1)S(1)} %get-tuple-element.34), channel_id=1, source_target_pairs={{0,2},{1,3},{2,0},{3,1},{4,6},{5,7},{6,4},{7,5},{8,10},{9,11},{10,... | collective-permute-start | bytes 786440 | tf_op jit(solution)/shard_map/ppermute | solution.py:252
  (4 other events, 24.4 us)
